TPU v7x, 512 devices: a whole 4x8x8 slice. The times are simulated.
512 devices in a mesh: mem: 32 (over y, x_hi, core), grid: 16 (over z, x_lo).
Axes of the slice: x: 4 (x_hi: 2, x_lo: 2; x = x_hi * 2 + x_lo), y: 8, z: 8, core: 2. Of those that a mesh axis runs over, the one named last changes fastest.
Arguments:
- ensemble: bfloat16 [64, 4, 128, 32, 128], P('mem', None, None, 'grid'), may hold values from -6 to 6
- control: bfloat16 [64, 128, 32, 128], P('mem', None, 'grid'), may hold values from -6 to 6
- vertical: bfloat16 [128, 128], replicated, may hold values from -0.5 to 0.5
- inverse_var: float32 [4, 128], replicated, may hold values from 0.25 to 4
- obs_code: int32 [64, 256], P('grid'), may hold values from 0 to 4
- obs_count: int32 [64, 256], P('grid'), may hold values from 0 to 3
Outputs:
- product: float32 [64, 128, 32, 128], P('mem', None, 'grid')
All inputs are finite; a program needn't handle non-finite values.
Results may differ from a plain program's by a relative error of at most 0.00045.
Values sent between devices are 32-bit elements; how exact they have to be, the bound alone decides.
No kernel may reach another device: no remote copies, remote signals or barrier semaphores. Data moves between devices by JAX's collectives and lax.ppermute only.
A program may use at most 64 MiB of HBM per device.

v0:
```python
import jax
import jax.numpy as jnp
from jax import lax
from jax.sharding import PartitionSpec as P

diffusion = 0.2
near_weight = 0.75
far_weight = 0.25


def with_halo(block, sides, width):
    for axis, dim in sides:
        count = lax.axis_size(axis)
        forward = [(i, i + 1) for i in range(count - 1)]
        backward = [(target, source) for source, target in forward]
        low = lax.ppermute(
            lax.slice_in_dim(block, block.shape[dim] - width, None, axis=dim), axis, forward
        )
        high = lax.ppermute(lax.slice_in_dim(block, 0, width, axis=dim), axis, backward)
        block = jnp.concatenate([low, block, high], axis=dim)
    return block


def shifted(shard, axis, by):
    size = lax.axis_size(axis)
    pairs = [(i, i + by) for i in range(size) if 0 <= i + by < size]
    return lax.ppermute(shard, axis, pairs)


def cut_along(shard, dim, size):
    before, after = (shard.shape[:dim], shard.shape[dim + 1 :])
    return jnp.moveaxis(shard.reshape(*before, size, -1, *after), dim, 0)


def summed_on_arrival(shard, axis, dim):
    tiles = cut_along(shard, dim, lax.axis_size(axis))
    arrived = lax.all_to_all(tiles, axis, split_axis=0, concat_axis=0, tiled=True)
    return arrived.sum(axis=0)


def from_everyone(shard, axis):
    size = lax.axis_size(axis)
    return lax.all_to_all(
        jnp.broadcast_to(shard[None], (size, *shard.shape)), axis, 0, 0, tiled=True
    )


def in_order(tiles, dim):
    lengths = list(tiles.shape[1:])
    lengths[dim] *= tiles.shape[0]
    return jnp.moveaxis(tiles, 0, dim).reshape(lengths)


def gathered_copies(shard, axis, dim):
    tiles = from_everyone(shard, axis)
    return in_order(tiles, dim)


def column_pair(field):
    padded = jnp.pad(field, [(0, 0)] * (field.ndim - 1) + [(1, 1)])
    return padded[..., 2:] + padded[..., :-2]


def smooth_rows(extended):
    center = extended[..., 1:-1, :]
    return center + diffusion * (
        extended[..., 2:, :] + extended[..., :-2, :] + column_pair(center) - 4.0 * center
    )


def refine(coarse, extended):
    upper = near_weight * coarse + far_weight * extended[..., :-2, :]
    lower = near_weight * coarse + far_weight * extended[..., 2:, :]
    rows_fine = jnp.stack([upper, lower], axis=-2)
    rows_fine = rows_fine.reshape(coarse.shape[:-2] + (2 * coarse.shape[-2], coarse.shape[-1]))
    padded = jnp.pad(rows_fine, [(0, 0)] * (rows_fine.ndim - 1) + [(1, 1)])
    left = near_weight * rows_fine + far_weight * padded[..., :-2]
    right = near_weight * rows_fine + far_weight * padded[..., 2:]
    both = jnp.stack([left, right], axis=-1)
    return both.reshape(rows_fine.shape[:-1] + (2 * rows_fine.shape[-1],))


def coarsen(fine_field, extended):
    half_rows = fine_field.shape[-2] // 2
    rows_coarse = near_weight * (fine_field[..., 0::2, :] + fine_field[..., 1::2, :])
    rows_coarse = rows_coarse + far_weight * (
        extended[..., 0 : 2 * half_rows : 2, :] + extended[..., 3::2, :]
    )
    width = rows_coarse.shape[-1]
    padded = jnp.pad(rows_coarse, [(0, 0)] * (rows_coarse.ndim - 1) + [(1, 1)])
    result = near_weight * (rows_coarse[..., 0::2] + rows_coarse[..., 1::2])
    return result + far_weight * (padded[..., 0:width:2] + padded[..., 3::2])


def obs_masks(code):
    return [(code == which).astype(jnp.float32) for which in range(1, 5)]


def observe(fine_field, extended, masks, count, weights):
    padded = jnp.pad(fine_field, [(0, 0)] * (fine_field.ndim - 1) + [(1, 1)])
    diff = fine_field - masks[0] * extended[..., 2:, :] - masks[1] * extended[..., :-2, :]
    diff = diff - masks[2] * padded[..., 2:] - masks[3] * padded[..., :-2]
    return count.astype(jnp.float32) * weights[:, :, None, None] * diff


def adjoint_rows(forcing, masks, above, below):
    first = masks[0] * forcing
    second = masks[1] * forcing
    from_above = jnp.concatenate([above, first[..., :-1, :]], axis=-2)
    from_below = jnp.concatenate([second[..., 1:, :], below], axis=-2)
    pad_spec = [(0, 0)] * (forcing.ndim - 1) + [(1, 1)]
    from_left = jnp.pad(masks[2] * forcing, pad_spec)[..., :-2]
    from_right = jnp.pad(masks[3] * forcing, pad_spec)[..., 2:]
    return forcing - from_above - from_below - from_left - from_right


def per_device(ensemble, control, vertical, inverse_var, obs_code, obs_count):
    member_count = ensemble.shape[0]
    factor = (member_count * lax.axis_size("mem")) ** (-0.5)

    def margin(field):
        return with_halo(field, (("grid", 2),), 1)

    def smooth_pair(field):
        extended = with_halo(field, (("grid", 2),), 2)
        row_count = field.shape[2]
        global_row = (
            lax.axis_index("grid") * row_count - 1 + jnp.arange(row_count + 2, dtype=jnp.int32)
        )
        inside = ((global_row >= 0) & (global_row < row_count * lax.axis_size("grid"))).astype(
            jnp.float32
        )
        first_pass = smooth_rows(extended) * inside[:, None]
        return smooth_rows(first_pass)

    masks = obs_masks(obs_code)
    mixed = jnp.einsum("lm,kmxy->klxy", vertical, control, preferred_element_type=jnp.float32)
    local = smooth_pair(mixed)
    partial_value = jnp.zeros(ensemble.shape[1:], jnp.float32)
    for member in range(member_count):
        partial_value = partial_value + ensemble[member].astype(jnp.float32) * local[member][None]
    partial_value = factor * partial_value
    share = summed_on_arrival(partial_value, "mem", 1)
    level_count = share.shape[1]
    weights = lax.dynamic_slice_in_dim(
        inverse_var, lax.axis_index("mem") * level_count, level_count, 1
    )
    fine_field = refine(share, margin(share))
    forcing = observe(fine_field, margin(fine_field), masks, obs_count, weights)
    above = shifted((masks[0] * forcing)[:, :, -1:, :], "grid", 1)
    below = shifted((masks[1] * forcing)[:, :, :1, :], "grid", -1)
    adjoint_fine = adjoint_rows(forcing, masks, above, below)
    adjoint = gathered_copies(coarsen(adjoint_fine, margin(adjoint_fine)), "mem", 1)
    projected = jnp.stack(
        [
            factor * jnp.sum(ensemble[member].astype(jnp.float32) * adjoint, axis=0)
            for member in range(member_count)
        ],
        axis=0,
    )
    rounded = smooth_pair(projected).astype(jnp.bfloat16)
    back = jnp.einsum("ml,kmxy->klxy", vertical, rounded, preferred_element_type=jnp.float32)
    return control.astype(jnp.float32) + back


def solution(mesh):
    return jax.shard_map(
        per_device,
        mesh=mesh,
        in_specs=(
            P("mem", None, None, "grid", None),
            P("mem", None, "grid", None),
            P(),
            P(),
            P("grid", None),
            P("grid", None),
        ),
        out_specs=P("mem", None, "grid", None),
        check_vma=False,
    )
```

profile of v0, /device:TPU:198, one launch (start us, length us, event | category | flops | bytes accessed | tf_op | source)
XLA Modules:
  0.0 148.1 jit_solution(13090571522316917174)
XLA Ops:
  0.0 1.0 copy.152
  1.1 0.2 convolution_bitcast_fusion.1
  1.2 5.8 %collective-permute-start = (f32[2,128,2,128]{1,3,2,0:T(8,128)S(1)}, f32[2,128,2,128]{1,3,2,0:T(8,128)S(1)}, u32[]{:S(2)}, u32[]{:S(2)}) collective-permute-start(f32[2,128,2,128]{1,3,2,0:T(8,128)S(1)} %convolution_bitcast_fusion.1), channel_id=1, source_target_pairs={{0,1},{1,2},{2,3},{3,4},{4,5},{5,6},{6,7},{7,8},{8,9},{9,10},{10,1... | collective-permute-start | bytes 786440 | tf_op jit(solution)/shard_map/ppermute | solution.py:16
  7.0 1.9 %collective-permute-start.1 = (f32[2,128,2,128]{1,3,2,0:T(8,128)S(1)}, f32[2,128,2,128]{1,3,2,0:T(8,128)S(1)}, u32[]{:S(2)}, u32[]{:S(2)}) collective-permute-start(f32[2,128,2,128]{1,3,2,0:T(8,128)S(1)} %convolution_bitcast_fusion.1), channel_id=1, source_target_pairs={{1,0},{2,1},{3,2},{4,3},{5,4},{6,5},{7,6},{8,7},{9,8},{10,9},{11,1... | collective-permute-start | bytes 786440 | tf_op jit(solution)/shard_map/ppermute | solution.py:19
  8.9 1.4 fusion.63
  10.4 2.1 %collective-permute-done = f32[2,128,2,128]{1,3,2,0:T(8,128)S(1)} collective-permute-done((f32[2,128,2,128]{1,3,2,0:T(8,128)S(1)}, f32[2,128,2,128]{1,3,2,0:T(8,128)S(1)}, u32[]{:S(2)}, u32[]{:S(2)}) %collective-permute-start) | collective-permute-done | bytes 262176 | tf_op jit(solution)/shard_map/ppermute | solution.py:16
  12.6 6.2 %collective-permute-done.1 = f32[2,128,2,128]{1,3,2,0:T(8,128)S(1)} collective-permute-done((f32[2,128,2,128]{1,3,2,0:T(8,128)S(1)}, f32[2,128,2,128]{1,3,2,0:T(8,128)S(1)}, u32[]{:S(2)}, u32[]{:S(2)}) %collective-permute-start.1) | collective-permute-done | bytes 262176 | tf_op jit(solution)/shard_map/ppermute | solution.py:19
  18.8 0.2 fusion.6
  19.1 0.1 fusion.22
  19.2 0.1 copy.155
  19.3 0.0 copy-start.1
  19.3 0.1 copy.157
  19.4 0.2 fusion.15
  19.6 0.4 copy.158
  20.1 27.7 %all_to_all.10 = f32[32,4,4,2,128]{4,3,2,1,0:T(2,128)S(1)} all-to-all(f32[32,4,4,2,128]{4,3,2,1,0:T(2,128)S(1)} %copy.158), channel_id=1, replica_groups=mesh['mem'=32,'grid'=16] {'mem'}, dimensions={0} | all-to-all | bytes 1048576 | tf_op jit(solution)/shard_map/all_to_all | solution.py:37
  47.7 0.2 reduce_sum.27
  47.9 5.9 %collective-permute-start.2 = (f32[4,4,1,128]{3,1,2,0:T(4,128)S(1)}, f32[4,4,1,128]{3,1,2,0:T(4,128)S(1)}, u32[]{:S(2)}, u32[]{:S(2)}) collective-permute-start(f32[4,4,1,128]{3,1,2,0:T(4,128)S(1)} %bitcast.69), channel_id=1, source_target_pairs={{0,1},{1,2},{2,3},{3,4},{4,5},{5,6},{6,7},{7,8},{8,9},{9,10},{10,1... | collective-permute-start | bytes 24584 | tf_op jit(solution)/shard_map/ppermute | solution.py:16
  53.8 1.9 %collective-permute-start.3 = (f32[4,4,1,128]{3,1,2,0:T(4,128)S(1)}, f32[4,4,1,128]{3,1,2,0:T(4,128)S(1)}, u32[]{:S(2)}, u32[]{:S(2)}) collective-permute-start(f32[4,4,1,128]{3,1,2,0:T(4,128)S(1)} %bitcast.68), channel_id=1, source_target_pairs={{1,0},{2,1},{3,2},{4,3},{5,4},{6,5},{7,6},{8,7},{9,8},{10,9},{11,1... | collective-permute-start | bytes 24584 | tf_op jit(solution)/shard_map/ppermute | solution.py:19
  55.8 0.0 collective-permute-done.2
  55.8 5.7 %collective-permute-done.3 = f32[4,4,1,128]{3,1,2,0:T(4,128)S(1)} collective-permute-done((f32[4,4,1,128]{3,1,2,0:T(4,128)S(1)}, f32[4,4,1,128]{3,1,2,0:T(4,128)S(1)}, u32[]{:S(2)}, u32[]{:S(2)}) %collective-permute-start.3) | collective-permute-done | bytes 8224 | tf_op jit(solution)/shard_map/ppermute | solution.py:19
  61.6 0.1 fusion.46
  61.7 1.1 copy.165
  62.9 2.7 %fusion.62 = (f32[4,4,1,256]{2,3,1,0:T(8,128)}, f32[4,4,1,256]{2,3,1,0:T(8,128)}) fusion(f32[4,4,4,256]{2,3,1,0:T(8,128)S(1)} %bitcast.49), kind=kLoop, calls=%fused_computation.112 | loop fusion | bytes 65536 | tf_op jit(solution)/shard_map/slice | solution.py:19
  65.6 2.2 %copy.166 = f32[4,4,1,256]{3,1,2,0:T(4,128)S(1)} copy(f32[4,4,1,256]{2,3,1,0:T(8,128)} %get-tuple-element.9) | data formatting | bytes 32768 | tf_op jit(solution)/shard_map/slice | solution.py:19
  67.8 1.9 %collective-permute-start.4 = (f32[4,4,1,256]{3,1,2,0:T(4,128)S(1)}, f32[4,4,1,256]{3,1,2,0:T(4,128)S(1)}, u32[]{:S(2)}, u32[]{:S(2)}) collective-permute-start(f32[4,4,1,256]{3,1,2,0:T(4,128)S(1)} %copy.166), channel_id=1, source_target_pairs={{1,0},{2,1},{3,2},{4,3},{5,4},{6,5},{7,6},{8,7},{9,8},{10,9},{11,1... | collective-permute-start | bytes 49160 | tf_op jit(solution)/shard_map/ppermute | solution.py:19
  69.8 2.2 %copy.170 = f32[4,4,1,256]{3,1,2,0:T(4,128)S(1)} copy(f32[4,4,1,256]{2,3,1,0:T(8,128)} %get-tuple-element.10) | data formatting | bytes 32768 | tf_op jit(solution)/shard_map/slice | solution.py:17
  72.0 6.0 %collective-permute-start.5 = (f32[4,4,1,256]{3,1,2,0:T(4,128)S(1)}, f32[4,4,1,256]{3,1,2,0:T(4,128)S(1)}, u32[]{:S(2)}, u32[]{:S(2)}) collective-permute-start(f32[4,4,1,256]{3,1,2,0:T(4,128)S(1)} %copy.170), channel_id=1, source_target_pairs={{0,1},{1,2},{2,3},{3,4},{4,5},{5,6},{6,7},{7,8},{8,9},{9,10},{10,1... | collective-permute-start | bytes 49160 | tf_op jit(solution)/shard_map/ppermute | solution.py:16
  78.0 0.1 constant_dynamic-slice_fusion
  78.1 0.6 copy.169
  78.7 0.0 collective-permute-done.4
  78.7 0.7 collective-permute-done.5
  79.4 0.2 broadcast_multiply_fusion.2
  79.7 6.3 %collective-permute-start.6 = (f32[4,4,1,256]{3,1,2,0:T(4,128)S(1)}, f32[4,4,1,256]{3,1,2,0:T(4,128)S(1)}, u32[]{:S(2)}, u32[]{:S(2)}) collective-permute-start(f32[4,4,1,256]{3,1,2,0:T(4,128)S(1)} %copy.174), channel_id=1, source_target_pairs={{0,1},{1,2},{2,3},{3,4},{4,5},{5,6},{6,7},{7,8},{8,9},{9,10},{10,1... | collective-permute-start | bytes 49160 | tf_op jit(solution)/shard_map/ppermute | solution.py:27
  86.1 1.9 %collective-permute-start.7 = (f32[4,4,1,256]{3,1,2,0:T(4,128)S(1)}, f32[4,4,1,256]{3,1,2,0:T(4,128)S(1)}, u32[]{:S(2)}, u32[]{:S(2)}) collective-permute-start(f32[4,4,1,256]{3,1,2,0:T(4,128)S(1)} %copy.176), channel_id=1, source_target_pairs={{1,0},{2,1},{3,2},{4,3},{5,4},{6,5},{7,6},{8,7},{9,8},{10,9},{11,1... | collective-permute-start | bytes 49160 | tf_op jit(solution)/shard_map/ppermute | solution.py:27
  88.0 0.0 collective-permute-done.6
  88.1 5.7 %collective-permute-done.7 = f32[4,4,1,256]{3,1,2,0:T(4,128)S(1)} collective-permute-done((f32[4,4,1,256]{3,1,2,0:T(4,128)S(1)}, f32[4,4,1,256]{3,1,2,0:T(4,128)S(1)}, u32[]{:S(2)}, u32[]{:S(2)}) %collective-permute-start.7) | collective-permute-done | bytes 16416 | tf_op jit(solution)/shard_map/ppermute | solution.py:27
  93.8 0.1 fusion.33
  94.0 1.9 %collective-permute-start.8 = (f32[4,4,1,256]{3,1,2,0:T(4,128)S(1)}, f32[4,4,1,256]{3,1,2,0:T(4,128)S(1)}, u32[]{:S(2)}, u32[]{:S(2)}) collective-permute-start(f32[4,4,1,256]{3,1,2,0:T(4,128)S(1)} %copy.178), channel_id=1, source_target_pairs={{0,1},{1,2},{2,3},{3,4},{4,5},{5,6},{6,7},{7,8},{8,9},{9,10},{10,1... | collective-permute-start | bytes 49160 | tf_op jit(solution)/shard_map/ppermute | solution.py:16
  96.0 3.9 %collective-permute-start.9 = (f32[4,4,1,256]{3,1,2,0:T(4,128)S(1)}, f32[4,4,1,256]{3,1,2,0:T(4,128)S(1)}, u32[]{:S(2)}, u32[]{:S(2)}) collective-permute-start(f32[4,4,1,256]{3,1,2,0:T(4,128)S(1)} %copy.179), channel_id=1, source_target_pairs={{1,0},{2,1},{3,2},{4,3},{5,4},{6,5},{7,6},{8,7},{9,8},{10,9},{11,1... | collective-permute-start | bytes 49160 | tf_op jit(solution)/shard_map/ppermute | solution.py:19
  99.9 0.1 slice.188
  100.0 0.1 slice.189
  100.2 0.0 collective-permute-done.8
  100.2 3.5 %collective-permute-done.9 = f32[4,4,1,256]{3,1,2,0:T(4,128)S(1)} collective-permute-done((f32[4,4,1,256]{3,1,2,0:T(4,128)S(1)}, f32[4,4,1,256]{3,1,2,0:T(4,128)S(1)}, u32[]{:S(2)}, u32[]{:S(2)}) %collective-permute-start.9) | collective-permute-done | bytes 16416 | tf_op jit(solution)/shard_map/ppermute | solution.py:19
  103.8 0.1 slice.192
  103.9 0.1 slice.193
  104.1 0.1 pad.38
  104.2 0.9 slice.196
  105.2 0.9 slice.197
  106.1 0.9 slice.194
  107.1 0.9 slice.195
  108.0 0.2 broadcast_in_dim.2
  108.3 22.7 %all_to_all.11 = f32[32,4,4,2,128]{4,3,2,1,0:T(2,128)S(1)} all-to-all(f32[32,4,4,2,128]{4,3,2,1,0:T(2,128)S(1)} %broadcast_in_dim.2), channel_id=1, replica_groups=mesh['mem'=32,'grid'=16] {'mem'}, dimensions={0} | all-to-all | bytes 1048576 | tf_op jit(solution)/shard_map/all_to_all | solution.py:43
  131.0 0.3 fusion.16
  131.3 0.1 copy.185
  131.4 0.1 copy.189
  131.5 0.1 copy.188
  131.6 0.1 copy.190
  131.8 1.9 %collective-permute-start.10 = (f32[2,128,2,128]{1,3,2,0:T(8,128)S(1)}, f32[2,128,2,128]{1,3,2,0:T(8,128)S(1)}, u32[]{:S(2)}, u32[]{:S(2)}) collective-permute-start(f32[2,128,2,128]{1,3,2,0:T(8,128)S(1)} %pad_maximum_fusion.5), channel_id=1, source_target_pairs={{0,1},{1,2},{2,3},{3,4},{4,5},{5,6},{6,7},{7,8},{8,9},{9,10},{10,1... | collective-permute-start | bytes 786440 | tf_op jit(solution)/shard_map/ppermute | solution.py:16
  133.7 3.9 %collective-permute-start.11 = (f32[2,128,2,128]{1,3,2,0:T(8,128)S(1)}, f32[2,128,2,128]{1,3,2,0:T(8,128)S(1)}, u32[]{:S(2)}, u32[]{:S(2)}) collective-permute-start(f32[2,128,2,128]{1,3,2,0:T(8,128)S(1)} %pad_maximum_fusion.5), channel_id=1, source_target_pairs={{1,0},{2,1},{3,2},{4,3},{5,4},{6,5},{7,6},{8,7},{9,8},{10,9},{11,1... | collective-permute-start | bytes 786440 | tf_op jit(solution)/shard_map/ppermute | solution.py:19
  137.6 9.1 %collective-permute-done.10 = f32[2,128,2,128]{1,3,2,0:T(8,128)S(1)} collective-permute-done((f32[2,128,2,128]{1,3,2,0:T(8,128)S(1)}, f32[2,128,2,128]{1,3,2,0:T(8,128)S(1)}, u32[]{:S(2)}, u32[]{:S(2)}) %collective-permute-start.10) | collective-permute-done | bytes 262176 | tf_op jit(solution)/shard_map/ppermute | solution.py:16
  146.7 0.0 collective-permute-done.11
  146.7 0.2 fusion.12
  147.0 0.2 fusion
  147.2 0.8 copy.191
  (45 shorter events, 0.8 us)
Async XLA Ops:
  0.0 1.0 copy-start
  1.2 11.3 %collective-permute-start = (f32[2,128,2,128]{1,3,2,0:T(8,128)S(1)}, f32[2,128,2,128]{1,3,2,0:T(8,128)S(1)}, u32[]{:S(2)}, u32[]{:S(2)}) collective-permute-start(f32[2,128,2,128]{1,3,2,0:T(8,128)S(1)} %convolution_bitcast_fusion.1), channel_id=1, source_target_pairs={{0,1},{1,2},{2,3},{3,4},{4,5},{5,6},{6,7},{7,8},{8,9},{9,10},{10,1... | collective-permute-start | bytes 786440 | tf_op jit(solution)/shard_map/ppermute | solution.py:16
  7.0 11.8 %collective-permute-start.1 = (f32[2,128,2,128]{1,3,2,0:T(8,128)S(1)}, f32[2,128,2,128]{1,3,2,0:T(8,128)S(1)}, u32[]{:S(2)}, u32[]{:S(2)}) collective-permute-start(f32[2,128,2,128]{1,3,2,0:T(8,128)S(1)} %convolution_bitcast_fusion.1), channel_id=1, source_target_pairs={{1,0},{2,1},{3,2},{4,3},{5,4},{6,5},{7,6},{8,7},{9,8},{10,9},{11,1... | collective-permute-start | bytes 786440 | tf_op jit(solution)/shard_map/ppermute | solution.py:19
  19.3 36.5 %copy-start.1 = (s32[4,256]{1,0:T(4,128)S(1)}, s32[4,256]{1,0:T(4,128)}, u32[]{:S(2)}) copy-start(s32[4,256]{1,0:T(4,128)} %param.10) | copy-start | bytes 12292
  47.9 7.9 %collective-permute-start.2 = (f32[4,4,1,128]{3,1,2,0:T(4,128)S(1)}, f32[4,4,1,128]{3,1,2,0:T(4,128)S(1)}, u32[]{:S(2)}, u32[]{:S(2)}) collective-permute-start(f32[4,4,1,128]{3,1,2,0:T(4,128)S(1)} %bitcast.69), channel_id=1, source_target_pairs={{0,1},{1,2},{2,3},{3,4},{4,5},{5,6},{6,7},{7,8},{8,9},{9,10},{10,1... | collective-permute-start | bytes 24584 | tf_op jit(solution)/shard_map/ppermute | solution.py:16
  53.8 7.7 %collective-permute-start.3 = (f32[4,4,1,128]{3,1,2,0:T(4,128)S(1)}, f32[4,4,1,128]{3,1,2,0:T(4,128)S(1)}, u32[]{:S(2)}, u32[]{:S(2)}) collective-permute-start(f32[4,4,1,128]{3,1,2,0:T(4,128)S(1)} %bitcast.68), channel_id=1, source_target_pairs={{1,0},{2,1},{3,2},{4,3},{5,4},{6,5},{7,6},{8,7},{9,8},{10,9},{11,1... | collective-permute-start | bytes 24584 | tf_op jit(solution)/shard_map/ppermute | solution.py:19
  65.6 12.4 %copy-start.3 = (f32[4,128]{1,0:T(4,128)S(1)}, f32[4,128]{1,0:T(4,128)}, u32[]{:S(2)}) copy-start(f32[4,128]{1,0:T(4,128)} %param.9) | copy-start | bytes 6148
  65.6 12.5 %copy-start.2 = (s32[4,256]{1,0:T(4,128)S(1)}, s32[4,256]{1,0:T(4,128)}, u32[]{:S(2)}) copy-start(s32[4,256]{1,0:T(4,128)} %param.11) | copy-start | bytes 12292
  67.8 10.9 %collective-permute-start.4 = (f32[4,4,1,256]{3,1,2,0:T(4,128)S(1)}, f32[4,4,1,256]{3,1,2,0:T(4,128)S(1)}, u32[]{:S(2)}, u32[]{:S(2)}) collective-permute-start(f32[4,4,1,256]{3,1,2,0:T(4,128)S(1)} %copy.166), channel_id=1, source_target_pairs={{1,0},{2,1},{3,2},{4,3},{5,4},{6,5},{7,6},{8,7},{9,8},{10,9},{11,1... | collective-permute-start | bytes 49160 | tf_op jit(solution)/shard_map/ppermute | solution.py:19
  72.0 7.5 %collective-permute-start.5 = (f32[4,4,1,256]{3,1,2,0:T(4,128)S(1)}, f32[4,4,1,256]{3,1,2,0:T(4,128)S(1)}, u32[]{:S(2)}, u32[]{:S(2)}) collective-permute-start(f32[4,4,1,256]{3,1,2,0:T(4,128)S(1)} %copy.170), channel_id=1, source_target_pairs={{0,1},{1,2},{2,3},{3,4},{4,5},{5,6},{6,7},{7,8},{8,9},{9,10},{10,1... | collective-permute-start | bytes 49160 | tf_op jit(solution)/shard_map/ppermute | solution.py:16
  79.7 8.3 %collective-permute-start.6 = (f32[4,4,1,256]{3,1,2,0:T(4,128)S(1)}, f32[4,4,1,256]{3,1,2,0:T(4,128)S(1)}, u32[]{:S(2)}, u32[]{:S(2)}) collective-permute-start(f32[4,4,1,256]{3,1,2,0:T(4,128)S(1)} %copy.174), channel_id=1, source_target_pairs={{0,1},{1,2},{2,3},{3,4},{4,5},{5,6},{6,7},{7,8},{8,9},{9,10},{10,1... | collective-permute-start | bytes 49160 | tf_op jit(solution)/shard_map/ppermute | solution.py:27
  86.1 7.7 %collective-permute-start.7 = (f32[4,4,1,256]{3,1,2,0:T(4,128)S(1)}, f32[4,4,1,256]{3,1,2,0:T(4,128)S(1)}, u32[]{:S(2)}, u32[]{:S(2)}) collective-permute-start(f32[4,4,1,256]{3,1,2,0:T(4,128)S(1)} %copy.176), channel_id=1, source_target_pairs={{1,0},{2,1},{3,2},{4,3},{5,4},{6,5},{7,6},{8,7},{9,8},{10,9},{11,1... | collective-permute-start | bytes 49160 | tf_op jit(solution)/shard_map/ppermute | solution.py:27
  94.0 6.2 %collective-permute-start.8 = (f32[4,4,1,256]{3,1,2,0:T(4,128)S(1)}, f32[4,4,1,256]{3,1,2,0:T(4,128)S(1)}, u32[]{:S(2)}, u32[]{:S(2)}) collective-permute-start(f32[4,4,1,256]{3,1,2,0:T(4,128)S(1)} %copy.178), channel_id=1, source_target_pairs={{0,1},{1,2},{2,3},{3,4},{4,5},{5,6},{6,7},{7,8},{8,9},{9,10},{10,1... | collective-permute-start | bytes 49160 | tf_op jit(solution)/shard_map/ppermute | solution.py:16
  96.0 7.7 %collective-permute-start.9 = (f32[4,4,1,256]{3,1,2,0:T(4,128)S(1)}, f32[4,4,1,256]{3,1,2,0:T(4,128)S(1)}, u32[]{:S(2)}, u32[]{:S(2)}) collective-permute-start(f32[4,4,1,256]{3,1,2,0:T(4,128)S(1)} %copy.179), channel_id=1, source_target_pairs={{1,0},{2,1},{3,2},{4,3},{5,4},{6,5},{7,6},{8,7},{9,8},{10,9},{11,1... | collective-permute-start | bytes 49160 | tf_op jit(solution)/shard_map/ppermute | solution.py:19
  131.8 14.9 %collective-permute-start.10 = (f32[2,128,2,128]{1,3,2,0:T(8,128)S(1)}, f32[2,128,2,128]{1,3,2,0:T(8,128)S(1)}, u32[]{:S(2)}, u32[]{:S(2)}) collective-permute-start(f32[2,128,2,128]{1,3,2,0:T(8,128)S(1)} %pad_maximum_fusion.5), channel_id=1, source_target_pairs={{0,1},{1,2},{2,3},{3,4},{4,5},{5,6},{6,7},{7,8},{8,9},{9,10},{10,1... | collective-permute-start | bytes 786440 | tf_op jit(solution)/shard_map/ppermute | solution.py:16
  133.7 13.0 %collective-permute-start.11 = (f32[2,128,2,128]{1,3,2,0:T(8,128)S(1)}, f32[2,128,2,128]{1,3,2,0:T(8,128)S(1)}, u32[]{:S(2)}, u32[]{:S(2)}) collective-permute-start(f32[2,128,2,128]{1,3,2,0:T(8,128)S(1)} %pad_maximum_fusion.5), channel_id=1, source_target_pairs={{1,0},{2,1},{3,2},{4,3},{5,4},{6,5},{7,6},{8,7},{9,8},{10,9},{11,1... | collective-permute-start | bytes 786440 | tf_op jit(solution)/shard_map/ppermute | solution.py:19
where the time goes:
time: 149 us; the launch traced here: 148 us
  blocking collectives  50.4 us (34%)
  starting transfers between devices  43.4 us (29%)
  waiting for transfers between devices  33 us (22%)
  local copies, waits for them, and re-layouts  18.3 us (12%)
  other arithmetic  2 us (1%)
    all_to_all x1, blocking collectives, summed_on_arrival(): lax.all_to_all(tiles, axis, split_axis=0, concat_axis=0, tiled=True)  27.7 us
    all_to_all x1, blocking collectives, from_everyone(): lax.all_to_all(jnp.broadcast_to(shard[None], (size, *shard.shape)), axis,...  22.7 us
    ppermute x5, starting transfers between devices, with_halo(): lax.ppermute(lax.slice_in_dim(block, block.shape[dim] - width, None, axis...  21.5 us
    ppermute x5, waiting for transfers between devices, with_halo(): lax.ppermute(lax.slice_in_dim(block, 0, width, axis=dim), axis, backward)  15.3 us
    ppermute x5, starting transfers between devices, with_halo(): lax.ppermute(lax.slice_in_dim(block, 0, width, axis=dim), axis, backward)  13.6 us
    ppermute x5, waiting for transfers between devices, with_halo(): lax.ppermute(lax.slice_in_dim(block, block.shape[dim] - width, None, axis...  11.9 us
    ppermute x2, starting transfers between devices, shifted(): return lax.ppermute(shard, axis, pairs)  8.23 us
    ppermute x2, waiting for transfers between devices, shifted(): return lax.ppermute(shard, axis, pairs)  5.75 us
  transfers between devices with their start and end apart: 12, of which 7 were waited for; matrix products, arithmetic and copies ran while one was open for 3% of the time, Pallas kernels for 0%

commit v1 on v0

v1 whole, which is shorter than its diff:
```python
import functools
import jax
import jax.numpy as jnp
from jax import lax
from jax.experimental import pallas as pl
from jax.experimental.pallas import tpu as pltpu
from jax.sharding import PartitionSpec as P

diffusion = 0.2
near_weight = 0.75
far_weight = 0.25

VMEM = pl.BlockSpec(memory_space=pltpu.VMEM)
SMEM = pl.BlockSpec(memory_space=pltpu.SMEM)
f32 = jnp.float32


def call(body, out_shapes, n_in, scratch=(), flops=1000000, scalars=1):
    return pl.pallas_call(
        body,
        out_shape=out_shapes,
        in_specs=[SMEM] * scalars + [VMEM] * (n_in - scalars),
        out_specs=jax.tree.map(lambda _: VMEM, out_shapes),
        scratch_shapes=list(scratch),
        compiler_params=pltpu.CompilerParams(vmem_limit_bytes=24 * 1024 * 1024),
        cost_estimate=pl.CostEstimate(flops=flops, bytes_accessed=1000000, transcendentals=0),
    )


def lanes(shape):
    return lax.broadcasted_iota(jnp.int32, shape, len(shape) - 1)


def from_left(x):
    return jnp.where(lanes(x.shape) == 0, 0.0, pltpu.roll(x, 1, x.ndim - 1))


def from_right(x):
    width = x.shape[-1]
    return jnp.where(lanes(x.shape) == width - 1, 0.0, pltpu.roll(x, width - 1, x.ndim - 1))


def smooth(row, up, down):
    pair = from_right(row) + from_left(row)
    return row + diffusion * (down + up + pair - 4.0 * row)


def smooth_twice(above, own, below, top, bottom):
    f_up = top * smooth(above[1], above[0], own[0])
    f_0 = smooth(own[0], above[1], own[1])
    f_1 = smooth(own[1], own[0], below[0])
    f_down = bottom * smooth(below[0], own[1], below[1])
    return smooth(f_0, f_up, f_1), smooth(f_1, f_0, f_down)


def rows_of(ref, start, count):
    return [ref[pl.ds(start + r, count, stride=2), :] for r in range(2)]


def neighbours(even, a, b):
    keep = even != 0
    return [jnp.where(keep, y, x) for x, y in zip(a, b)], [jnp.where(keep, x, y) for x, y in zip(a, b)]


def mix_kernel(control, vertical, code, count, out, wide):
    levels = vertical.shape[0]
    members = control.shape[0]
    for k in range(members):
        wide[...] = control[k].astype(f32)
        for r in range(2):
            row = wide[pl.ds(r, levels, stride=2), :].astype(jnp.bfloat16)
            out[pl.ds(2 * levels * k + r, levels, stride=2), :] = jnp.dot(
                vertical[...], row, preferred_element_type=f32
            )
    width = code.shape[1]
    source = lax.broadcasted_iota(jnp.int32, (width, width // 2), 0)
    target = lax.broadcasted_iota(jnp.int32, (width, width // 2), 1)
    at = 2 * levels * members
    n = code.shape[0]
    for i, what in enumerate((code, count)):
        values = what[...].astype(f32)
        for phase in range(2):
            pick = jnp.where(source == 2 * target + phase, 1.0, 0.0)
            out[pl.ds(at + (2 * i + phase) * n, n), :] = jnp.dot(
                values, pick, preferred_element_type=f32, precision=lax.Precision.HIGHEST
            )


def partial_kernel(factor, place, mixed, side_a, side_b, ensemble, keep, send, local):
    members, variables, height = ensemble.shape[:3]
    levels = height // 2
    even, top, bottom, first_core = (place[i] for i in range(4))
    for k in range(members):
        at = k * height
        above, below = neighbours(even, rows_of(side_a, at, levels), rows_of(side_b, at, levels))
        both = smooth_twice(
            above, rows_of(mixed, at, levels), below, top.astype(f32), bottom.astype(f32)
        )
        for r in range(2):
            local[k, pl.ds(r, levels, stride=2), :] = both[r]
    mine = first_core != 0
    for j in range(keep.shape[0]):
        at = pl.ds(16 * j, 16)
        fields = [local[k, at, :] for k in range(members)]
        for v in range(variables):
            total = ensemble[0, v, at, :].astype(f32) * fields[0]
            for k in range(1, members):
                total = total + ensemble[k, v, at, :].astype(f32) * fields[k]
            total = factor * total
            keep[j, v] = jnp.where(mine, total[:8], total[8:])
            send[j, v] = jnp.where(mine, total[8:], total[:8])


def pair_sum_kernel(place, keep, gathered, out):
    first = place[3] != 0
    for j in range(out.shape[0]):
        out[j] = keep[j] + jnp.where(first, gathered[1, j], gathered[0, j])


def total_kernel(arrived, out):
    total = arrived[0]
    for j in range(1, arrived.shape[0]):
        total = total + arrived[j]
    out[...] = total


def observe_kernel(place, share, swap_b, pair_a, meta, meta_a, meta_b, weights, out, rows):
    even, top, bottom = (place[i] for i in range(3))
    n = share.shape[0] // 2
    own = rows_of(share, 0, n)
    keep_even = even != 0
    a = [
        jnp.where(keep_even, pair_a[1, pl.ds(r, n, stride=2), :], pair_a[0, pl.ds(r, n, stride=2), :])
        for r in range(2)
    ]
    above, below = neighbours(even, a, rows_of(swap_b, 0, n))
    u = dict(zip(range(-2, 4), above + own + below))
    top, bottom = top.astype(f32), bottom.astype(f32)

    def inside(f):
        return top if f < 0 else bottom if f > 3 else None

    def masked(x, f):
        scale = inside(f)
        return x if scale is None else x * scale

    fine = {}
    for f in range(-3, 7):
        a_row = f // 2
        other = a_row - 1 if f % 2 == 0 else a_row + 1
        line = near_weight * u[a_row] + far_weight * u[other]
        fine[f] = [
            masked(near_weight * line + far_weight * from_left(line), f),
            masked(near_weight * line + far_weight * from_right(line), f),
        ]
    wanted_above, wanted_below = neighbours(even, [meta_a[...]], [meta_b[...]])
    table = [wanted_above[0], meta[...], wanted_below[0]]

    def lookup(which, phase, f):
        block, line = (f + 4) // 4, f % 4
        at = (2 * which + phase) * 4 + line
        return table[block][at : at + 1, :]

    scale = weights[...]
    forcing, first, second, third, fourth = {}, {}, {}, {}, {}
    for f in range(-2, 6):
        e, o = fine[f]
        nexts = (o, from_right(e))
        previous = (from_left(o), e)
        for phase in range(2):
            code = lookup(0, phase, f)
            count = lookup(1, phase, f)
            m = [(code == float(which)).astype(f32) for which in range(1, 5)]
            diff = fine[f][phase] - m[0] * fine[f + 1][phase] - m[1] * fine[f - 1][phase]
            diff = diff - m[2] * nexts[phase] - m[3] * previous[phase]
            value = count * scale * diff
            forcing[f, phase] = value
            first[f, phase] = m[0] * value
            second[f, phase] = m[1] * value
            third[f, phase] = m[2] * value
            fourth[f, phase] = m[3] * value
    adjoint = {}
    for f in range(-1, 5):
        came_left = (from_left(third[f, 1]), third[f, 0])
        came_right = (fourth[f, 1], from_right(fourth[f, 0]))
        for phase in range(2):
            value = forcing[f, phase] - first[f - 1, phase] - second[f + 1, phase]
            adjoint[f, phase] = masked(value - came_left[phase] - came_right[phase], f)
    for a_row in range(2):
        f = 2 * a_row
        e, o = (
            near_weight * (adjoint[f, p] + adjoint[f + 1, p])
            + far_weight * (adjoint[f - 1, p] + adjoint[f + 2, p])
            for p in range(2)
        )
        result = near_weight * (e + o) + far_weight * (from_left(o) + from_right(e))
        rows[pl.ds(a_row, n, stride=2), :] = result
    variables = out.shape[1]
    for v in range(variables):
        tile = rows[8 * v : 8 * v + 8, :]
        for j in range(out.shape[0]):
            out[j, v] = tile


def project_kernel(factor, adjoint, ensemble, out):
    members, variables, height = ensemble.shape[:3]
    for j in range(adjoint.shape[1]):
        at = pl.ds(16 * j, 16)
        for k in range(members):
            total = None
            for v in range(variables):
                wide = jnp.concatenate([adjoint[0, j, v], adjoint[1, j, v]], axis=0)
                term = ensemble[k, v, at, :].astype(f32) * wide
                total = term if total is None else total + term
            out[pl.ds(k * height + 16 * j, 16), :] = factor * total


def product_kernel(place, projected, side_a, side_b, control, transposed, out, wide):
    members, height = control.shape[:2]
    levels = height // 2
    even, top, bottom = (place[i] for i in range(3))
    for k in range(members):
        at = k * height
        above, below = neighbours(even, rows_of(side_a, at, levels), rows_of(side_b, at, levels))
        both = smooth_twice(
            above, rows_of(projected, at, levels), below, top.astype(f32), bottom.astype(f32)
        )
        wide[...] = control[k].astype(f32)
        for r in range(2):
            back = jnp.dot(
                transposed[...], both[r].astype(jnp.bfloat16), preferred_element_type=f32
            )
            out[k, pl.ds(r, levels, stride=2), :] = wide[pl.ds(r, levels, stride=2), :] + back


def per_device(ensemble, control, vertical, inverse_var, obs_code, obs_count):
    members, variables, levels, own_rows, width = ensemble.shape
    mem_size, grid_size = lax.axis_size("mem"), lax.axis_size("grid")
    factor = (members * mem_size) ** (-0.5)
    height = levels * own_rows
    half = mem_size // 2
    per_owner = levels // mem_size
    assert own_rows == 2 and per_owner * own_rows == 8
    mem_at, grid_at = lax.axis_index("mem"), lax.axis_index("grid")
    place = jnp.stack(
        [
            (grid_at % 2 == 0).astype(jnp.int32),
            (grid_at > 0).astype(jnp.int32),
            (grid_at < grid_size - 1).astype(jnp.int32),
            (mem_at % 2 == 0).astype(jnp.int32),
        ]
    )
    swap_a = [(i, i ^ 1) for i in range(grid_size)]
    swap_b = [(i, ((i + 1) ^ 1) - 1) for i in range(1, grid_size - 1)]
    pairs_a = [[2 * i, 2 * i + 1] for i in range(grid_size // 2)]
    cores = [[2 * i, 2 * i + 1] for i in range(half)]
    same_core = [[2 * i + c for i in range(half)] for c in range(2)]

    ens = ensemble.reshape(members, variables, height, width)
    ctl = control.reshape(members, height, width)
    meta_rows = 4 * obs_code.shape[0]
    sent_rows = members * height + meta_rows

    mixed = call(
        mix_kernel,
        jax.ShapeDtypeStruct((sent_rows, width), f32),
        4,
        [pltpu.VMEM((height, width), f32)],
        scalars=0,
    )(ctl, vertical, obs_code, obs_count)
    mixed_b = lax.ppermute(mixed, "grid", swap_b)
    mixed_a = lax.ppermute(mixed, "grid", swap_a)

    block = jax.ShapeDtypeStruct((half, variables, 8, width), f32)
    keep, send = call(
        functools.partial(partial_kernel, factor),
        (block, block),
        5,
        [pltpu.VMEM((members, height, width), f32)],
    )(place, mixed, mixed_a, mixed_b, ens)
    gathered = lax.all_gather(send, "mem", axis=0, axis_index_groups=cores)
    paired = call(pair_sum_kernel, block, 3)(place, keep, gathered)
    arrived = lax.all_to_all(paired, "mem", 0, 0, axis_index_groups=same_core, tiled=True)
    share = call(
        total_kernel, jax.ShapeDtypeStruct((variables, 8, width), f32), 1, scalars=0
    )(arrived).reshape(variables * 8, width)

    share_b = lax.ppermute(share, "grid", swap_b)
    share_a = lax.all_gather(share, "grid", axis=0, axis_index_groups=pairs_a)
    weights = lax.dynamic_slice_in_dim(inverse_var, mem_at * per_owner, per_owner, 1)
    weights = jnp.broadcast_to(weights.reshape(-1, 1), (variables * per_owner, width))
    meta, meta_a, meta_b = (x[members * height :] for x in (mixed, mixed_a, mixed_b))
    spread = call(
        observe_kernel, block, 8, [pltpu.VMEM((variables * 8, width), f32)]
    )(place, share, share_b, share_a, meta, meta_a, meta_b, weights)
    mine = lax.all_to_all(spread, "mem", 0, 0, axis_index_groups=same_core, tiled=True)
    adjoint = lax.all_gather(mine, "mem", axis=0, axis_index_groups=cores)

    projected = call(
        functools.partial(project_kernel, factor),
        jax.ShapeDtypeStruct((members * height, width), f32),
        2,
        scalars=0,
    )(adjoint, ens)
    projected_b = lax.ppermute(projected, "grid", swap_b)
    projected_a = lax.ppermute(projected, "grid", swap_a)
    out = call(
        product_kernel,
        jax.ShapeDtypeStruct((members, height, width), f32),
        6,
        [pltpu.VMEM((height, width), f32)],
    )(place, projected, projected_a, projected_b, ctl, vertical.T)
    return out.reshape(control.shape)


def solution(mesh):
    return jax.shard_map(
        per_device,
        mesh=mesh,
        in_specs=(
            P("mem", None, None, "grid", None),
            P("mem", None, "grid", None),
            P(),
            P(),
            P("grid", None),
            P("grid", None),
        ),
        out_specs=P("mem", None, "grid", None),
        check_vma=False,
    )
```

time: 149 us -> 99.9 us (0.67)
  the two profiles are of different devices: /device:TPU:198 before, /device:TPU:195 now
where the time goes in v1:
time: 99.9 us; the launch traced here: 99.4 us
  waiting for transfers between devices  36.4 us (36%)
  starting transfers between devices  26.5 us (27%)
  blocking collectives  26 us (26%)
  Pallas kernels  5.84 us (6%)
  local copies, waits for them, and re-layouts  4.45 us (4%)
    all_to_all x1, blocking collectives, per_device(): lax.all_to_all(spread, 'mem', 0, 0, axis_index_groups=same_core, tiled=True)  14.2 us
    all_to_all x1, waiting for transfers between devices, per_device(): lax.all_to_all(paired, 'mem', 0, 0, axis_index_groups=same_core, tiled=True)  12.5 us
    all_to_all x1, starting transfers between devices, per_device(): lax.all_to_all(paired, 'mem', 0, 0, axis_index_groups=same_core, tiled=True)  8.49 us
    ppermute x1, waiting for transfers between devices, per_device(): mixed_a = lax.ppermute(mixed, 'grid', swap_a)  6.83 us
    ppermute x1, waiting for transfers between devices, per_device(): projected_b = lax.ppermute(projected, 'grid', swap_b)  6.6 us
    ppermute x1, waiting for transfers between devices, per_device(): projected_a = lax.ppermute(projected, 'grid', swap_a)  6.31 us
    all_gather x1, blocking collectives, per_device(): adjoint = lax.all_gather(mine, 'mem', axis=0, axis_index_groups=cores)  6.12 us
    ppermute x1, starting transfers between devices, per_device(): share_b = lax.ppermute(share, 'grid', swap_b)  6.08 us
  transfers between devices with their start and end apart: 6, of which 5 were waited for; matrix products, arithmetic and copies ran while one was open for 0% of the time, Pallas kernels for 0%

profile of v1, /device:TPU:195, one launch (start us, length us, event | category | flops | bytes accessed | tf_op | source)
XLA Modules:
  0.0 99.4 jit_solution(16822738862832691752)
XLA Ops:
  0.0 0.0 copy-start
  0.0 0.0 copy-start.3
  0.0 0.9 copy-done.3
  0.9 0.0 copy-start.5
  0.9 0.8 copy-done.5
  1.7 0.0 copy-start.7
  1.7 0.7 copy-done.7
  2.4 0.0 copy-start.8
  2.4 0.7 copy-done.8
  3.1 0.4 shard_map.64.mixed
  3.4 5.2 %collective-permute-start.1 = (f32[528,128]{1,0:T(8,128)S(1)}, f32[528,128]{1,0:T(8,128)S(1)}, u32[]{:S(2)}, u32[]{:S(2)}) collective-permute-start(f32[528,128]{1,0:T(8,128)S(1)} %shard_map.64.mixed), channel_id=1, source_target_pairs={{1,2},{2,1},{3,4},{4,3},{5,6},{6,5},{7,8},{8,7},{9,10},{10,9},{11,... | collective-permute-start | bytes 811016 | tf_op jit(solution)/shard_map/ppermute | solution.py:271
  8.6 1.9 %collective-permute-start = (f32[528,128]{1,0:T(8,128)S(1)}, f32[528,128]{1,0:T(8,128)S(1)}, u32[]{:S(2)}, u32[]{:S(2)}) collective-permute-start(f32[528,128]{1,0:T(8,128)S(1)} %shard_map.64.mixed), channel_id=1, source_target_pairs={{0,1},{1,0},{2,3},{3,2},{4,5},{5,4},{6,7},{7,6},{8,9},{9,8},{10,11... | collective-permute-start | bytes 811016 | tf_op jit(solution)/shard_map/ppermute | solution.py:272
  10.6 0.1 add_convert_fusion.place
  10.7 4.1 %collective-permute-done.1.side_b = f32[528,128]{1,0:T(8,128)S(1)} collective-permute-done((f32[528,128]{1,0:T(8,128)S(1)}, f32[528,128]{1,0:T(8,128)S(1)}, u32[]{:S(2)}, u32[]{:S(2)}) %collective-permute-start.1) | collective-permute-done | bytes 270368 | tf_op jit(solution)/shard_map/ppermute | solution.py:271
  14.8 6.8 %collective-permute-done.side_a = f32[528,128]{1,0:T(8,128)S(1)} collective-permute-done((f32[528,128]{1,0:T(8,128)S(1)}, f32[528,128]{1,0:T(8,128)S(1)}, u32[]{:S(2)}, u32[]{:S(2)}) %collective-permute-start) | collective-permute-done | bytes 270368 | tf_op jit(solution)/shard_map/ppermute | solution.py:272
  21.6 0.0 copy-start.1
  21.7 1.0 %copy-done.1 = bf16[2,4,128,2,128]{4,3,2,1,0:T(2,128)(2,1)S(1)} copy-done((bf16[2,4,128,2,128]{4,3,2,1,0:T(2,128)(2,1)S(1)}, bf16[2,4,128,2,128]{4,3,2,1,0:T(2,128)(2,1)}, u32[]{:S(2)}) %copy-start.1) | copy-done | bytes 524312
  22.7 1.2 %shard_map.65 = (f32[16,4,8,128]{3,2,1,0:T(8,128)S(1)}, f32[16,4,8,128]{3,2,1,0:T(8,128)S(1)}) custom-call(s32[4]{0:T(128)S(1)} %add_convert_fusion.place, f32[528,128]{1,0:T(8,128)S(1)} %shard_map.64.mixed, f32[528,128]{1,0:T(8,128)S(1)} %collective-permute-done.side_a, f32[528,128]{1,0:T(8,128)S(1)} %collective-permute-done.1.side_b, ...), custom_call_target="tpu_custom_call" | custom-call | flops 1000000 | bytes 1000000 | tf_op jit(solution)/shard_map/pallas_call | solution.py:275
  23.9 2.3 %all-gather = f32[32,4,8,128]{3,2,1,0:T(8,128)S(1)} all-gather(f32[16,4,8,128]{3,2,1,0:T(8,128)S(1)} %get-tuple-element.8), channel_id=2, replica_groups={{0,16},{32,48},{64,80},{96,112},{128,144},{160,176},{192,208},{224,240}..., dimensions={0}, use_global_device_ids=true | all-gather | bytes 786432 | tf_op jit(solution)/shard_map/all_gather | solution.py:281
  26.2 1.3 %shard_map.66 = f32[16,4,8,128]{3,2,1,0:T(8,128)} custom-call(s32[4]{0:T(128)S(1)} %add_convert_fusion.place, f32[16,4,8,128]{3,2,1,0:T(8,128)S(1)} %get-tuple-element.7.keep, f32[2,16,4,8,128]{4,3,2,1,0:T(8,128)S(1)} %bitcast.14), custom_call_target="tpu_custom_call" | custom-call | flops 1000000 | bytes 1000000 | tf_op jit(solution)/shard_map/pallas_call | solution.py:282
  27.5 8.5 %all-to-all-start = ((f32[16,4,8,128]{3,2,1,0:T(8,128)}), f32[16,4,8,128]{3,2,1,0:T(8,128)S(1)}, u32[]{:S(2)}, u32[]{:S(2)}) async-start(f32[16,4,8,128]{3,2,1,0:T(8,128)} %shard_map.66), calls=%async_computation | async-start | bytes 524288 | tf_op jit(solution)/shard_map/all_to_all | solution.py:283
  36.0 12.5 %all-to-all-done.arrived = f32[16,4,8,128]{3,2,1,0:T(8,128)S(1)} async-done(((f32[16,4,8,128]{3,2,1,0:T(8,128)}), f32[16,4,8,128]{3,2,1,0:T(8,128)S(1)}, u32[]{:S(2)}, u32[]{:S(2)}) %all-to-all-start) | async-done | bytes 262176 | tf_op jit(solution)/shard_map/all_to_all | solution.py:283
  48.5 6.1 %collective-permute-start.2 = (f32[32,128]{1,0:T(8,128)S(1)}, f32[32,128]{1,0:T(8,128)S(1)}, u32[]{:S(2)}, u32[]{:S(2)}) collective-permute-start(f32[32,128]{1,0:T(8,128)S(1)} %bitcast.18), channel_id=1, source_target_pairs={{1,2},{2,1},{3,4},{4,3},{5,6},{6,5},{7,8},{8,7},{9,10},{10,9},{11,... | collective-permute-start | bytes 49160 | tf_op jit(solution)/shard_map/ppermute | solution.py:288
  54.6 0.0 copy-done
  54.6 0.1 constant_dynamic-slice_fusion
  54.7 0.1 broadcast_in_dim.7
  54.8 3.4 %all_gather.17.pair_a = f32[2,32,128]{2,1,0:T(8,128)S(1)} all-gather(f32[1,32,128]{2,1,0:T(8,128)S(1)} %bitcast.19), channel_id=1, replica_groups={{0,1},{2,3},{4,5},{6,7},{8,9},{10,11},{12,13},{14,15},{16,17},{18,19},{..., dimensions={0}, use_global_device_ids=true | all-gather | bytes 49152 | tf_op jit(solution)/shard_map/all_gather | solution.py:289
  58.1 0.0 collective-permute-done.2.swap_b
  58.1 0.1 broadcast_in_dim.8.weights
  58.2 0.9 shard_map.68
  59.1 14.2 %all_to_all.10 = f32[16,4,8,128]{3,2,1,0:T(8,128)S(1)} all-to-all(f32[16,4,8,128]{3,2,1,0:T(8,128)S(1)} %shard_map.68), channel_id=1, replica_groups={{0,32,64,96,128,160,192,224,256,288,320,352,384,416,448,480},{16,48,80,..., dimensions={0} | all-to-all | bytes 524288 | tf_op jit(solution)/shard_map/all_to_all | solution.py:296
  73.4 0.0 copy-start.2
  73.4 6.1 %all-gather.1 = f32[32,4,8,128]{3,2,1,0:T(8,128)S(1)} all-gather(f32[16,4,8,128]{3,2,1,0:T(8,128)S(1)} %all_to_all.10), channel_id=3, replica_groups={{0,16},{32,48},{64,80},{96,112},{128,144},{160,176},{192,208},{224,240}..., dimensions={0}, use_global_device_ids=true | all-gather | bytes 786432 | tf_op jit(solution)/shard_map/all_gather | solution.py:297
  79.5 0.0 copy-done.2
  79.5 0.0 copy-start.6
  79.5 0.0 copy-start.4
  79.5 0.1 shard_map.69.projected
  79.6 2.9 %collective-permute-start.4 = (f32[512,128]{1,0:T(8,128)S(1)}, f32[512,128]{1,0:T(8,128)S(1)}, u32[]{:S(2)}, u32[]{:S(2)}) collective-permute-start(f32[512,128]{1,0:T(8,128)S(1)} %shard_map.69.projected), channel_id=1, source_target_pairs={{1,2},{2,1},{3,4},{4,3},{5,6},{6,5},{7,8},{8,7},{9,10},{10,9},{11,... | collective-permute-start | bytes 786440 | tf_op jit(solution)/shard_map/ppermute | solution.py:305
  82.5 1.9 %collective-permute-start.3 = (f32[512,128]{1,0:T(8,128)S(1)}, f32[512,128]{1,0:T(8,128)S(1)}, u32[]{:S(2)}, u32[]{:S(2)}) collective-permute-start(f32[512,128]{1,0:T(8,128)S(1)} %shard_map.69.projected), channel_id=1, source_target_pairs={{0,1},{1,0},{2,3},{3,2},{4,5},{5,4},{6,7},{7,6},{8,9},{9,8},{10,11... | collective-permute-start | bytes 786440 | tf_op jit(solution)/shard_map/ppermute | solution.py:306
  84.4 0.0 copy-done.6
  84.4 0.1 copy.8
  84.6 6.6 %collective-permute-done.4.side_b = f32[512,128]{1,0:T(8,128)S(1)} collective-permute-done((f32[512,128]{1,0:T(8,128)S(1)}, f32[512,128]{1,0:T(8,128)S(1)}, u32[]{:S(2)}, u32[]{:S(2)}) %collective-permute-start.4) | collective-permute-done | bytes 262176 | tf_op jit(solution)/shard_map/ppermute | solution.py:305
  91.1 6.3 %collective-permute-done.3.side_a = f32[512,128]{1,0:T(8,128)S(1)} collective-permute-done((f32[512,128]{1,0:T(8,128)S(1)}, f32[512,128]{1,0:T(8,128)S(1)}, u32[]{:S(2)}, u32[]{:S(2)}) %collective-permute-start.3) | collective-permute-done | bytes 262176 | tf_op jit(solution)/shard_map/ppermute | solution.py:306
  97.5 0.0 copy-done.4
  97.5 1.9 %shard_map.70 = f32[2,256,128]{2,1,0:T(8,128)} custom-call(s32[4]{0:T(128)S(1)} %add_convert_fusion.place, f32[512,128]{1,0:T(8,128)S(1)} %shard_map.69.projected, f32[512,128]{1,0:T(8,128)S(1)} %collective-permute-done.3.side_a, f32[512,128]{1,0:T(8,128)S(1)} %collective-permute-done.4.side_b, bf16[2,256,128]{2,1,0:T(8,128)(2,1)S(1)} %bitcast.17, ...), custom_call_target="tpu_custom_call" | custom-call | flops 1000000 | bytes 1000000 | tf_op jit(solution)/shard_map/pallas_call | solution.py:307
  (4 shorter events, 0.0 us)
Async XLA Ops:
  0.0 54.6 %copy-start = (f32[4,128]{1,0:T(4,128)S(1)}, f32[4,128]{1,0:T(4,128)}, u32[]{:S(2)}) copy-start(f32[4,128]{1,0:T(4,128)} %param.9) | copy-start | bytes 6148
  0.0 0.9 copy-start.3
  0.9 0.8 copy-start.5
  1.7 0.7 copy-start.7
  2.4 0.7 copy-start.8
  3.4 11.4 %collective-permute-start.1 = (f32[528,128]{1,0:T(8,128)S(1)}, f32[528,128]{1,0:T(8,128)S(1)}, u32[]{:S(2)}, u32[]{:S(2)}) collective-permute-start(f32[528,128]{1,0:T(8,128)S(1)} %shard_map.64.mixed), channel_id=1, source_target_pairs={{1,2},{2,1},{3,4},{4,3},{5,6},{6,5},{7,8},{8,7},{9,10},{10,9},{11,... | collective-permute-start | bytes 811016 | tf_op jit(solution)/shard_map/ppermute | solution.py:271
  8.6 13.0 %collective-permute-start = (f32[528,128]{1,0:T(8,128)S(1)}, f32[528,128]{1,0:T(8,128)S(1)}, u32[]{:S(2)}, u32[]{:S(2)}) collective-permute-start(f32[528,128]{1,0:T(8,128)S(1)} %shard_map.64.mixed), channel_id=1, source_target_pairs={{0,1},{1,0},{2,3},{3,2},{4,5},{5,4},{6,7},{7,6},{8,9},{9,8},{10,11... | collective-permute-start | bytes 811016 | tf_op jit(solution)/shard_map/ppermute | solution.py:272
  21.6 1.0 %copy-start.1 = (bf16[2,4,128,2,128]{4,3,2,1,0:T(2,128)(2,1)S(1)}, bf16[2,4,128,2,128]{4,3,2,1,0:T(2,128)(2,1)}, u32[]{:S(2)}) copy-start(bf16[2,4,128,2,128]{4,3,2,1,0:T(2,128)(2,1)} %param.6) | copy-start | bytes 1572868
  27.5 21.0 %all-to-all-start = ((f32[16,4,8,128]{3,2,1,0:T(8,128)}), f32[16,4,8,128]{3,2,1,0:T(8,128)S(1)}, u32[]{:S(2)}, u32[]{:S(2)}) async-start(f32[16,4,8,128]{3,2,1,0:T(8,128)} %shard_map.66), calls=%async_computation | async-start | bytes 524288 | tf_op jit(solution)/shard_map/all_to_all | solution.py:283
  48.5 9.6 %collective-permute-start.2 = (f32[32,128]{1,0:T(8,128)S(1)}, f32[32,128]{1,0:T(8,128)S(1)}, u32[]{:S(2)}, u32[]{:S(2)}) collective-permute-start(f32[32,128]{1,0:T(8,128)S(1)} %bitcast.18), channel_id=1, source_target_pairs={{1,2},{2,1},{3,4},{4,3},{5,6},{6,5},{7,8},{8,7},{9,10},{10,9},{11,... | collective-permute-start | bytes 49160 | tf_op jit(solution)/shard_map/ppermute | solution.py:288
  73.4 6.1 %copy-start.2 = (bf16[2,4,128,2,128]{4,3,2,1,0:T(2,128)(2,1)S(1)}, bf16[2,4,128,2,128]{4,3,2,1,0:T(2,128)(2,1)}, u32[]{:S(2)}) copy-start(bf16[2,4,128,2,128]{4,3,2,1,0:T(2,128)(2,1)} %param.6) | copy-start | bytes 1572868
  79.5 4.9 %copy-start.6 = (bf16[128,128]{1,0:T(8,128)(2,1)S(1)}, bf16[128,128]{1,0:T(8,128)(2,1)}, u32[]{:S(2)}) copy-start(bf16[128,128]{1,0:T(8,128)(2,1)} %vertical.1) | copy-start | bytes 98308
  79.5 18.0 %copy-start.4 = (bf16[2,128,2,128]{3,2,1,0:T(2,128)(2,1)S(1)}, bf16[2,128,2,128]{3,2,1,0:T(2,128)(2,1)}, u32[]{:S(2)}) copy-start(bf16[2,128,2,128]{3,2,1,0:T(2,128)(2,1)} %param.7) | copy-start | bytes 393220
  79.6 11.5 %collective-permute-start.4 = (f32[512,128]{1,0:T(8,128)S(1)}, f32[512,128]{1,0:T(8,128)S(1)}, u32[]{:S(2)}, u32[]{:S(2)}) collective-permute-start(f32[512,128]{1,0:T(8,128)S(1)} %shard_map.69.projected), channel_id=1, source_target_pairs={{1,2},{2,1},{3,4},{4,3},{5,6},{6,5},{7,8},{8,7},{9,10},{10,9},{11,... | collective-permute-start | bytes 786440 | tf_op jit(solution)/shard_map/ppermute | solution.py:305
  82.5 15.0 %collective-permute-start.3 = (f32[512,128]{1,0:T(8,128)S(1)}, f32[512,128]{1,0:T(8,128)S(1)}, u32[]{:S(2)}, u32[]{:S(2)}) collective-permute-start(f32[512,128]{1,0:T(8,128)S(1)} %shard_map.69.projected), channel_id=1, source_target_pairs={{0,1},{1,0},{2,3},{3,2},{4,5},{5,4},{6,7},{7,6},{8,9},{9,8},{10,11... | collective-permute-start | bytes 786440 | tf_op jit(solution)/shard_map/ppermute | solution.py:306

commit v2 on v1

--- a/solution.py
+++ b/solution.py
@@ -15,12 +15,15 @@
 f32 = jnp.float32
 
 
-def call(body, out_shapes, n_in, scratch=(), flops=1000000, scalars=1):
+ANY = pl.BlockSpec(memory_space=pl.ANY)
+
+
+def call(body, out_shapes, in_specs, scratch=(), flops=1000000, out_spec=VMEM):
     return pl.pallas_call(
         body,
         out_shape=out_shapes,
-        in_specs=[SMEM] * scalars + [VMEM] * (n_in - scalars),
-        out_specs=jax.tree.map(lambda _: VMEM, out_shapes),
+        in_specs=list(in_specs),
+        out_specs=jax.tree.map(lambda _: out_spec, out_shapes),
         scratch_shapes=list(scratch),
         compiler_params=pltpu.CompilerParams(vmem_limit_bytes=24 * 1024 * 1024),
         cost_estimate=pl.CostEstimate(flops=flops, bytes_accessed=1000000, transcendentals=0),
@@ -62,7 +65,7 @@
     return [jnp.where(keep, y, x) for x, y in zip(a, b)], [jnp.where(keep, x, y) for x, y in zip(a, b)]
 
 
-def mix_kernel(control, vertical, code, count, out, wide):
+def mix_kernel(control, vertical, out, wide):
     levels = vertical.shape[0]
     members = control.shape[0]
     for k in range(members):
@@ -72,21 +75,23 @@
             out[pl.ds(2 * levels * k + r, levels, stride=2), :] = jnp.dot(
                 vertical[...], row, preferred_element_type=f32
             )
+
+
+def meta_kernel(after, code, count, ensemble, out):
     width = code.shape[1]
     source = lax.broadcasted_iota(jnp.int32, (width, width // 2), 0)
     target = lax.broadcasted_iota(jnp.int32, (width, width // 2), 1)
-    at = 2 * levels * members
     n = code.shape[0]
     for i, what in enumerate((code, count)):
         values = what[...].astype(f32)
         for phase in range(2):
             pick = jnp.where(source == 2 * target + phase, 1.0, 0.0)
-            out[pl.ds(at + (2 * i + phase) * n, n), :] = jnp.dot(
+            out[pl.ds((2 * i + phase) * n, n), :] = jnp.dot(
                 values, pick, preferred_element_type=f32, precision=lax.Precision.HIGHEST
             )
 
 
-def partial_kernel(factor, place, mixed, side_a, side_b, ensemble, keep, send, local):
+def partial_kernel(factor, place, after, mixed, side_a, side_b, ensemble, keep, send, local):
     members, variables, height = ensemble.shape[:3]
     levels = height // 2
     even, top, bottom, first_core = (place[i] for i in range(4))
@@ -117,16 +122,20 @@
         out[j] = keep[j] + jnp.where(first, gathered[1, j], gathered[0, j])
 
 
-def total_kernel(arrived, out):
+def total_kernel(arrived, meta, out):
     total = arrived[0]
     for j in range(1, arrived.shape[0]):
         total = total + arrived[j]
-    out[...] = total
-
-
-def observe_kernel(place, share, swap_b, pair_a, meta, meta_a, meta_b, weights, out, rows):
+    rows = 8 * total.shape[0]
+    for v in range(total.shape[0]):
+        out[8 * v : 8 * v + 8, :] = total[v]
+    out[rows:, :] = meta[...]
+
+
+def observe_kernel(place, share, swap_b, pair_a, weights, out, rows):
     even, top, bottom = (place[i] for i in range(3))
-    n = share.shape[0] // 2
+    height = rows.shape[0]
+    n = height // 2
     own = rows_of(share, 0, n)
     keep_even = even != 0
     a = [
@@ -153,8 +162,9 @@
             masked(near_weight * line + far_weight * from_left(line), f),
             masked(near_weight * line + far_weight * from_right(line), f),
         ]
-    wanted_above, wanted_below = neighbours(even, [meta_a[...]], [meta_b[...]])
-    table = [wanted_above[0], meta[...], wanted_below[0]]
+    meta_a = jnp.where(keep_even, pair_a[1, height:, :], pair_a[0, height:, :])
+    wanted_above, wanted_below = neighbours(even, [meta_a], [swap_b[height:, :]])
+    table = [wanted_above[0], share[height:, :], wanted_below[0]]
 
     def lookup(which, phase, f):
         block, line = (f + 4) // 4, f % 4
@@ -215,7 +225,7 @@
             out[pl.ds(k * height + 16 * j, 16), :] = factor * total
 
 
-def product_kernel(place, projected, side_a, side_b, control, transposed, out, wide):
+def product_kernel(place, projected, side_a, side_b, control, transposed, far, out, wide, sems):
     members, height = control.shape[:2]
     levels = height // 2
     even, top, bottom = (place[i] for i in range(3))
@@ -231,6 +241,9 @@
                 transposed[...], both[r].astype(jnp.bfloat16), preferred_element_type=f32
             )
             out[k, pl.ds(r, levels, stride=2), :] = wide[pl.ds(r, levels, stride=2), :] + back
+        pltpu.make_async_copy(out.at[k], far.at[k], sems.at[k]).start()
+    for k in range(members):
+        pltpu.make_async_copy(out.at[k], far.at[k], sems.at[k]).wait()
 
 
 def per_device(ensemble, control, vertical, inverse_var, obs_code, obs_count):
@@ -259,57 +272,69 @@
     ens = ensemble.reshape(members, variables, height, width)
     ctl = control.reshape(members, height, width)
     meta_rows = 4 * obs_code.shape[0]
-    sent_rows = members * height + meta_rows
 
     mixed = call(
         mix_kernel,
-        jax.ShapeDtypeStruct((sent_rows, width), f32),
-        4,
+        jax.ShapeDtypeStruct((members * height, width), f32),
+        [VMEM, VMEM],
         [pltpu.VMEM((height, width), f32)],
-        scalars=0,
-    )(ctl, vertical, obs_code, obs_count)
+    )(ctl, vertical)
     mixed_b = lax.ppermute(mixed, "grid", swap_b)
     mixed_a = lax.ppermute(mixed, "grid", swap_a)
+    meta = call(
+        meta_kernel, jax.ShapeDtypeStruct((meta_rows, width), f32), [ANY, VMEM, VMEM, VMEM]
+    )(mixed, obs_code, obs_count, ens)
+    weights = lax.dynamic_slice_in_dim(inverse_var, mem_at * per_owner, per_owner, 1)
+    weights = jnp.broadcast_to(weights.reshape(-1, 1), (variables * per_owner, width))
 
     block = jax.ShapeDtypeStruct((half, variables, 8, width), f32)
     keep, send = call(
         functools.partial(partial_kernel, factor),
         (block, block),
-        5,
+        [SMEM, ANY] + [VMEM] * 4,
         [pltpu.VMEM((members, height, width), f32)],
-    )(place, mixed, mixed_a, mixed_b, ens)
+    )(place, meta, mixed, mixed_a, mixed_b, ens)
     gathered = lax.all_gather(send, "mem", axis=0, axis_index_groups=cores)
-    paired = call(pair_sum_kernel, block, 3)(place, keep, gathered)
+    paired = call(pair_sum_kernel, block, [SMEM, VMEM, VMEM])(place, keep, gathered)
+    turned = vertical.T
+    paired, meta, weights, place, turned = lax.optimization_barrier(
+        (paired, meta, weights, place, turned)
+    )
     arrived = lax.all_to_all(paired, "mem", 0, 0, axis_index_groups=same_core, tiled=True)
     share = call(
-        total_kernel, jax.ShapeDtypeStruct((variables, 8, width), f32), 1, scalars=0
-    )(arrived).reshape(variables * 8, width)
+        total_kernel, jax.ShapeDtypeStruct((variables * 8 + meta_rows, width), f32), [VMEM, VMEM]
+    )(arrived, meta)
 
     share_b = lax.ppermute(share, "grid", swap_b)
     share_a = lax.all_gather(share, "grid", axis=0, axis_index_groups=pairs_a)
-    weights = lax.dynamic_slice_in_dim(inverse_var, mem_at * per_owner, per_owner, 1)
-    weights = jnp.broadcast_to(weights.reshape(-1, 1), (variables * per_owner, width))
-    meta, meta_a, meta_b = (x[members * height :] for x in (mixed, mixed_a, mixed_b))
     spread = call(
-        observe_kernel, block, 8, [pltpu.VMEM((variables * 8, width), f32)]
-    )(place, share, share_b, share_a, meta, meta_a, meta_b, weights)
+        observe_kernel,
+        block,
+        [SMEM] + [VMEM] * 4,
+        [pltpu.VMEM((variables * 8, width), f32)],
+    )(place, share, share_b, share_a, weights)
     mine = lax.all_to_all(spread, "mem", 0, 0, axis_index_groups=same_core, tiled=True)
     adjoint = lax.all_gather(mine, "mem", axis=0, axis_index_groups=cores)
 
     projected = call(
         functools.partial(project_kernel, factor),
         jax.ShapeDtypeStruct((members * height, width), f32),
-        2,
-        scalars=0,
+        [VMEM, VMEM],
     )(adjoint, ens)
     projected_b = lax.ppermute(projected, "grid", swap_b)
     projected_a = lax.ppermute(projected, "grid", swap_a)
+    whole = jax.ShapeDtypeStruct((members, height, width), f32)
     out = call(
         product_kernel,
-        jax.ShapeDtypeStruct((members, height, width), f32),
-        6,
-        [pltpu.VMEM((height, width), f32)],
-    )(place, projected, projected_a, projected_b, ctl, vertical.T)
+        whole,
+        [SMEM] + [VMEM] * 5,
+        [
+            pltpu.VMEM(whole.shape, f32),
+            pltpu.VMEM((height, width), f32),
+            pltpu.SemaphoreType.DMA((members,)),
+        ],
+        out_spec=ANY,
+    )(place, projected, projected_a, projected_b, ctl, turned)
     return out.reshape(control.shape)
 
 

time: 99.9 us -> 91.4 us (0.915)
  waiting for transfers between devices: 36.4 us -> 12.5 us
  blocking collectives: 26 us -> 48.4 us
  starting transfers between devices: 26.5 us -> 20.6 us
  local copies, waits for them, and re-layouts: 4.45 us -> 3.35 us
    all_to_all x0 -> x1, blocking collectives: none -> 20.8 us  [per_device(): lax.all_to_all(paired, 'mem', 0, 0, axis_index_groups=same_core, tiled=True)]
    all_to_all x1 -> x0, waiting for transfers between devices: 12.5 us -> none  [per_device(): lax.all_to_all(paired, 'mem', 0, 0, axis_index_groups=same_core, tiled=True)]
    all_to_all x1 -> x0, starting transfers between devices: 8.49 us -> none  [per_device(): lax.all_to_all(paired, 'mem', 0, 0, axis_index_groups=same_core, tiled=True)]
    ppermute x1, waiting for transfers between devices: 6.83 us -> 0.01 us  [per_device(): mixed_a = lax.ppermute(mixed, 'grid', swap_a)]
    ppermute x1, waiting for transfers between devices: 6.6 us -> 0.01 us  [per_device(): projected_b = lax.ppermute(projected, 'grid', swap_b)]
    ppermute x1, waiting for transfers between devices: 6.31 us -> 8.8 us  [per_device(): projected_a = lax.ppermute(projected, 'grid', swap_a)]
    all_gather x1, blocking collectives: 2.3 us -> 3.97 us  [per_device(): gathered = lax.all_gather(send, 'mem', axis=0, axis_index_groups=cores)]
    ppermute x1, starting transfers between devices: 2.88 us -> 4.27 us  [per_device(): projected_b = lax.ppermute(projected, 'grid', swap_b)]
  transfers between devices with their start and end apart: 6 -> 5, of which waited for: 5 -> 2; matrix products, arithmetic and copies ran while one was open for 0% -> 1% of each run, Pallas kernels for 0% -> 0%
where the time goes in v2:
time: 91.4 us; the launch traced here: 90.3 us
  blocking collectives  48.4 us (53%)
  starting transfers between devices  20.6 us (23%)
  waiting for transfers between devices  12.5 us (14%)
  Pallas kernels  5.22 us (6%)
  local copies, waits for them, and re-layouts  3.35 us (4%)
    all_to_all x1, blocking collectives, per_device(): lax.all_to_all(paired, 'mem', 0, 0, axis_index_groups=same_core, tiled=True)  20.8 us
    all_to_all x1, blocking collectives, per_device(): lax.all_to_all(spread, 'mem', 0, 0, axis_index_groups=same_core, tiled=True)  14.1 us
    ppermute x1, waiting for transfers between devices, per_device(): projected_a = lax.ppermute(projected, 'grid', swap_a)  8.8 us
    ppermute x1, starting transfers between devices, per_device(): mixed_b = lax.ppermute(mixed, 'grid', swap_b)  6.14 us
    ppermute x1, starting transfers between devices, per_device(): share_b = lax.ppermute(share, 'grid', swap_b)  6.08 us
    all_gather x1, blocking collectives, per_device(): adjoint = lax.all_gather(mine, 'mem', axis=0, axis_index_groups=cores)  5.99 us
    ppermute x1, starting transfers between devices, per_device(): projected_b = lax.ppermute(projected, 'grid', swap_b)  4.27 us
    all_gather x1, blocking collectives, per_device(): gathered = lax.all_gather(send, 'mem', axis=0, axis_index_groups=cores)  3.97 us
  transfers between devices with their start and end apart: 5, of which 2 were waited for; matrix products, arithmetic and copies ran while one was open for 1% of the time, Pallas kernels for 0%

profile of v2, /device:TPU:195, one launch (start us, length us, event | category | flops | bytes accessed | tf_op | source)
XLA Modules:
  0.0 90.3 jit_solution(6599532260926884836)
XLA Ops:
  0.0 0.0 copy-start
  0.0 0.0 copy-start.1
  0.0 0.0 copy-start.2
  0.0 1.0 %copy-done.2 = bf16[2,128,2,128]{3,2,1,0:T(2,128)(2,1)S(1)} copy-done((bf16[2,128,2,128]{3,2,1,0:T(2,128)(2,1)S(1)}, bf16[2,128,2,128]{3,2,1,0:T(2,128)(2,1)}, u32[]{:S(2)}) %copy-start.2) | copy-done | bytes 131096
  1.0 0.0 copy-start.4
  1.0 0.8 copy-done.4
  1.7 0.2 shard_map.64.after.mixed
  1.9 2.2 %collective-permute-start = (f32[512,128]{1,0:T(8,128)S(1)}, f32[512,128]{1,0:T(8,128)S(1)}, u32[]{:S(2)}, u32[]{:S(2)}) collective-permute-start(f32[512,128]{1,0:T(8,128)S(1)} %shard_map.64.after.mixed), channel_id=1, source_target_pairs={{0,1},{1,0},{2,3},{3,2},{4,5},{5,4},{6,7},{7,6},{8,9},{9,8},{10,11... | collective-permute-start | bytes 786440 | tf_op jit(solution)/shard_map/ppermute | solution.py:283
  4.1 6.1 %collective-permute-start.1 = (f32[512,128]{1,0:T(8,128)S(1)}, f32[512,128]{1,0:T(8,128)S(1)}, u32[]{:S(2)}, u32[]{:S(2)}) collective-permute-start(f32[512,128]{1,0:T(8,128)S(1)} %shard_map.64.after.mixed), channel_id=1, source_target_pairs={{1,2},{2,1},{3,4},{4,3},{5,6},{6,5},{7,8},{8,7},{9,10},{10,9},{11,... | collective-permute-start | bytes 786440 | tf_op jit(solution)/shard_map/ppermute | solution.py:282
  10.2 0.9 copy.8
  11.1 0.0 copy-done
  11.2 0.0 copy-start.5
  11.2 0.0 copy-start.6
  11.2 0.1 constant_dynamic-slice_fusion
  11.3 0.1 broadcast_in_dim.7
  11.3 0.0 copy-done.1
  11.3 0.5 copy-done.5
  11.8 0.0 copy-done.6
  11.9 0.3 shard_map.65.after.meta
  12.2 0.1 add_convert_fusion.place
  12.3 0.0 collective-permute-done.side_a
  12.3 3.7 %collective-permute-done.1.side_b = f32[512,128]{1,0:T(8,128)S(1)} collective-permute-done((f32[512,128]{1,0:T(8,128)S(1)}, f32[512,128]{1,0:T(8,128)S(1)}, u32[]{:S(2)}, u32[]{:S(2)}) %collective-permute-start.1) | collective-permute-done | bytes 262176 | tf_op jit(solution)/shard_map/ppermute | solution.py:282
  16.0 1.2 %shard_map.66 = (f32[16,4,8,128]{3,2,1,0:T(8,128)S(1)}, f32[16,4,8,128]{3,2,1,0:T(8,128)S(1)}) custom-call(s32[4]{0:T(128)S(1)} %add_convert_fusion.place, f32[16,128]{1,0:T(8,128)S(1)} %shard_map.65.after.meta, f32[512,128]{1,0:T(8,128)S(1)} %shard_map.64.after.mixed, f32[512,128]{1,0:T(8,128)S(1)} %collective-permute-done.side_a, ...), custom_call_target="tpu_custom_call" | custom-call | flops 1000000 | bytes 1000000 | tf_op jit(solution)/shard_map/pallas_call | solution.py:291
  17.2 4.0 %all-gather = f32[32,4,8,128]{3,2,1,0:T(8,128)S(1)} all-gather(f32[16,4,8,128]{3,2,1,0:T(8,128)S(1)} %get-tuple-element.13), channel_id=2, replica_groups={{0,16},{32,48},{64,80},{96,112},{128,144},{160,176},{192,208},{224,240}..., dimensions={0}, use_global_device_ids=true | all-gather | bytes 786432 | tf_op jit(solution)/shard_map/all_gather | solution.py:297
  21.2 0.6 shard_map.67
  21.7 0.1 broadcast_in_dim.8.weights
  21.8 20.8 %all_to_all.10.arrived = f32[16,4,8,128]{3,2,1,0:T(8,128)S(1)} all-to-all(f32[16,4,8,128]{3,2,1,0:T(8,128)S(1)} %shard_map.67), channel_id=1, replica_groups={{0,32,64,96,128,160,192,224,256,288,320,352,384,416,448,480},{16,48,80,..., dimensions={0} | all-to-all | bytes 524288 | tf_op jit(solution)/shard_map/all_to_all | solution.py:303
  42.6 6.1 %collective-permute-start.2 = (f32[48,128]{1,0:T(8,128)S(1)}, f32[48,128]{1,0:T(8,128)S(1)}, u32[]{:S(2)}, u32[]{:S(2)}) collective-permute-start(f32[48,128]{1,0:T(8,128)S(1)} %shard_map.68.share), channel_id=1, source_target_pairs={{1,2},{2,1},{3,4},{4,3},{5,6},{6,5},{7,8},{8,7},{9,10},{10,9},{11,... | collective-permute-start | bytes 73736 | tf_op jit(solution)/shard_map/ppermute | solution.py:308
  48.7 3.6 %all-gather.1 = f32[96,128]{1,0:T(8,128)S(1)} all-gather(f32[48,128]{1,0:T(8,128)S(1)} %shard_map.68.share), channel_id=3, replica_groups={{0,1},{2,3},{4,5},{6,7},{8,9},{10,11},{12,13},{14,15},{16,17},{18,19},{..., dimensions={0}, use_global_device_ids=true | all-gather | bytes 73728 | tf_op jit(solution)/shard_map/all_gather | solution.py:309
  52.3 0.0 collective-permute-done.2.swap_b
  52.3 0.9 %shard_map.69 = f32[16,4,8,128]{3,2,1,0:T(8,128)S(1)} custom-call(s32[4]{0:T(128)S(1)} %add_convert_fusion.place, f32[48,128]{1,0:T(8,128)S(1)} %shard_map.68.share, f32[48,128]{1,0:T(8,128)S(1)} %collective-permute-done.2.swap_b, f32[2,48,128]{2,1,0:T(8,128)S(1)} %bitcast.18, f32[16,128]{1,0:T(8,128)S(1)} %broadcast_in_dim.8.weights), custom_call_target="tpu_custom_call" | custom-call | flops 1000000 | bytes 1000000 | tf_op jit(solution)/shard_map/pallas_call | solution.py:310
  53.2 14.1 %all_to_all.11 = f32[16,4,8,128]{3,2,1,0:T(8,128)S(1)} all-to-all(f32[16,4,8,128]{3,2,1,0:T(8,128)S(1)} %shard_map.69), channel_id=1, replica_groups={{0,32,64,96,128,160,192,224,256,288,320,352,384,416,448,480},{16,48,80,..., dimensions={0} | all-to-all | bytes 524288 | tf_op jit(solution)/shard_map/all_to_all | solution.py:316
  67.3 6.0 %all-gather.2 = f32[32,4,8,128]{3,2,1,0:T(8,128)S(1)} all-gather(f32[16,4,8,128]{3,2,1,0:T(8,128)S(1)} %all_to_all.11), channel_id=4, replica_groups={{0,16},{32,48},{64,80},{96,112},{128,144},{160,176},{192,208},{224,240}..., dimensions={0}, use_global_device_ids=true | all-gather | bytes 786432 | tf_op jit(solution)/shard_map/all_gather | solution.py:317
  73.3 0.0 copy-start.3
  73.3 0.1 shard_map.70.projected
  73.4 1.9 %collective-permute-start.3 = (f32[512,128]{1,0:T(8,128)S(1)}, f32[512,128]{1,0:T(8,128)S(1)}, u32[]{:S(2)}, u32[]{:S(2)}) collective-permute-start(f32[512,128]{1,0:T(8,128)S(1)} %shard_map.70.projected), channel_id=1, source_target_pairs={{0,1},{1,0},{2,3},{3,2},{4,5},{5,4},{6,7},{7,6},{8,9},{9,8},{10,11... | collective-permute-start | bytes 786440 | tf_op jit(solution)/shard_map/ppermute | solution.py:325
  75.4 4.3 %collective-permute-start.4 = (f32[512,128]{1,0:T(8,128)S(1)}, f32[512,128]{1,0:T(8,128)S(1)}, u32[]{:S(2)}, u32[]{:S(2)}) collective-permute-start(f32[512,128]{1,0:T(8,128)S(1)} %shard_map.70.projected), channel_id=1, source_target_pairs={{1,2},{2,1},{3,4},{4,3},{5,6},{6,5},{7,8},{8,7},{9,10},{10,9},{11,... | collective-permute-start | bytes 786440 | tf_op jit(solution)/shard_map/ppermute | solution.py:324
  79.6 8.8 %collective-permute-done.3.side_a = f32[512,128]{1,0:T(8,128)S(1)} collective-permute-done((f32[512,128]{1,0:T(8,128)S(1)}, f32[512,128]{1,0:T(8,128)S(1)}, u32[]{:S(2)}, u32[]{:S(2)}) %collective-permute-start.3) | collective-permute-done | bytes 262176 | tf_op jit(solution)/shard_map/ppermute | solution.py:325
  88.4 0.0 collective-permute-done.4.side_b
  88.4 0.0 copy-done.3
  88.4 1.9 %shard_map.71 = f32[2,256,128]{2,1,0:T(8,128)} custom-call(s32[4]{0:T(128)S(1)} %add_convert_fusion.place, f32[512,128]{1,0:T(8,128)S(1)} %shard_map.70.projected, f32[512,128]{1,0:T(8,128)S(1)} %collective-permute-done.3.side_a, f32[512,128]{1,0:T(8,128)S(1)} %collective-permute-done.4.side_b, bf16[2,256,128]{2,1,0:T(8,128)(2,1)S(1)} %bitcast.17, ...), custom_call_target="tpu_custom_call" | custom-call | flops 1000000 | bytes 1000000 | tf_op jit(solution)/shard_map/pallas_call | solution.py:327
  (1 shorter events, 0.0 us)
Async XLA Ops:
  0.0 11.1 %copy-start = (f32[4,128]{1,0:T(4,128)S(1)}, f32[4,128]{1,0:T(4,128)}, u32[]{:S(2)}) copy-start(f32[4,128]{1,0:T(4,128)} %param.9) | copy-start | bytes 6148
  0.0 11.3 %copy-start.1 = (bf16[2,4,128,2,128]{4,3,2,1,0:T(2,128)(2,1)S(1)}, bf16[2,4,128,2,128]{4,3,2,1,0:T(2,128)(2,1)}, u32[]{:S(2)}) copy-start(bf16[2,4,128,2,128]{4,3,2,1,0:T(2,128)(2,1)} %param.6) | copy-start | bytes 1572868
  0.0 1.0 %copy-start.2 = (bf16[2,128,2,128]{3,2,1,0:T(2,128)(2,1)S(1)}, bf16[2,128,2,128]{3,2,1,0:T(2,128)(2,1)}, u32[]{:S(2)}) copy-start(bf16[2,128,2,128]{3,2,1,0:T(2,128)(2,1)} %param.7) | copy-start | bytes 393220
  1.0 0.8 copy-start.4
  1.9 10.4 %collective-permute-start = (f32[512,128]{1,0:T(8,128)S(1)}, f32[512,128]{1,0:T(8,128)S(1)}, u32[]{:S(2)}, u32[]{:S(2)}) collective-permute-start(f32[512,128]{1,0:T(8,128)S(1)} %shard_map.64.after.mixed), channel_id=1, source_target_pairs={{0,1},{1,0},{2,3},{3,2},{4,5},{5,4},{6,7},{7,6},{8,9},{9,8},{10,11... | collective-permute-start | bytes 786440 | tf_op jit(solution)/shard_map/ppermute | solution.py:283
  4.1 11.9 %collective-permute-start.1 = (f32[512,128]{1,0:T(8,128)S(1)}, f32[512,128]{1,0:T(8,128)S(1)}, u32[]{:S(2)}, u32[]{:S(2)}) collective-permute-start(f32[512,128]{1,0:T(8,128)S(1)} %shard_map.64.after.mixed), channel_id=1, source_target_pairs={{1,2},{2,1},{3,4},{4,3},{5,6},{6,5},{7,8},{8,7},{9,10},{10,9},{11,... | collective-permute-start | bytes 786440 | tf_op jit(solution)/shard_map/ppermute | solution.py:282
  11.2 0.7 copy-start.5
  11.2 0.7 copy-start.6
  42.6 9.7 %collective-permute-start.2 = (f32[48,128]{1,0:T(8,128)S(1)}, f32[48,128]{1,0:T(8,128)S(1)}, u32[]{:S(2)}, u32[]{:S(2)}) collective-permute-start(f32[48,128]{1,0:T(8,128)S(1)} %shard_map.68.share), channel_id=1, source_target_pairs={{1,2},{2,1},{3,4},{4,3},{5,6},{6,5},{7,8},{8,7},{9,10},{10,9},{11,... | collective-permute-start | bytes 73736 | tf_op jit(solution)/shard_map/ppermute | solution.py:308
  73.3 15.1 %copy-start.3 = (bf16[2,128,2,128]{3,2,1,0:T(2,128)(2,1)S(1)}, bf16[2,128,2,128]{3,2,1,0:T(2,128)(2,1)}, u32[]{:S(2)}) copy-start(bf16[2,128,2,128]{3,2,1,0:T(2,128)(2,1)} %param.7) | copy-start | bytes 393220
  73.4 15.0 %collective-permute-start.3 = (f32[512,128]{1,0:T(8,128)S(1)}, f32[512,128]{1,0:T(8,128)S(1)}, u32[]{:S(2)}, u32[]{:S(2)}) collective-permute-start(f32[512,128]{1,0:T(8,128)S(1)} %shard_map.70.projected), channel_id=1, source_target_pairs={{0,1},{1,0},{2,3},{3,2},{4,5},{5,4},{6,7},{7,6},{8,9},{9,8},{10,11... | collective-permute-start | bytes 786440 | tf_op jit(solution)/shard_map/ppermute | solution.py:325
  75.4 13.1 %collective-permute-start.4 = (f32[512,128]{1,0:T(8,128)S(1)}, f32[512,128]{1,0:T(8,128)S(1)}, u32[]{:S(2)}, u32[]{:S(2)}) collective-permute-start(f32[512,128]{1,0:T(8,128)S(1)} %shard_map.70.projected), channel_id=1, source_target_pairs={{1,2},{2,1},{3,4},{4,3},{5,6},{6,5},{7,8},{8,7},{9,10},{10,9},{11,... | collective-permute-start | bytes 786440 | tf_op jit(solution)/shard_map/ppermute | solution.py:324

commit v3 on v2

--- a/solution.py
+++ b/solution.py
@@ -54,6 +54,21 @@
     f_1 = smooth(own[1], own[0], below[0])
     f_down = bottom * smooth(below[0], own[1], below[1])
     return smooth(f_0, f_up, f_1), smooth(f_1, f_0, f_down)
+
+
+def own_part(own, top, bottom):
+    zero = jnp.zeros_like(own[0])
+    return smooth_twice((zero, zero), own, (zero, zero), top, bottom)
+
+
+def halo_part(above, below, top, bottom):
+    up = from_right(above[1]) + from_left(above[1])
+    down = from_right(below[0]) + from_left(below[0])
+    f_up = top * (above[1] + diffusion * (above[0] + up - 4.0 * above[1]))
+    f_down = bottom * (below[0] + diffusion * (below[1] + down - 4.0 * below[0]))
+    first = above[1] + diffusion * (up - 4.0 * above[1]) + f_up + diffusion * below[0]
+    second = below[0] + diffusion * (down - 4.0 * below[0]) + f_down + diffusion * above[1]
+    return diffusion * first, diffusion * second
 
 
 def rows_of(ref, start, count):
@@ -91,16 +106,40 @@
             )
 
 
-def partial_kernel(factor, place, after, mixed, side_a, side_b, ensemble, keep, send, local):
+def own_kernel(place, field, out):
+    members, _, levels = out.shape[:3]
+    top, bottom = place[1].astype(f32), place[2].astype(f32)
+    for k in range(members):
+        both = own_part(rows_of(field, 2 * k * levels, levels), top, bottom)
+        for r in range(2):
+            out[k, r] = both[r]
+
+
+def own_control_kernel(place, field, control, vertical, out, wide, turned, spare):
+    own_kernel(place, field, out)
+    turned[...] = vertical[...].astype(f32).T.astype(turned.dtype)
+    members, _, levels = out.shape[:3]
+    for k in range(members):
+        spare[...] = control[k].astype(f32)
+        for r in range(2):
+            wide[k, r] = spare[pl.ds(r, levels, stride=2), :]
+
+
+def smoothed_rows(place, k, own, side_a, side_b):
+    even, top, bottom = (place[i] for i in range(3))
+    levels = own.shape[2]
+    at = 2 * k * levels
+    above, below = neighbours(even, rows_of(side_a, at, levels), rows_of(side_b, at, levels))
+    both = halo_part(above, below, top.astype(f32), bottom.astype(f32))
+    return [own[k, r] + both[r] for r in range(2)]
+
+
+def partial_kernel(factor, place, after, own, side_a, side_b, ensemble, keep, send, local):
     members, variables, height = ensemble.shape[:3]
     levels = height // 2
-    even, top, bottom, first_core = (place[i] for i in range(4))
-    for k in range(members):
-        at = k * height
-        above, below = neighbours(even, rows_of(side_a, at, levels), rows_of(side_b, at, levels))
-        both = smooth_twice(
-            above, rows_of(mixed, at, levels), below, top.astype(f32), bottom.astype(f32)
-        )
+    first_core = place[3]
+    for k in range(members):
+        both = smoothed_rows(place, k, own, side_a, side_b)
         for r in range(2):
             local[k, pl.ds(r, levels, stride=2), :] = both[r]
     mine = first_core != 0
@@ -132,7 +171,7 @@
     out[rows:, :] = meta[...]
 
 
-def observe_kernel(place, share, swap_b, pair_a, weights, out, rows):
+def observe_kernel(place, inverse_var, share, swap_b, pair_a, out, rows):
     even, top, bottom = (place[i] for i in range(3))
     height = rows.shape[0]
     n = height // 2
@@ -171,7 +210,14 @@
         at = (2 * which + phase) * 4 + line
         return table[block][at : at + 1, :]
 
-    scale = weights[...]
+    variables = out.shape[1]
+    per_owner = n // variables
+    line = lax.broadcasted_iota(jnp.int32, own[0].shape, 0)
+    scale = jnp.zeros(own[0].shape, f32)
+    for v in range(variables):
+        for l in range(per_owner):
+            value = inverse_var[v, place[4] + l]
+            scale = jnp.where(line == v * per_owner + l, value, scale)
     forcing, first, second, third, fourth = {}, {}, {}, {}, {}
     for f in range(-2, 6):
         e, o = fine[f]
@@ -205,7 +251,6 @@
         )
         result = near_weight * (e + o) + far_weight * (from_left(o) + from_right(e))
         rows[pl.ds(a_row, n, stride=2), :] = result
-    variables = out.shape[1]
     for v in range(variables):
         tile = rows[8 * v : 8 * v + 8, :]
         for j in range(out.shape[0]):
@@ -225,22 +270,16 @@
             out[pl.ds(k * height + 16 * j, 16), :] = factor * total
 
 
-def product_kernel(place, projected, side_a, side_b, control, transposed, far, out, wide, sems):
-    members, height = control.shape[:2]
-    levels = height // 2
-    even, top, bottom = (place[i] for i in range(3))
-    for k in range(members):
-        at = k * height
-        above, below = neighbours(even, rows_of(side_a, at, levels), rows_of(side_b, at, levels))
-        both = smooth_twice(
-            above, rows_of(projected, at, levels), below, top.astype(f32), bottom.astype(f32)
-        )
-        wide[...] = control[k].astype(f32)
-        for r in range(2):
-            back = jnp.dot(
-                transposed[...], both[r].astype(jnp.bfloat16), preferred_element_type=f32
+def product_kernel(place, own, side_a, side_b, control, transposed, far, out, sems):
+    members, _, levels, width = control.shape
+    for k in range(members):
+        both = smoothed_rows(place, k, own, side_a, side_b)
+        rounded = jnp.concatenate([row.astype(jnp.bfloat16) for row in both], axis=1)
+        back = jnp.dot(transposed[...], rounded, preferred_element_type=f32)
+        for r in range(2):
+            out[k, pl.ds(r, levels, stride=2), :] = (
+                control[k, r] + back[:, r * width : (r + 1) * width]
             )
-            out[k, pl.ds(r, levels, stride=2), :] = wide[pl.ds(r, levels, stride=2), :] + back
         pltpu.make_async_copy(out.at[k], far.at[k], sems.at[k]).start()
     for k in range(members):
         pltpu.make_async_copy(out.at[k], far.at[k], sems.at[k]).wait()
@@ -261,6 +300,7 @@
             (grid_at > 0).astype(jnp.int32),
             (grid_at < grid_size - 1).astype(jnp.int32),
             (mem_at % 2 == 0).astype(jnp.int32),
+            (mem_at * per_owner).astype(jnp.int32),
         ]
     )
     swap_a = [(i, i ^ 1) for i in range(grid_size)]
@@ -279,13 +319,13 @@
         [VMEM, VMEM],
         [pltpu.VMEM((height, width), f32)],
     )(ctl, vertical)
+    mixed_a = lax.ppermute(mixed, "grid", swap_a)
     mixed_b = lax.ppermute(mixed, "grid", swap_b)
-    mixed_a = lax.ppermute(mixed, "grid", swap_a)
     meta = call(
         meta_kernel, jax.ShapeDtypeStruct((meta_rows, width), f32), [ANY, VMEM, VMEM, VMEM]
     )(mixed, obs_code, obs_count, ens)
-    weights = lax.dynamic_slice_in_dim(inverse_var, mem_at * per_owner, per_owner, 1)
-    weights = jnp.broadcast_to(weights.reshape(-1, 1), (variables * per_owner, width))
+    own_shape = jax.ShapeDtypeStruct((members, own_rows, levels, width), f32)
+    own = call(own_kernel, own_shape, [SMEM, VMEM])(place, mixed)
 
     block = jax.ShapeDtypeStruct((half, variables, 8, width), f32)
     keep, send = call(
@@ -293,13 +333,10 @@
         (block, block),
         [SMEM, ANY] + [VMEM] * 4,
         [pltpu.VMEM((members, height, width), f32)],
-    )(place, meta, mixed, mixed_a, mixed_b, ens)
+    )(place, meta, own, mixed_a, mixed_b, ens)
     gathered = lax.all_gather(send, "mem", axis=0, axis_index_groups=cores)
     paired = call(pair_sum_kernel, block, [SMEM, VMEM, VMEM])(place, keep, gathered)
-    turned = vertical.T
-    paired, meta, weights, place, turned = lax.optimization_barrier(
-        (paired, meta, weights, place, turned)
-    )
+    paired, meta, place = lax.optimization_barrier((paired, meta, place))
     arrived = lax.all_to_all(paired, "mem", 0, 0, axis_index_groups=same_core, tiled=True)
     share = call(
         total_kernel, jax.ShapeDtypeStruct((variables * 8 + meta_rows, width), f32), [VMEM, VMEM]
@@ -310,9 +347,9 @@
     spread = call(
         observe_kernel,
         block,
-        [SMEM] + [VMEM] * 4,
+        [SMEM, SMEM] + [VMEM] * 3,
         [pltpu.VMEM((variables * 8, width), f32)],
-    )(place, share, share_b, share_a, weights)
+    )(place, inverse_var, share, share_b, share_a)
     mine = lax.all_to_all(spread, "mem", 0, 0, axis_index_groups=same_core, tiled=True)
     adjoint = lax.all_gather(mine, "mem", axis=0, axis_index_groups=cores)
 
@@ -321,20 +358,22 @@
         jax.ShapeDtypeStruct((members * height, width), f32),
         [VMEM, VMEM],
     )(adjoint, ens)
+    projected_a = lax.ppermute(projected, "grid", swap_a)
     projected_b = lax.ppermute(projected, "grid", swap_b)
-    projected_a = lax.ppermute(projected, "grid", swap_a)
+    own, wide, turned = call(
+        own_control_kernel,
+        (own_shape, own_shape, jax.ShapeDtypeStruct(vertical.shape, vertical.dtype)),
+        [SMEM, VMEM, VMEM, VMEM],
+        [pltpu.VMEM((height, width), f32)],
+    )(place, projected, ctl, vertical)
     whole = jax.ShapeDtypeStruct((members, height, width), f32)
     out = call(
         product_kernel,
         whole,
         [SMEM] + [VMEM] * 5,
-        [
-            pltpu.VMEM(whole.shape, f32),
-            pltpu.VMEM((height, width), f32),
-            pltpu.SemaphoreType.DMA((members,)),
-        ],
+        [pltpu.VMEM(whole.shape, f32), pltpu.SemaphoreType.DMA((members,))],
         out_spec=ANY,
-    )(place, projected, projected_a, projected_b, ctl, turned)
+    )(place, own, projected_a, projected_b, wide, turned)
     return out.reshape(control.shape)
 
 

time: 91.4 us -> 95.2 us (1.042)
  waiting for transfers between devices: 12.5 us -> 21.2 us
  starting transfers between devices: 20.6 us -> 18.1 us
  blocking collectives: 48.4 us -> 46.8 us
  local copies, waits for them, and re-layouts: 3.35 us -> 1.83 us
  Pallas kernels: 5.22 us -> 6.68 us
    ppermute x1, waiting for transfers between devices: 0.01 us -> 6.65 us  [per_device(): mixed_a = lax.ppermute(mixed, 'grid', swap_a)]
    ppermute x1, waiting for transfers between devices: 0.01 us -> 5.6 us  [per_device(): projected_b = lax.ppermute(projected, 'grid', swap_b)]
    ppermute x1, waiting for transfers between devices: 8.8 us -> 6.31 us  [per_device(): projected_a = lax.ppermute(projected, 'grid', swap_a)]
    pallas_call x1 -> x3, Pallas kernels: 0.91 us -> 2.86 us  [the longest x1 0.99 us: per_device(): call(own_control_kernel, (own_shape, own_shape, jax.ShapeDtypeStruct(vert...]
    all_gather x1, blocking collectives: 3.97 us -> 2.3 us  [per_device(): gathered = lax.all_gather(send, 'mem', axis=0, axis_index_groups=cores)]
    unnamed x15 -> x16, local copies, waits for them, and re-layouts: 3.12 us -> 1.74 us
    ppermute x1, starting transfers between devices: 4.27 us -> 3 us  [per_device(): projected_b = lax.ppermute(projected, 'grid', swap_b)]
    ppermute x1, waiting for transfers between devices: 3.7 us -> 2.65 us  [per_device(): mixed_b = lax.ppermute(mixed, 'grid', swap_b)]
  transfers between devices with their start and end apart: 5 -> 5, of which waited for: 2 -> 4; matrix products, arithmetic and copies ran while one was open for 1% -> 0% of each run, Pallas kernels for 0% -> 2%
where the time goes in v3:
time: 95.2 us; the launch traced here: 94.8 us
  blocking collectives  46.8 us (49%)
  waiting for transfers between devices  21.2 us (22%)
  starting transfers between devices  18.1 us (19%)
  Pallas kernels  6.68 us (7%)
  local copies, waits for them, and re-layouts  1.83 us (2%)
    all_to_all x1, blocking collectives, per_device(): lax.all_to_all(paired, 'mem', 0, 0, axis_index_groups=same_core, tiled=True)  20.8 us
    all_to_all x1, blocking collectives, per_device(): lax.all_to_all(spread, 'mem', 0, 0, axis_index_groups=same_core, tiled=True)  14.1 us
    ppermute x1, waiting for transfers between devices, per_device(): mixed_a = lax.ppermute(mixed, 'grid', swap_a)  6.65 us
    ppermute x1, waiting for transfers between devices, per_device(): projected_a = lax.ppermute(projected, 'grid', swap_a)  6.31 us
    ppermute x1, starting transfers between devices, per_device(): share_b = lax.ppermute(share, 'grid', swap_b)  6.08 us
    all_gather x1, blocking collectives, per_device(): adjoint = lax.all_gather(mine, 'mem', axis=0, axis_index_groups=cores)  5.99 us
    ppermute x1, waiting for transfers between devices, per_device(): projected_b = lax.ppermute(projected, 'grid', swap_b)  5.6 us
    ppermute x1, starting transfers between devices, per_device(): mixed_b = lax.ppermute(mixed, 'grid', swap_b)  5.18 us
  transfers between devices with their start and end apart: 5, of which 4 were waited for; matrix products, arithmetic and copies ran while one was open for 0% of the time, Pallas kernels for 2%

profile of v3, /device:TPU:195, one launch (start us, length us, event | category | flops | bytes accessed | tf_op | source)
XLA Modules:
  0.0 94.8 jit_solution(509008062861777394)
XLA Ops:
  0.0 0.0 copy-start
  0.0 0.0 copy-start.1
  0.0 1.0 %copy-done.1 = bf16[2,128,2,128]{3,2,1,0:T(2,128)(2,1)S(1)} copy-done((bf16[2,128,2,128]{3,2,1,0:T(2,128)(2,1)S(1)}, bf16[2,128,2,128]{3,2,1,0:T(2,128)(2,1)}, u32[]{:S(2)}) %copy-start.1) | copy-done | bytes 131096
  1.0 0.0 copy-start.3
  1.0 0.8 copy-done.3
  1.7 0.2 shard_map.64.after.field
  1.9 5.2 %collective-permute-start.1 = (f32[512,128]{1,0:T(8,128)S(1)}, f32[512,128]{1,0:T(8,128)S(1)}, u32[]{:S(2)}, u32[]{:S(2)}) collective-permute-start(f32[512,128]{1,0:T(8,128)S(1)} %shard_map.64.after.field), channel_id=1, source_target_pairs={{1,2},{2,1},{3,4},{4,3},{5,6},{6,5},{7,8},{8,7},{9,10},{10,9},{11,... | collective-permute-start | bytes 786440 | tf_op jit(solution)/shard_map/ppermute | solution.py:323
  7.1 1.9 %collective-permute-start = (f32[512,128]{1,0:T(8,128)S(1)}, f32[512,128]{1,0:T(8,128)S(1)}, u32[]{:S(2)}, u32[]{:S(2)}) collective-permute-start(f32[512,128]{1,0:T(8,128)S(1)} %shard_map.64.after.field), channel_id=1, source_target_pairs={{0,1},{1,0},{2,3},{3,2},{4,5},{5,4},{6,7},{7,6},{8,9},{9,8},{10,11... | collective-permute-start | bytes 786440 | tf_op jit(solution)/shard_map/ppermute | solution.py:322
  9.1 0.1 stack.39.place
  9.1 0.0 copy-start.5
  9.1 0.0 copy-start.6
  9.1 0.9 shard_map.66.own
  10.1 0.0 copy-done
  10.1 0.0 copy-done.5
  10.1 0.0 copy-done.6
  10.1 0.3 shard_map.65.after.meta
  10.5 2.7 %collective-permute-done.1.side_b = f32[512,128]{1,0:T(8,128)S(1)} collective-permute-done((f32[512,128]{1,0:T(8,128)S(1)}, f32[512,128]{1,0:T(8,128)S(1)}, u32[]{:S(2)}, u32[]{:S(2)}) %collective-permute-start.1) | collective-permute-done | bytes 262176 | tf_op jit(solution)/shard_map/ppermute | solution.py:323
  13.1 6.7 %collective-permute-done.side_a = f32[512,128]{1,0:T(8,128)S(1)} collective-permute-done((f32[512,128]{1,0:T(8,128)S(1)}, f32[512,128]{1,0:T(8,128)S(1)}, u32[]{:S(2)}, u32[]{:S(2)}) %collective-permute-start) | collective-permute-done | bytes 262176 | tf_op jit(solution)/shard_map/ppermute | solution.py:322
  19.8 0.9 shard_map.67
  20.7 2.3 %all-gather = f32[32,4,8,128]{3,2,1,0:T(8,128)S(1)} all-gather(f32[16,4,8,128]{3,2,1,0:T(8,128)S(1)} %get-tuple-element.14), channel_id=2, replica_groups={{0,16},{32,48},{64,80},{96,112},{128,144},{160,176},{192,208},{224,240}..., dimensions={0}, use_global_device_ids=true | all-gather | bytes 786432 | tf_op jit(solution)/shard_map/all_gather | solution.py:337
  23.0 0.6 shard_map.68
  23.6 20.8 %all_to_all.10.arrived = f32[16,4,8,128]{3,2,1,0:T(8,128)S(1)} all-to-all(f32[16,4,8,128]{3,2,1,0:T(8,128)S(1)} %shard_map.68), channel_id=1, replica_groups={{0,32,64,96,128,160,192,224,256,288,320,352,384,416,448,480},{16,48,80,..., dimensions={0} | all-to-all | bytes 524288 | tf_op jit(solution)/shard_map/all_to_all | solution.py:340
  44.4 6.1 %collective-permute-start.2 = (f32[48,128]{1,0:T(8,128)S(1)}, f32[48,128]{1,0:T(8,128)S(1)}, u32[]{:S(2)}, u32[]{:S(2)}) collective-permute-start(f32[48,128]{1,0:T(8,128)S(1)} %shard_map.69.share), channel_id=1, source_target_pairs={{1,2},{2,1},{3,4},{4,3},{5,6},{6,5},{7,8},{8,7},{9,10},{10,9},{11,... | collective-permute-start | bytes 73736 | tf_op jit(solution)/shard_map/ppermute | solution.py:345
  50.5 0.0 copy-start.7
  50.5 3.6 %all-gather.1 = f32[96,128]{1,0:T(8,128)S(1)} all-gather(f32[48,128]{1,0:T(8,128)S(1)} %shard_map.69.share), channel_id=3, replica_groups={{0,1},{2,3},{4,5},{6,7},{8,9},{10,11},{12,13},{14,15},{16,17},{18,19},{..., dimensions={0}, use_global_device_ids=true | all-gather | bytes 73728 | tf_op jit(solution)/shard_map/all_gather | solution.py:346
  54.1 0.0 collective-permute-done.2.swap_b
  54.1 0.0 copy-done.7
  54.1 0.9 shard_map.70
  55.1 14.1 %all_to_all.11 = f32[16,4,8,128]{3,2,1,0:T(8,128)S(1)} all-to-all(f32[16,4,8,128]{3,2,1,0:T(8,128)S(1)} %shard_map.70), channel_id=1, replica_groups={{0,32,64,96,128,160,192,224,256,288,320,352,384,416,448,480},{16,48,80,..., dimensions={0} | all-to-all | bytes 524288 | tf_op jit(solution)/shard_map/all_to_all | solution.py:353
  69.2 6.0 %all-gather.2 = f32[32,4,8,128]{3,2,1,0:T(8,128)S(1)} all-gather(f32[16,4,8,128]{3,2,1,0:T(8,128)S(1)} %all_to_all.11), channel_id=4, replica_groups={{0,16},{32,48},{64,80},{96,112},{128,144},{160,176},{192,208},{224,240}..., dimensions={0}, use_global_device_ids=true | all-gather | bytes 786432 | tf_op jit(solution)/shard_map/all_gather | solution.py:354
  75.2 0.0 copy-start.2
  75.2 0.0 copy-start.4
  75.2 0.1 shard_map.71.field
  75.3 3.0 %collective-permute-start.4 = (f32[512,128]{1,0:T(8,128)S(1)}, f32[512,128]{1,0:T(8,128)S(1)}, u32[]{:S(2)}, u32[]{:S(2)}) collective-permute-start(f32[512,128]{1,0:T(8,128)S(1)} %shard_map.71.field), channel_id=1, source_target_pairs={{1,2},{2,1},{3,4},{4,3},{5,6},{6,5},{7,8},{8,7},{9,10},{10,9},{11,... | collective-permute-start | bytes 786440 | tf_op jit(solution)/shard_map/ppermute | solution.py:362
  78.3 1.9 %collective-permute-start.3 = (f32[512,128]{1,0:T(8,128)S(1)}, f32[512,128]{1,0:T(8,128)S(1)}, u32[]{:S(2)}, u32[]{:S(2)}) collective-permute-start(f32[512,128]{1,0:T(8,128)S(1)} %shard_map.71.field), channel_id=1, source_target_pairs={{0,1},{1,0},{2,3},{3,2},{4,5},{5,4},{6,7},{7,6},{8,9},{9,8},{10,11... | collective-permute-start | bytes 786440 | tf_op jit(solution)/shard_map/ppermute | solution.py:361
  80.2 0.0 copy-done.2
  80.2 0.0 copy-done.4
  80.2 1.0 %shard_map.72 = (f32[2,2,128,128]{3,2,1,0:T(8,128)S(1)}, f32[2,2,128,128]{3,2,1,0:T(8,128)S(1)}, bf16[128,128]{1,0:T(8,128)(2,1)S(1)}) custom-call(s32[5]{0:T(128)S(1)} %stack.39.place, f32[512,128]{1,0:T(8,128)S(1)} %shard_map.71.field, bf16[2,256,128]{2,1,0:T(8,128)(2,1)S(1)} %bitcast.17, bf16[128,128]{1,0:T(8,128)(2,1)S(1)} %copy-done.4), custom_call_target="tpu_custom_call" | custom-call | flops 1000000 | bytes 1000000 | tf_op jit(solution)/shard_map/pallas_call | solution.py:363
  81.2 5.6 %collective-permute-done.4.side_b = f32[512,128]{1,0:T(8,128)S(1)} collective-permute-done((f32[512,128]{1,0:T(8,128)S(1)}, f32[512,128]{1,0:T(8,128)S(1)}, u32[]{:S(2)}, u32[]{:S(2)}) %collective-permute-start.4) | collective-permute-done | bytes 262176 | tf_op jit(solution)/shard_map/ppermute | solution.py:362
  86.8 6.3 %collective-permute-done.3.side_a = f32[512,128]{1,0:T(8,128)S(1)} collective-permute-done((f32[512,128]{1,0:T(8,128)S(1)}, f32[512,128]{1,0:T(8,128)S(1)}, u32[]{:S(2)}, u32[]{:S(2)}) %collective-permute-start.3) | collective-permute-done | bytes 262176 | tf_op jit(solution)/shard_map/ppermute | solution.py:361
  93.1 1.7 %shard_map.73 = f32[2,256,128]{2,1,0:T(8,128)} custom-call(s32[5]{0:T(128)S(1)} %stack.39.place, f32[2,2,128,128]{3,2,1,0:T(8,128)S(1)} %get-tuple-element.18.own, f32[512,128]{1,0:T(8,128)S(1)} %collective-permute-done.3.side_a, f32[512,128]{1,0:T(8,128)S(1)} %collective-permute-done.4.side_b, f32[2,2,128,128]{3,2,1,0:T(8,128)S(1)} %get-tuple-element.19.control, ...), custom_call_target="tpu_custom_call" | custom-call | flops 1000000 | bytes 1000000 | tf_op jit(solution)/shard_map/pallas_call | solution.py:370
  (1 shorter events, 0.0 us)
Async XLA Ops:
  0.0 10.1 %copy-start = (bf16[2,4,128,2,128]{4,3,2,1,0:T(2,128)(2,1)S(1)}, bf16[2,4,128,2,128]{4,3,2,1,0:T(2,128)(2,1)}, u32[]{:S(2)}) copy-start(bf16[2,4,128,2,128]{4,3,2,1,0:T(2,128)(2,1)} %param.6) | copy-start | bytes 1572868
  0.0 1.0 %copy-start.1 = (bf16[2,128,2,128]{3,2,1,0:T(2,128)(2,1)S(1)}, bf16[2,128,2,128]{3,2,1,0:T(2,128)(2,1)}, u32[]{:S(2)}) copy-start(bf16[2,128,2,128]{3,2,1,0:T(2,128)(2,1)} %param.7) | copy-start | bytes 393220
  1.0 0.8 copy-start.3
  1.9 11.2 %collective-permute-start.1 = (f32[512,128]{1,0:T(8,128)S(1)}, f32[512,128]{1,0:T(8,128)S(1)}, u32[]{:S(2)}, u32[]{:S(2)}) collective-permute-start(f32[512,128]{1,0:T(8,128)S(1)} %shard_map.64.after.field), channel_id=1, source_target_pairs={{1,2},{2,1},{3,4},{4,3},{5,6},{6,5},{7,8},{8,7},{9,10},{10,9},{11,... | collective-permute-start | bytes 786440 | tf_op jit(solution)/shard_map/ppermute | solution.py:323
  7.1 12.7 %collective-permute-start = (f32[512,128]{1,0:T(8,128)S(1)}, f32[512,128]{1,0:T(8,128)S(1)}, u32[]{:S(2)}, u32[]{:S(2)}) collective-permute-start(f32[512,128]{1,0:T(8,128)S(1)} %shard_map.64.after.field), channel_id=1, source_target_pairs={{0,1},{1,0},{2,3},{3,2},{4,5},{5,4},{6,7},{7,6},{8,9},{9,8},{10,11... | collective-permute-start | bytes 786440 | tf_op jit(solution)/shard_map/ppermute | solution.py:322
  9.1 0.9 %copy-start.5 = (s32[4,256]{1,0:T(4,128)S(1)}, s32[4,256]{1,0:T(4,128)}, u32[]{:S(2)}) copy-start(s32[4,256]{1,0:T(4,128)} %code.1) | copy-start | bytes 12292
  9.1 1.0 %copy-start.6 = (s32[4,256]{1,0:T(4,128)S(1)}, s32[4,256]{1,0:T(4,128)}, u32[]{:S(2)}) copy-start(s32[4,256]{1,0:T(4,128)} %count.1) | copy-start | bytes 12292
  44.4 9.7 %collective-permute-start.2 = (f32[48,128]{1,0:T(8,128)S(1)}, f32[48,128]{1,0:T(8,128)S(1)}, u32[]{:S(2)}, u32[]{:S(2)}) collective-permute-start(f32[48,128]{1,0:T(8,128)S(1)} %shard_map.69.share), channel_id=1, source_target_pairs={{1,2},{2,1},{3,4},{4,3},{5,6},{6,5},{7,8},{8,7},{9,10},{10,9},{11,... | collective-permute-start | bytes 73736 | tf_op jit(solution)/shard_map/ppermute | solution.py:345
  50.5 3.6 %copy-start.7 = (f32[4,128]{1,0:T(4,128)S(1)}, f32[4,128]{1,0:T(4,128)}, u32[]{:S(2)}) copy-start(f32[4,128]{1,0:T(4,128)} %inverse_var.1) | copy-start | bytes 6148
  75.2 5.0 %copy-start.2 = (bf16[2,128,2,128]{3,2,1,0:T(2,128)(2,1)S(1)}, bf16[2,128,2,128]{3,2,1,0:T(2,128)(2,1)}, u32[]{:S(2)}) copy-start(bf16[2,128,2,128]{3,2,1,0:T(2,128)(2,1)} %param.7) | copy-start | bytes 393220
  75.2 5.1 %copy-start.4 = (bf16[128,128]{1,0:T(8,128)(2,1)S(1)}, bf16[128,128]{1,0:T(8,128)(2,1)}, u32[]{:S(2)}) copy-start(bf16[128,128]{1,0:T(8,128)(2,1)} %vertical.3) | copy-start | bytes 98308
  75.3 11.5 %collective-permute-start.4 = (f32[512,128]{1,0:T(8,128)S(1)}, f32[512,128]{1,0:T(8,128)S(1)}, u32[]{:S(2)}, u32[]{:S(2)}) collective-permute-start(f32[512,128]{1,0:T(8,128)S(1)} %shard_map.71.field), channel_id=1, source_target_pairs={{1,2},{2,1},{3,4},{4,3},{5,6},{6,5},{7,8},{8,7},{9,10},{10,9},{11,... | collective-permute-start | bytes 786440 | tf_op jit(solution)/shard_map/ppermute | solution.py:362
  78.3 14.8 %collective-permute-start.3 = (f32[512,128]{1,0:T(8,128)S(1)}, f32[512,128]{1,0:T(8,128)S(1)}, u32[]{:S(2)}, u32[]{:S(2)}) collective-permute-start(f32[512,128]{1,0:T(8,128)S(1)} %shard_map.71.field), channel_id=1, source_target_pairs={{0,1},{1,0},{2,3},{3,2},{4,5},{5,4},{6,7},{7,6},{8,9},{9,8},{10,11... | collective-permute-start | bytes 786440 | tf_op jit(solution)/shard_map/ppermute | solution.py:361

commit v4 on v3

--- a/solution.py
+++ b/solution.py
@@ -11,7 +11,6 @@
 far_weight = 0.25
 
 VMEM = pl.BlockSpec(memory_space=pltpu.VMEM)
-SMEM = pl.BlockSpec(memory_space=pltpu.SMEM)
 f32 = jnp.float32
 
 
@@ -76,20 +75,25 @@
 
 
 def neighbours(even, a, b):
-    keep = even != 0
+    keep = even > 0.5
     return [jnp.where(keep, y, x) for x, y in zip(a, b)], [jnp.where(keep, x, y) for x, y in zip(a, b)]
 
 
-def mix_kernel(control, vertical, out, wide):
-    levels = vertical.shape[0]
-    members = control.shape[0]
-    for k in range(members):
-        wide[...] = control[k].astype(f32)
-        for r in range(2):
-            row = wide[pl.ds(r, levels, stride=2), :].astype(jnp.bfloat16)
-            out[pl.ds(2 * levels * k + r, levels, stride=2), :] = jnp.dot(
-                vertical[...], row, preferred_element_type=f32
-            )
+def flags_of(place):
+    return [place[i : i + 1, :] for i in range(4)]
+
+
+def widen_kernel(control, out):
+    members, height = control.shape[:2]
+    for k in range(members):
+        out[k * height : (k + 1) * height, :] = control[k].astype(f32)
+
+
+def mixed_rows(vertical, fields):
+    width = fields[0].shape[1]
+    side_by_side = jnp.concatenate([x.astype(jnp.bfloat16) for x in fields], axis=1)
+    product = jnp.dot(vertical[...], side_by_side, preferred_element_type=f32)
+    return [product[:, i * width : (i + 1) * width] for i in range(len(fields))]
 
 
 def meta_kernel(after, code, count, ensemble, out):
@@ -106,43 +110,50 @@
             )
 
 
-def own_kernel(place, field, out):
+def own_kernel(place, control, vertical, out):
     members, _, levels = out.shape[:3]
-    top, bottom = place[1].astype(f32), place[2].astype(f32)
-    for k in range(members):
-        both = own_part(rows_of(field, 2 * k * levels, levels), top, bottom)
+    _, top, bottom, _ = flags_of(place)
+    for k in range(members):
+        rows = mixed_rows(vertical, rows_of(control, 2 * k * levels, levels))
+        both = own_part(rows, top, bottom)
         for r in range(2):
             out[k, r] = both[r]
 
 
 def own_control_kernel(place, field, control, vertical, out, wide, turned, spare):
-    own_kernel(place, field, out)
     turned[...] = vertical[...].astype(f32).T.astype(turned.dtype)
     members, _, levels = out.shape[:3]
-    for k in range(members):
+    _, top, bottom, _ = flags_of(place)
+    for k in range(members):
+        both = own_part(rows_of(field, 2 * k * levels, levels), top, bottom)
         spare[...] = control[k].astype(f32)
         for r in range(2):
+            out[k, r] = both[r]
             wide[k, r] = spare[pl.ds(r, levels, stride=2), :]
 
 
-def smoothed_rows(place, k, own, side_a, side_b):
-    even, top, bottom = (place[i] for i in range(3))
+def smoothed_rows(place, k, own, side_a, side_b, vertical=None):
+    even, top, bottom, _ = flags_of(place)
     levels = own.shape[2]
     at = 2 * k * levels
     above, below = neighbours(even, rows_of(side_a, at, levels), rows_of(side_b, at, levels))
-    both = halo_part(above, below, top.astype(f32), bottom.astype(f32))
+    if vertical is not None:
+        rows = mixed_rows(vertical, above + below)
+        above, below = rows[:2], rows[2:]
+    both = halo_part(above, below, top, bottom)
     return [own[k, r] + both[r] for r in range(2)]
 
 
-def partial_kernel(factor, place, after, own, side_a, side_b, ensemble, keep, send, local):
+def partial_kernel(
+    factor, place, after, own, side_a, side_b, vertical, ensemble, keep, send, local
+):
     members, variables, height = ensemble.shape[:3]
     levels = height // 2
-    first_core = place[3]
-    for k in range(members):
-        both = smoothed_rows(place, k, own, side_a, side_b)
+    for k in range(members):
+        both = smoothed_rows(place, k, own, side_a, side_b, vertical)
         for r in range(2):
             local[k, pl.ds(r, levels, stride=2), :] = both[r]
-    mine = first_core != 0
+    mine = flags_of(place)[3] > 0.5
     for j in range(keep.shape[0]):
         at = pl.ds(16 * j, 16)
         fields = [local[k, at, :] for k in range(members)]
@@ -156,7 +167,7 @@
 
 
 def pair_sum_kernel(place, keep, gathered, out):
-    first = place[3] != 0
+    first = flags_of(place)[3] > 0.5
     for j in range(out.shape[0]):
         out[j] = keep[j] + jnp.where(first, gathered[1, j], gathered[0, j])
 
@@ -171,19 +182,18 @@
     out[rows:, :] = meta[...]
 
 
-def observe_kernel(place, inverse_var, share, swap_b, pair_a, out, rows):
-    even, top, bottom = (place[i] for i in range(3))
+def observe_kernel(place, weights, share, swap_b, pair_a, out, rows):
+    even, top, bottom, _ = flags_of(place)
     height = rows.shape[0]
     n = height // 2
     own = rows_of(share, 0, n)
-    keep_even = even != 0
+    keep_even = even > 0.5
     a = [
         jnp.where(keep_even, pair_a[1, pl.ds(r, n, stride=2), :], pair_a[0, pl.ds(r, n, stride=2), :])
         for r in range(2)
     ]
     above, below = neighbours(even, a, rows_of(swap_b, 0, n))
     u = dict(zip(range(-2, 4), above + own + below))
-    top, bottom = top.astype(f32), bottom.astype(f32)
 
     def inside(f):
         return top if f < 0 else bottom if f > 3 else None
@@ -210,14 +220,7 @@
         at = (2 * which + phase) * 4 + line
         return table[block][at : at + 1, :]
 
-    variables = out.shape[1]
-    per_owner = n // variables
-    line = lax.broadcasted_iota(jnp.int32, own[0].shape, 0)
-    scale = jnp.zeros(own[0].shape, f32)
-    for v in range(variables):
-        for l in range(per_owner):
-            value = inverse_var[v, place[4] + l]
-            scale = jnp.where(line == v * per_owner + l, value, scale)
+    scale = weights[...]
     forcing, first, second, third, fourth = {}, {}, {}, {}, {}
     for f in range(-2, 6):
         e, o = fine[f]
@@ -251,7 +254,7 @@
         )
         result = near_weight * (e + o) + far_weight * (from_left(o) + from_right(e))
         rows[pl.ds(a_row, n, stride=2), :] = result
-    for v in range(variables):
+    for v in range(out.shape[1]):
         tile = rows[8 * v : 8 * v + 8, :]
         for j in range(out.shape[0]):
             out[j, v] = tile
@@ -294,15 +297,10 @@
     per_owner = levels // mem_size
     assert own_rows == 2 and per_owner * own_rows == 8
     mem_at, grid_at = lax.axis_index("mem"), lax.axis_index("grid")
-    place = jnp.stack(
-        [
-            (grid_at % 2 == 0).astype(jnp.int32),
-            (grid_at > 0).astype(jnp.int32),
-            (grid_at < grid_size - 1).astype(jnp.int32),
-            (mem_at % 2 == 0).astype(jnp.int32),
-            (mem_at * per_owner).astype(jnp.int32),
-        ]
-    )
+    flags = jnp.stack([grid_at % 2 == 0, grid_at > 0, grid_at < grid_size - 1, mem_at % 2 == 0])
+    place = jnp.broadcast_to(jnp.pad(flags.astype(f32), (0, 4))[:, None], (8, width))
+    weights = lax.dynamic_slice_in_dim(inverse_var, mem_at * per_owner, per_owner, 1)
+    weights = jnp.broadcast_to(weights.reshape(-1, 1), (variables * per_owner, width))
     swap_a = [(i, i ^ 1) for i in range(grid_size)]
     swap_b = [(i, ((i + 1) ^ 1) - 1) for i in range(1, grid_size - 1)]
     pairs_a = [[2 * i, 2 * i + 1] for i in range(grid_size // 2)]
@@ -313,30 +311,26 @@
     ctl = control.reshape(members, height, width)
     meta_rows = 4 * obs_code.shape[0]
 
-    mixed = call(
-        mix_kernel,
-        jax.ShapeDtypeStruct((members * height, width), f32),
-        [VMEM, VMEM],
-        [pltpu.VMEM((height, width), f32)],
-    )(ctl, vertical)
-    mixed_a = lax.ppermute(mixed, "grid", swap_a)
-    mixed_b = lax.ppermute(mixed, "grid", swap_b)
+    field = jax.ShapeDtypeStruct((members * height, width), f32)
+    wide = call(widen_kernel, field, [VMEM])(ctl)
+    wide_a = lax.ppermute(wide, "grid", swap_a)
+    wide_b = lax.ppermute(wide, "grid", swap_b)
     meta = call(
         meta_kernel, jax.ShapeDtypeStruct((meta_rows, width), f32), [ANY, VMEM, VMEM, VMEM]
-    )(mixed, obs_code, obs_count, ens)
+    )(wide, obs_code, obs_count, ens)
     own_shape = jax.ShapeDtypeStruct((members, own_rows, levels, width), f32)
-    own = call(own_kernel, own_shape, [SMEM, VMEM])(place, mixed)
+    own = call(own_kernel, own_shape, [VMEM] * 3)(place, wide, vertical)
 
     block = jax.ShapeDtypeStruct((half, variables, 8, width), f32)
     keep, send = call(
         functools.partial(partial_kernel, factor),
         (block, block),
-        [SMEM, ANY] + [VMEM] * 4,
+        [VMEM, ANY] + [VMEM] * 5,
         [pltpu.VMEM((members, height, width), f32)],
-    )(place, meta, own, mixed_a, mixed_b, ens)
+    )(place, meta, own, wide_a, wide_b, vertical, ens)
     gathered = lax.all_gather(send, "mem", axis=0, axis_index_groups=cores)
-    paired = call(pair_sum_kernel, block, [SMEM, VMEM, VMEM])(place, keep, gathered)
-    paired, meta, place = lax.optimization_barrier((paired, meta, place))
+    paired = call(pair_sum_kernel, block, [VMEM, VMEM, VMEM])(place, keep, gathered)
+    paired, meta, place, weights = lax.optimization_barrier((paired, meta, place, weights))
     arrived = lax.all_to_all(paired, "mem", 0, 0, axis_index_groups=same_core, tiled=True)
     share = call(
         total_kernel, jax.ShapeDtypeStruct((variables * 8 + meta_rows, width), f32), [VMEM, VMEM]
@@ -347,15 +341,15 @@
     spread = call(
         observe_kernel,
         block,
-        [SMEM, SMEM] + [VMEM] * 3,
+        [VMEM] * 5,
         [pltpu.VMEM((variables * 8, width), f32)],
-    )(place, inverse_var, share, share_b, share_a)
+    )(place, weights, share, share_b, share_a)
     mine = lax.all_to_all(spread, "mem", 0, 0, axis_index_groups=same_core, tiled=True)
     adjoint = lax.all_gather(mine, "mem", axis=0, axis_index_groups=cores)
 
     projected = call(
         functools.partial(project_kernel, factor),
-        jax.ShapeDtypeStruct((members * height, width), f32),
+        field,
         [VMEM, VMEM],
     )(adjoint, ens)
     projected_a = lax.ppermute(projected, "grid", swap_a)
@@ -363,14 +357,14 @@
     own, wide, turned = call(
         own_control_kernel,
         (own_shape, own_shape, jax.ShapeDtypeStruct(vertical.shape, vertical.dtype)),
-        [SMEM, VMEM, VMEM, VMEM],
+        [VMEM, VMEM, VMEM, VMEM],
         [pltpu.VMEM((height, width), f32)],
     )(place, projected, ctl, vertical)
     whole = jax.ShapeDtypeStruct((members, height, width), f32)
     out = call(
         product_kernel,
         whole,
-        [SMEM] + [VMEM] * 5,
+        [VMEM] + [VMEM] * 5,
         [pltpu.VMEM(whole.shape, f32), pltpu.SemaphoreType.DMA((members,))],
         out_spec=ANY,
     )(place, own, projected_a, projected_b, wide, turned)

time: 95.2 us -> 92.4 us (0.971)
  Pallas kernels: 6.68 us -> 3.48 us
    pallas_call x7, Pallas kernels: 5.33 us -> 2.7 us  [the longest x1 1.13 us: per_device(): call(product_kernel, whole, [VMEM] + [VMEM] * 5, [pltpu.VMEM(whole.shape,...]
  transfers between devices with their start and end apart: 5 -> 5, of which waited for: 4 -> 4; matrix products, arithmetic and copies ran while one was open for 0% -> 0% of each run, Pallas kernels for 2% -> 1%
where the time goes in v4:
time: 92.4 us; the launch traced here: 91.9 us
  blocking collectives  46.8 us (51%)
  waiting for transfers between devices  21 us (23%)
  starting transfers between devices  18.2 us (20%)
  Pallas kernels  3.48 us (4%)
  local copies, waits for them, and re-layouts  2.2 us (2%)
    all_to_all x1, blocking collectives, per_device(): lax.all_to_all(paired, 'mem', 0, 0, axis_index_groups=same_core, tiled=True)  20.8 us
    all_to_all x1, blocking collectives, per_device(): lax.all_to_all(spread, 'mem', 0, 0, axis_index_groups=same_core, tiled=True)  14.1 us
    ppermute x1, waiting for transfers between devices, per_device(): wide_a = lax.ppermute(wide, 'grid', swap_a)  6.65 us
    ppermute x1, waiting for transfers between devices, per_device(): projected_a = lax.ppermute(projected, 'grid', swap_a)  6.31 us
    ppermute x1, waiting for transfers between devices, per_device(): projected_b = lax.ppermute(projected, 'grid', swap_b)  6.15 us
    ppermute x1, starting transfers between devices, per_device(): share_b = lax.ppermute(share, 'grid', swap_b)  6.08 us
    all_gather x1, blocking collectives, per_device(): adjoint = lax.all_gather(mine, 'mem', axis=0, axis_index_groups=cores)  5.99 us
    ppermute x1, starting transfers between devices, per_device(): wide_b = lax.ppermute(wide, 'grid', swap_b)  5.31 us
  transfers between devices with their start and end apart: 5, of which 4 were waited for; matrix products, arithmetic and copies ran while one was open for 0% of the time, Pallas kernels for 1%

profile of v4, /device:TPU:195, one launch (start us, length us, event | category | flops | bytes accessed | tf_op | source)
XLA Modules:
  0.0 91.9 jit_solution(10143749138938029754)
XLA Ops:
  0.0 0.0 copy-start
  0.0 0.0 copy-start.2
  0.0 0.9 copy-done.2
  0.9 0.0 copy-start.1
  0.9 5.3 %collective-permute-start.1 = (f32[512,128]{1,0:T(8,128)S(1)}, f32[512,128]{1,0:T(8,128)S(1)}, u32[]{:S(2)}, u32[]{:S(2)}) collective-permute-start(f32[512,128]{1,0:T(8,128)S(1)} %shard_map.64.after.control), channel_id=1, source_target_pairs={{1,2},{2,1},{3,4},{4,3},{5,6},{6,5},{7,8},{8,7},{9,10},{10,9},{11,... | collective-permute-start | bytes 786440 | tf_op jit(solution)/shard_map/ppermute | solution.py:317
  6.3 1.9 %collective-permute-start = (f32[512,128]{1,0:T(8,128)S(1)}, f32[512,128]{1,0:T(8,128)S(1)}, u32[]{:S(2)}, u32[]{:S(2)}) collective-permute-start(f32[512,128]{1,0:T(8,128)S(1)} %shard_map.64.after.control), channel_id=1, source_target_pairs={{0,1},{1,0},{2,3},{3,2},{4,5},{5,4},{6,7},{7,6},{8,9},{9,8},{10,11... | collective-permute-start | bytes 786440 | tf_op jit(solution)/shard_map/ppermute | solution.py:316
  8.2 0.0 copy-done
  8.2 0.1 constant_dynamic-slice_fusion
  8.3 0.1 broadcast_in_dim.14
  8.4 0.1 pad_add_fusion
  8.5 0.1 broadcast_in_dim.6.place
  8.5 0.0 copy-start.4
  8.5 0.8 copy-done.4
  9.3 0.0 copy-start.6
  9.3 0.0 copy-start.7
  9.3 0.5 shard_map.66.own
  9.8 0.0 copy-done.1
  9.8 0.2 copy-done.6
  10.0 0.0 copy-done.7
  10.0 0.0 copy-start.5
  10.0 0.3 shard_map.65.after.meta
  10.3 1.9 %collective-permute-done.1.side_b = f32[512,128]{1,0:T(8,128)S(1)} collective-permute-done((f32[512,128]{1,0:T(8,128)S(1)}, f32[512,128]{1,0:T(8,128)S(1)}, u32[]{:S(2)}, u32[]{:S(2)}) %collective-permute-start.1) | collective-permute-done | bytes 262176 | tf_op jit(solution)/shard_map/ppermute | solution.py:317
  12.3 6.7 %collective-permute-done.side_a = f32[512,128]{1,0:T(8,128)S(1)} collective-permute-done((f32[512,128]{1,0:T(8,128)S(1)}, f32[512,128]{1,0:T(8,128)S(1)}, u32[]{:S(2)}, u32[]{:S(2)}) %collective-permute-start) | collective-permute-done | bytes 262176 | tf_op jit(solution)/shard_map/ppermute | solution.py:316
  18.9 0.0 copy-done.5
  18.9 0.5 shard_map.67
  19.5 2.3 %all-gather = f32[32,4,8,128]{3,2,1,0:T(8,128)S(1)} all-gather(f32[16,4,8,128]{3,2,1,0:T(8,128)S(1)} %get-tuple-element.15), channel_id=2, replica_groups={{0,16},{32,48},{64,80},{96,112},{128,144},{160,176},{192,208},{224,240}..., dimensions={0}, use_global_device_ids=true | all-gather | bytes 786432 | tf_op jit(solution)/shard_map/all_gather | solution.py:331
  21.8 0.1 broadcast_in_dim.15.weights
  21.9 20.8 %all_to_all.10.arrived = f32[16,4,8,128]{3,2,1,0:T(8,128)S(1)} all-to-all(f32[16,4,8,128]{3,2,1,0:T(8,128)S(1)} %shard_map.68), channel_id=1, replica_groups={{0,32,64,96,128,160,192,224,256,288,320,352,384,416,448,480},{16,48,80,..., dimensions={0} | all-to-all | bytes 524288 | tf_op jit(solution)/shard_map/all_to_all | solution.py:334
  42.7 6.1 %collective-permute-start.2 = (f32[48,128]{1,0:T(8,128)S(1)}, f32[48,128]{1,0:T(8,128)S(1)}, u32[]{:S(2)}, u32[]{:S(2)}) collective-permute-start(f32[48,128]{1,0:T(8,128)S(1)} %shard_map.69.share), channel_id=1, source_target_pairs={{1,2},{2,1},{3,4},{4,3},{5,6},{6,5},{7,8},{8,7},{9,10},{10,9},{11,... | collective-permute-start | bytes 73736 | tf_op jit(solution)/shard_map/ppermute | solution.py:339
  48.8 3.6 %all-gather.1 = f32[96,128]{1,0:T(8,128)S(1)} all-gather(f32[48,128]{1,0:T(8,128)S(1)} %shard_map.69.share), channel_id=3, replica_groups={{0,1},{2,3},{4,5},{6,7},{8,9},{10,11},{12,13},{14,15},{16,17},{18,19},{..., dimensions={0}, use_global_device_ids=true | all-gather | bytes 73728 | tf_op jit(solution)/shard_map/all_gather | solution.py:340
  52.4 0.0 collective-permute-done.2.swap_b
  52.4 0.4 shard_map.70
  52.8 14.1 %all_to_all.11 = f32[16,4,8,128]{3,2,1,0:T(8,128)S(1)} all-to-all(f32[16,4,8,128]{3,2,1,0:T(8,128)S(1)} %shard_map.70), channel_id=1, replica_groups={{0,32,64,96,128,160,192,224,256,288,320,352,384,416,448,480},{16,48,80,..., dimensions={0} | all-to-all | bytes 524288 | tf_op jit(solution)/shard_map/all_to_all | solution.py:347
  66.9 6.0 %all-gather.2 = f32[32,4,8,128]{3,2,1,0:T(8,128)S(1)} all-gather(f32[16,4,8,128]{3,2,1,0:T(8,128)S(1)} %all_to_all.11), channel_id=4, replica_groups={{0,16},{32,48},{64,80},{96,112},{128,144},{160,176},{192,208},{224,240}..., dimensions={0}, use_global_device_ids=true | all-gather | bytes 786432 | tf_op jit(solution)/shard_map/all_gather | solution.py:348
  72.8 0.0 copy-start.3
  72.8 0.1 shard_map.71.field
  73.0 3.0 %collective-permute-start.4 = (f32[512,128]{1,0:T(8,128)S(1)}, f32[512,128]{1,0:T(8,128)S(1)}, u32[]{:S(2)}, u32[]{:S(2)}) collective-permute-start(f32[512,128]{1,0:T(8,128)S(1)} %shard_map.71.field), channel_id=1, source_target_pairs={{1,2},{2,1},{3,4},{4,3},{5,6},{6,5},{7,8},{8,7},{9,10},{10,9},{11,... | collective-permute-start | bytes 786440 | tf_op jit(solution)/shard_map/ppermute | solution.py:356
  76.0 1.9 %collective-permute-start.3 = (f32[512,128]{1,0:T(8,128)S(1)}, f32[512,128]{1,0:T(8,128)S(1)}, u32[]{:S(2)}, u32[]{:S(2)}) collective-permute-start(f32[512,128]{1,0:T(8,128)S(1)} %shard_map.71.field), channel_id=1, source_target_pairs={{0,1},{1,0},{2,3},{3,2},{4,5},{5,4},{6,7},{7,6},{8,9},{9,8},{10,11... | collective-permute-start | bytes 786440 | tf_op jit(solution)/shard_map/ppermute | solution.py:355
  77.9 0.0 copy-done.3
  77.9 0.4 shard_map.72
  78.4 6.2 %collective-permute-done.4.side_b = f32[512,128]{1,0:T(8,128)S(1)} collective-permute-done((f32[512,128]{1,0:T(8,128)S(1)}, f32[512,128]{1,0:T(8,128)S(1)}, u32[]{:S(2)}, u32[]{:S(2)}) %collective-permute-start.4) | collective-permute-done | bytes 262176 | tf_op jit(solution)/shard_map/ppermute | solution.py:356
  84.5 6.3 %collective-permute-done.3.side_a = f32[512,128]{1,0:T(8,128)S(1)} collective-permute-done((f32[512,128]{1,0:T(8,128)S(1)}, f32[512,128]{1,0:T(8,128)S(1)}, u32[]{:S(2)}, u32[]{:S(2)}) %collective-permute-start.3) | collective-permute-done | bytes 262176 | tf_op jit(solution)/shard_map/ppermute | solution.py:355
  90.8 1.1 %shard_map.73 = f32[2,256,128]{2,1,0:T(8,128)} custom-call(f32[8,128]{1,0:T(8,128)S(1)} %broadcast_in_dim.6.place, f32[2,2,128,128]{3,2,1,0:T(8,128)S(1)} %get-tuple-element.20.own, f32[512,128]{1,0:T(8,128)S(1)} %collective-permute-done.3.side_a, f32[512,128]{1,0:T(8,128)S(1)} %collective-permute-done.4.side_b, ...), custom_call_target="tpu_custom_call" | custom-call | flops 1000000 | bytes 1000000 | tf_op jit(solution)/shard_map/pallas_call | solution.py:364
  (4 shorter events, 0.1 us)
Async XLA Ops:
  0.0 8.2 %copy-start = (f32[4,128]{1,0:T(4,128)S(1)}, f32[4,128]{1,0:T(4,128)}, u32[]{:S(2)}) copy-start(f32[4,128]{1,0:T(4,128)} %param.9) | copy-start | bytes 6148
  0.0 0.9 copy-start.2
  0.9 8.9 %copy-start.1 = (bf16[2,4,128,2,128]{4,3,2,1,0:T(2,128)(2,1)S(1)}, bf16[2,4,128,2,128]{4,3,2,1,0:T(2,128)(2,1)}, u32[]{:S(2)}) copy-start(bf16[2,4,128,2,128]{4,3,2,1,0:T(2,128)(2,1)} %param.6) | copy-start | bytes 1572868
  0.9 11.3 %collective-permute-start.1 = (f32[512,128]{1,0:T(8,128)S(1)}, f32[512,128]{1,0:T(8,128)S(1)}, u32[]{:S(2)}, u32[]{:S(2)}) collective-permute-start(f32[512,128]{1,0:T(8,128)S(1)} %shard_map.64.after.control), channel_id=1, source_target_pairs={{1,2},{2,1},{3,4},{4,3},{5,6},{6,5},{7,8},{8,7},{9,10},{10,9},{11,... | collective-permute-start | bytes 786440 | tf_op jit(solution)/shard_map/ppermute | solution.py:317
  6.3 12.7 %collective-permute-start = (f32[512,128]{1,0:T(8,128)S(1)}, f32[512,128]{1,0:T(8,128)S(1)}, u32[]{:S(2)}, u32[]{:S(2)}) collective-permute-start(f32[512,128]{1,0:T(8,128)S(1)} %shard_map.64.after.control), channel_id=1, source_target_pairs={{0,1},{1,0},{2,3},{3,2},{4,5},{5,4},{6,7},{7,6},{8,9},{9,8},{10,11... | collective-permute-start | bytes 786440 | tf_op jit(solution)/shard_map/ppermute | solution.py:316
  8.5 0.8 copy-start.4
  9.3 0.7 copy-start.6
  9.3 0.7 copy-start.7
  10.0 8.9 %copy-start.5 = (bf16[128,128]{1,0:T(8,128)(2,1)S(1)}, bf16[128,128]{1,0:T(8,128)(2,1)}, u32[]{:S(2)}) copy-start(bf16[128,128]{1,0:T(8,128)(2,1)} %vertical.5) | copy-start | bytes 98308
  42.7 9.7 %collective-permute-start.2 = (f32[48,128]{1,0:T(8,128)S(1)}, f32[48,128]{1,0:T(8,128)S(1)}, u32[]{:S(2)}, u32[]{:S(2)}) collective-permute-start(f32[48,128]{1,0:T(8,128)S(1)} %shard_map.69.share), channel_id=1, source_target_pairs={{1,2},{2,1},{3,4},{4,3},{5,6},{6,5},{7,8},{8,7},{9,10},{10,9},{11,... | collective-permute-start | bytes 73736 | tf_op jit(solution)/shard_map/ppermute | solution.py:339
  72.8 5.1 %copy-start.3 = (bf16[2,128,2,128]{3,2,1,0:T(2,128)(2,1)S(1)}, bf16[2,128,2,128]{3,2,1,0:T(2,128)(2,1)}, u32[]{:S(2)}) copy-start(bf16[2,128,2,128]{3,2,1,0:T(2,128)(2,1)} %param.7) | copy-start | bytes 393220
  73.0 11.5 %collective-permute-start.4 = (f32[512,128]{1,0:T(8,128)S(1)}, f32[512,128]{1,0:T(8,128)S(1)}, u32[]{:S(2)}, u32[]{:S(2)}) collective-permute-start(f32[512,128]{1,0:T(8,128)S(1)} %shard_map.71.field), channel_id=1, source_target_pairs={{1,2},{2,1},{3,4},{4,3},{5,6},{6,5},{7,8},{8,7},{9,10},{10,9},{11,... | collective-permute-start | bytes 786440 | tf_op jit(solution)/shard_map/ppermute | solution.py:356
  76.0 14.8 %collective-permute-start.3 = (f32[512,128]{1,0:T(8,128)S(1)}, f32[512,128]{1,0:T(8,128)S(1)}, u32[]{:S(2)}, u32[]{:S(2)}) collective-permute-start(f32[512,128]{1,0:T(8,128)S(1)} %shard_map.71.field), channel_id=1, source_target_pairs={{0,1},{1,0},{2,3},{3,2},{4,5},{5,4},{6,7},{7,6},{8,9},{9,8},{10,11... | collective-permute-start | bytes 786440 | tf_op jit(solution)/shard_map/ppermute | solution.py:355

commit v5 on v4

--- a/solution.py
+++ b/solution.py
@@ -83,12 +83,6 @@
     return [place[i : i + 1, :] for i in range(4)]
 
 
-def widen_kernel(control, out):
-    members, height = control.shape[:2]
-    for k in range(members):
-        out[k * height : (k + 1) * height, :] = control[k].astype(f32)
-
-
 def mixed_rows(vertical, fields):
     width = fields[0].shape[1]
     side_by_side = jnp.concatenate([x.astype(jnp.bfloat16) for x in fields], axis=1)
@@ -96,7 +90,16 @@
     return [product[:, i * width : (i + 1) * width] for i in range(len(fields))]
 
 
-def meta_kernel(after, code, count, ensemble, out):
+def meta_kernel(after, place, inverse_var, code, count, ensemble, out, weights):
+    values = inverse_var[...]
+    variables = values.shape[0]
+    per_owner = weights.shape[0] // variables
+    lane = lanes(values.shape).astype(f32)
+    for l in range(per_owner):
+        picked = jnp.where(lane == place[4:5, :] + float(l), values, 0.0)
+        weights[pl.ds(l, variables, stride=per_owner), :] = jnp.broadcast_to(
+            jnp.sum(picked, axis=1, keepdims=True), values.shape
+        )
     width = code.shape[1]
     source = lax.broadcasted_iota(jnp.int32, (width, width // 2), 0)
     target = lax.broadcasted_iota(jnp.int32, (width, width // 2), 1)
@@ -120,16 +123,14 @@
             out[k, r] = both[r]
 
 
-def own_control_kernel(place, field, control, vertical, out, wide, turned, spare):
+def own_turned_kernel(place, field, vertical, out, turned):
     turned[...] = vertical[...].astype(f32).T.astype(turned.dtype)
     members, _, levels = out.shape[:3]
     _, top, bottom, _ = flags_of(place)
     for k in range(members):
         both = own_part(rows_of(field, 2 * k * levels, levels), top, bottom)
-        spare[...] = control[k].astype(f32)
         for r in range(2):
             out[k, r] = both[r]
-            wide[k, r] = spare[pl.ds(r, levels, stride=2), :]
 
 
 def smoothed_rows(place, k, own, side_a, side_b, vertical=None):
@@ -274,14 +275,15 @@
 
 
 def product_kernel(place, own, side_a, side_b, control, transposed, far, out, sems):
-    members, _, levels, width = control.shape
-    for k in range(members):
+    members, _, levels, width = own.shape
+    for k in range(members):
+        before = rows_of(control, 2 * k * levels, levels)
         both = smoothed_rows(place, k, own, side_a, side_b)
         rounded = jnp.concatenate([row.astype(jnp.bfloat16) for row in both], axis=1)
         back = jnp.dot(transposed[...], rounded, preferred_element_type=f32)
         for r in range(2):
             out[k, pl.ds(r, levels, stride=2), :] = (
-                control[k, r] + back[:, r * width : (r + 1) * width]
+                before[r] + back[:, r * width : (r + 1) * width]
             )
         pltpu.make_async_copy(out.at[k], far.at[k], sems.at[k]).start()
     for k in range(members):
@@ -297,10 +299,9 @@
     per_owner = levels // mem_size
     assert own_rows == 2 and per_owner * own_rows == 8
     mem_at, grid_at = lax.axis_index("mem"), lax.axis_index("grid")
-    flags = jnp.stack([grid_at % 2 == 0, grid_at > 0, grid_at < grid_size - 1, mem_at % 2 == 0])
-    place = jnp.broadcast_to(jnp.pad(flags.astype(f32), (0, 4))[:, None], (8, width))
-    weights = lax.dynamic_slice_in_dim(inverse_var, mem_at * per_owner, per_owner, 1)
-    weights = jnp.broadcast_to(weights.reshape(-1, 1), (variables * per_owner, width))
+    facts = [grid_at % 2 == 0, grid_at > 0, grid_at < grid_size - 1, mem_at % 2 == 0]
+    facts = jnp.stack([x.astype(f32) for x in facts] + [(mem_at * per_owner).astype(f32)])
+    place = jnp.broadcast_to(jnp.pad(facts, (0, 3))[:, None], (8, width))
     swap_a = [(i, i ^ 1) for i in range(grid_size)]
     swap_b = [(i, ((i + 1) ^ 1) - 1) for i in range(1, grid_size - 1)]
     pairs_a = [[2 * i, 2 * i + 1] for i in range(grid_size // 2)]
@@ -312,12 +313,17 @@
     meta_rows = 4 * obs_code.shape[0]
 
     field = jax.ShapeDtypeStruct((members * height, width), f32)
-    wide = call(widen_kernel, field, [VMEM])(ctl)
+    wide = ctl.reshape(members * height, width).astype(f32)
     wide_a = lax.ppermute(wide, "grid", swap_a)
     wide_b = lax.ppermute(wide, "grid", swap_b)
-    meta = call(
-        meta_kernel, jax.ShapeDtypeStruct((meta_rows, width), f32), [ANY, VMEM, VMEM, VMEM]
-    )(wide, obs_code, obs_count, ens)
+    meta, weights = call(
+        meta_kernel,
+        (
+            jax.ShapeDtypeStruct((meta_rows, width), f32),
+            jax.ShapeDtypeStruct((variables * per_owner, width), f32),
+        ),
+        [ANY] + [VMEM] * 5,
+    )(wide, place, inverse_var, obs_code, obs_count, ens)
     own_shape = jax.ShapeDtypeStruct((members, own_rows, levels, width), f32)
     own = call(own_kernel, own_shape, [VMEM] * 3)(place, wide, vertical)
 
@@ -354,12 +360,11 @@
     )(adjoint, ens)
     projected_a = lax.ppermute(projected, "grid", swap_a)
     projected_b = lax.ppermute(projected, "grid", swap_b)
-    own, wide, turned = call(
-        own_control_kernel,
-        (own_shape, own_shape, jax.ShapeDtypeStruct(vertical.shape, vertical.dtype)),
-        [VMEM, VMEM, VMEM, VMEM],
-        [pltpu.VMEM((height, width), f32)],
-    )(place, projected, ctl, vertical)
+    own, turned = call(
+        own_turned_kernel,
+        (own_shape, jax.ShapeDtypeStruct(vertical.shape, vertical.dtype)),
+        [VMEM] * 3,
+    )(place, projected, vertical)
     whole = jax.ShapeDtypeStruct((members, height, width), f32)
     out = call(
         product_kernel,

time: 92.4 us -> 92.1 us (level)
  local copies, waits for them, and re-layouts: 2.2 us -> 0.38 us
  waiting for transfers between devices: 21 us -> 22 us
    unnamed x16 -> x10, local copies, waits for them, and re-layouts: 1.9 us -> 0.21 us
    convert_element_type x0 -> x1, other arithmetic: none -> 0.98 us  [per_device(): wide = ctl.reshape(members * height, width).astype(f32)]
where the time goes in v5:
time: 92.1 us; the launch traced here: 91.8 us
  blocking collectives  46.8 us (51%)
  waiting for transfers between devices  22 us (24%)
  starting transfers between devices  18.1 us (20%)
  Pallas kernels  3.45 us (4%)
  other arithmetic  0.98 us (1%)
    all_to_all x1, blocking collectives, per_device(): lax.all_to_all(paired, 'mem', 0, 0, axis_index_groups=same_core, tiled=True)  20.8 us
    all_to_all x1, blocking collectives, per_device(): lax.all_to_all(spread, 'mem', 0, 0, axis_index_groups=same_core, tiled=True)  14.1 us
    ppermute x1, waiting for transfers between devices, per_device(): wide_a = lax.ppermute(wide, 'grid', swap_a)  6.65 us
    ppermute x1, waiting for transfers between devices, per_device(): projected_a = lax.ppermute(projected, 'grid', swap_a)  6.31 us
    ppermute x1, waiting for transfers between devices, per_device(): projected_b = lax.ppermute(projected, 'grid', swap_b)  6.17 us
    ppermute x1, starting transfers between devices, per_device(): share_b = lax.ppermute(share, 'grid', swap_b)  6.08 us
    all_gather x1, blocking collectives, per_device(): adjoint = lax.all_gather(mine, 'mem', axis=0, axis_index_groups=cores)  5.99 us
    ppermute x1, starting transfers between devices, per_device(): wide_b = lax.ppermute(wide, 'grid', swap_b)  5.18 us
  transfers between devices with their start and end apart: 5, of which 4 were waited for; matrix products, arithmetic and copies ran while one was open for 0% of the time, Pallas kernels for 1%

profile of v5, /device:TPU:195, one launch (start us, length us, event | category | flops | bytes accessed | tf_op | source)
XLA Modules:
  0.0 91.8 jit_solution(13172130379060536184)
XLA Ops:
  0.0 0.0 copy-start.1
  0.0 0.0 copy-start
  0.0 1.0 %convert.5.after.control = f32[512,128]{1,0:T(8,128)S(1)} convert(bf16[512,128]{1,0:T(8,128)(2,1)} %bitcast.18) | non-fusion elementwise | flops 65536 | bytes 393216 | tf_op jit(solution)/shard_map/convert_element_type | solution.py:316
  1.0 5.2 %collective-permute-start.1 = (f32[512,128]{1,0:T(8,128)S(1)}, f32[512,128]{1,0:T(8,128)S(1)}, u32[]{:S(2)}, u32[]{:S(2)}) collective-permute-start(f32[512,128]{1,0:T(8,128)S(1)} %convert.5.after.control), channel_id=1, source_target_pairs={{1,2},{2,1},{3,4},{4,3},{5,6},{6,5},{7,8},{8,7},{9,10},{10,9},{11,... | collective-permute-start | bytes 786440 | tf_op jit(solution)/shard_map/ppermute | solution.py:318
  6.2 1.9 %collective-permute-start = (f32[512,128]{1,0:T(8,128)S(1)}, f32[512,128]{1,0:T(8,128)S(1)}, u32[]{:S(2)}, u32[]{:S(2)}) collective-permute-start(f32[512,128]{1,0:T(8,128)S(1)} %convert.5.after.control), channel_id=1, source_target_pairs={{0,1},{1,0},{2,3},{3,2},{4,5},{5,4},{6,7},{7,6},{8,9},{9,8},{10,11... | collective-permute-start | bytes 786440 | tf_op jit(solution)/shard_map/ppermute | solution.py:317
  8.1 0.1 stack.39
  8.2 0.1 broadcast_in_dim.2.place
  8.3 0.0 copy-done.1
  8.3 0.0 copy-start.2
  8.3 0.0 copy-start.3
  8.3 0.0 copy-start.4
  8.3 0.5 shard_map.65.own
  8.8 0.0 copy-done
  8.8 0.2 copy-done.2
  9.0 0.0 copy-done.3
  9.0 0.0 copy-done.4
  9.0 0.3 shard_map.64
  9.4 2.8 %collective-permute-done.1.side_b = f32[512,128]{1,0:T(8,128)S(1)} collective-permute-done((f32[512,128]{1,0:T(8,128)S(1)}, f32[512,128]{1,0:T(8,128)S(1)}, u32[]{:S(2)}, u32[]{:S(2)}) %collective-permute-start.1) | collective-permute-done | bytes 262176 | tf_op jit(solution)/shard_map/ppermute | solution.py:318
  12.2 6.7 %collective-permute-done.side_a = f32[512,128]{1,0:T(8,128)S(1)} collective-permute-done((f32[512,128]{1,0:T(8,128)S(1)}, f32[512,128]{1,0:T(8,128)S(1)}, u32[]{:S(2)}, u32[]{:S(2)}) %collective-permute-start) | collective-permute-done | bytes 262176 | tf_op jit(solution)/shard_map/ppermute | solution.py:317
  18.8 0.5 shard_map.66
  19.4 2.3 %all-gather = f32[32,4,8,128]{3,2,1,0:T(8,128)S(1)} all-gather(f32[16,4,8,128]{3,2,1,0:T(8,128)S(1)} %get-tuple-element.17), channel_id=2, replica_groups={{0,16},{32,48},{64,80},{96,112},{128,144},{160,176},{192,208},{224,240}..., dimensions={0}, use_global_device_ids=true | all-gather | bytes 786432 | tf_op jit(solution)/shard_map/all_gather | solution.py:337
  21.7 0.1 shard_map.67
  21.7 20.8 %all_to_all.10.arrived = f32[16,4,8,128]{3,2,1,0:T(8,128)S(1)} all-to-all(f32[16,4,8,128]{3,2,1,0:T(8,128)S(1)} %shard_map.67), channel_id=1, replica_groups={{0,32,64,96,128,160,192,224,256,288,320,352,384,416,448,480},{16,48,80,..., dimensions={0} | all-to-all | bytes 524288 | tf_op jit(solution)/shard_map/all_to_all | solution.py:340
  42.6 6.1 %collective-permute-start.2 = (f32[48,128]{1,0:T(8,128)S(1)}, f32[48,128]{1,0:T(8,128)S(1)}, u32[]{:S(2)}, u32[]{:S(2)}) collective-permute-start(f32[48,128]{1,0:T(8,128)S(1)} %shard_map.68.share), channel_id=1, source_target_pairs={{1,2},{2,1},{3,4},{4,3},{5,6},{6,5},{7,8},{8,7},{9,10},{10,9},{11,... | collective-permute-start | bytes 73736 | tf_op jit(solution)/shard_map/ppermute | solution.py:345
  48.6 3.6 %all-gather.1 = f32[96,128]{1,0:T(8,128)S(1)} all-gather(f32[48,128]{1,0:T(8,128)S(1)} %shard_map.68.share), channel_id=3, replica_groups={{0,1},{2,3},{4,5},{6,7},{8,9},{10,11},{12,13},{14,15},{16,17},{18,19},{..., dimensions={0}, use_global_device_ids=true | all-gather | bytes 73728 | tf_op jit(solution)/shard_map/all_gather | solution.py:346
  52.2 0.0 collective-permute-done.2.swap_b
  52.3 0.4 shard_map.69
  52.6 14.1 %all_to_all.11 = f32[16,4,8,128]{3,2,1,0:T(8,128)S(1)} all-to-all(f32[16,4,8,128]{3,2,1,0:T(8,128)S(1)} %shard_map.69), channel_id=1, replica_groups={{0,32,64,96,128,160,192,224,256,288,320,352,384,416,448,480},{16,48,80,..., dimensions={0} | all-to-all | bytes 524288 | tf_op jit(solution)/shard_map/all_to_all | solution.py:353
  66.7 6.0 %all-gather.2 = f32[32,4,8,128]{3,2,1,0:T(8,128)S(1)} all-gather(f32[16,4,8,128]{3,2,1,0:T(8,128)S(1)} %all_to_all.11), channel_id=4, replica_groups={{0,16},{32,48},{64,80},{96,112},{128,144},{160,176},{192,208},{224,240}..., dimensions={0}, use_global_device_ids=true | all-gather | bytes 786432 | tf_op jit(solution)/shard_map/all_gather | solution.py:354
  72.7 0.1 shard_map.70.field
  72.8 3.0 %collective-permute-start.4 = (f32[512,128]{1,0:T(8,128)S(1)}, f32[512,128]{1,0:T(8,128)S(1)}, u32[]{:S(2)}, u32[]{:S(2)}) collective-permute-start(f32[512,128]{1,0:T(8,128)S(1)} %shard_map.70.field), channel_id=1, source_target_pairs={{1,2},{2,1},{3,4},{4,3},{5,6},{6,5},{7,8},{8,7},{9,10},{10,9},{11,... | collective-permute-start | bytes 786440 | tf_op jit(solution)/shard_map/ppermute | solution.py:362
  75.8 1.9 %collective-permute-start.3 = (f32[512,128]{1,0:T(8,128)S(1)}, f32[512,128]{1,0:T(8,128)S(1)}, u32[]{:S(2)}, u32[]{:S(2)}) collective-permute-start(f32[512,128]{1,0:T(8,128)S(1)} %shard_map.70.field), channel_id=1, source_target_pairs={{0,1},{1,0},{2,3},{3,2},{4,5},{5,4},{6,7},{7,6},{8,9},{9,8},{10,11... | collective-permute-start | bytes 786440 | tf_op jit(solution)/shard_map/ppermute | solution.py:361
  77.8 0.4 shard_map.71
  78.2 6.2 %collective-permute-done.4.side_b = f32[512,128]{1,0:T(8,128)S(1)} collective-permute-done((f32[512,128]{1,0:T(8,128)S(1)}, f32[512,128]{1,0:T(8,128)S(1)}, u32[]{:S(2)}, u32[]{:S(2)}) %collective-permute-start.4) | collective-permute-done | bytes 262176 | tf_op jit(solution)/shard_map/ppermute | solution.py:362
  84.3 6.3 %collective-permute-done.3.side_a = f32[512,128]{1,0:T(8,128)S(1)} collective-permute-done((f32[512,128]{1,0:T(8,128)S(1)}, f32[512,128]{1,0:T(8,128)S(1)}, u32[]{:S(2)}, u32[]{:S(2)}) %collective-permute-start.3) | collective-permute-done | bytes 262176 | tf_op jit(solution)/shard_map/ppermute | solution.py:361
  90.7 1.1 %shard_map.72 = f32[2,256,128]{2,1,0:T(8,128)} custom-call(f32[8,128]{1,0:T(8,128)S(1)} %broadcast_in_dim.2.place, f32[2,2,128,128]{3,2,1,0:T(8,128)S(1)} %get-tuple-element.23.own, f32[512,128]{1,0:T(8,128)S(1)} %collective-permute-done.3.side_a, f32[512,128]{1,0:T(8,128)S(1)} %collective-permute-done.4.side_b, f32[512,128]{1,0:T(8,128)S(1)} %convert.5.after.control, ...), custom_call_target="tpu_custom_call" | custom-call | flops 1000000 | bytes 1000000 | tf_op jit(solution)/shard_map/pallas_call | solution.py:369
  (2 shorter events, 0.0 us)
Async XLA Ops:
  0.0 8.3 %copy-start.1 = (bf16[128,128]{1,0:T(8,128)(2,1)S(1)}, bf16[128,128]{1,0:T(8,128)(2,1)}, u32[]{:S(2)}) copy-start(bf16[128,128]{1,0:T(8,128)(2,1)} %vertical.5) | copy-start | bytes 98308
  0.0 8.8 %copy-start = (bf16[2,4,128,2,128]{4,3,2,1,0:T(2,128)(2,1)S(1)}, bf16[2,4,128,2,128]{4,3,2,1,0:T(2,128)(2,1)}, u32[]{:S(2)}) copy-start(bf16[2,4,128,2,128]{4,3,2,1,0:T(2,128)(2,1)} %param.6) | copy-start | bytes 1572868
  1.0 11.2 %collective-permute-start.1 = (f32[512,128]{1,0:T(8,128)S(1)}, f32[512,128]{1,0:T(8,128)S(1)}, u32[]{:S(2)}, u32[]{:S(2)}) collective-permute-start(f32[512,128]{1,0:T(8,128)S(1)} %convert.5.after.control), channel_id=1, source_target_pairs={{1,2},{2,1},{3,4},{4,3},{5,6},{6,5},{7,8},{8,7},{9,10},{10,9},{11,... | collective-permute-start | bytes 786440 | tf_op jit(solution)/shard_map/ppermute | solution.py:318
  6.2 12.7 %collective-permute-start = (f32[512,128]{1,0:T(8,128)S(1)}, f32[512,128]{1,0:T(8,128)S(1)}, u32[]{:S(2)}, u32[]{:S(2)}) collective-permute-start(f32[512,128]{1,0:T(8,128)S(1)} %convert.5.after.control), channel_id=1, source_target_pairs={{0,1},{1,0},{2,3},{3,2},{4,5},{5,4},{6,7},{7,6},{8,9},{9,8},{10,11... | collective-permute-start | bytes 786440 | tf_op jit(solution)/shard_map/ppermute | solution.py:317
  8.3 0.7 copy-start.2
  8.3 0.7 copy-start.3
  8.3 0.7 copy-start.4
  42.6 9.7 %collective-permute-start.2 = (f32[48,128]{1,0:T(8,128)S(1)}, f32[48,128]{1,0:T(8,128)S(1)}, u32[]{:S(2)}, u32[]{:S(2)}) collective-permute-start(f32[48,128]{1,0:T(8,128)S(1)} %shard_map.68.share), channel_id=1, source_target_pairs={{1,2},{2,1},{3,4},{4,3},{5,6},{6,5},{7,8},{8,7},{9,10},{10,9},{11,... | collective-permute-start | bytes 73736 | tf_op jit(solution)/shard_map/ppermute | solution.py:345
  72.8 11.5 %collective-permute-start.4 = (f32[512,128]{1,0:T(8,128)S(1)}, f32[512,128]{1,0:T(8,128)S(1)}, u32[]{:S(2)}, u32[]{:S(2)}) collective-permute-start(f32[512,128]{1,0:T(8,128)S(1)} %shard_map.70.field), channel_id=1, source_target_pairs={{1,2},{2,1},{3,4},{4,3},{5,6},{6,5},{7,8},{8,7},{9,10},{10,9},{11,... | collective-permute-start | bytes 786440 | tf_op jit(solution)/shard_map/ppermute | solution.py:362
  75.8 14.8 %collective-permute-start.3 = (f32[512,128]{1,0:T(8,128)S(1)}, f32[512,128]{1,0:T(8,128)S(1)}, u32[]{:S(2)}, u32[]{:S(2)}) collective-permute-start(f32[512,128]{1,0:T(8,128)S(1)} %shard_map.70.field), channel_id=1, source_target_pairs={{0,1},{1,0},{2,3},{3,2},{4,5},{5,4},{6,7},{7,6},{8,9},{9,8},{10,11... | collective-permute-start | bytes 786440 | tf_op jit(solution)/shard_map/ppermute | solution.py:361

commit v6 on v5

--- a/solution.py
+++ b/solution.py
@@ -183,17 +183,12 @@
     out[rows:, :] = meta[...]
 
 
-def observe_kernel(place, weights, share, swap_b, pair_a, out, rows):
+def observe_kernel(place, weights, share, swap_b, swap_a, out, rows):
     even, top, bottom, _ = flags_of(place)
     height = rows.shape[0]
     n = height // 2
     own = rows_of(share, 0, n)
-    keep_even = even > 0.5
-    a = [
-        jnp.where(keep_even, pair_a[1, pl.ds(r, n, stride=2), :], pair_a[0, pl.ds(r, n, stride=2), :])
-        for r in range(2)
-    ]
-    above, below = neighbours(even, a, rows_of(swap_b, 0, n))
+    above, below = neighbours(even, rows_of(swap_a, 0, n), rows_of(swap_b, 0, n))
     u = dict(zip(range(-2, 4), above + own + below))
 
     def inside(f):
@@ -212,8 +207,7 @@
             masked(near_weight * line + far_weight * from_left(line), f),
             masked(near_weight * line + far_weight * from_right(line), f),
         ]
-    meta_a = jnp.where(keep_even, pair_a[1, height:, :], pair_a[0, height:, :])
-    wanted_above, wanted_below = neighbours(even, [meta_a], [swap_b[height:, :]])
+    wanted_above, wanted_below = neighbours(even, [swap_a[height:, :]], [swap_b[height:, :]])
     table = [wanted_above[0], share[height:, :], wanted_below[0]]
 
     def lookup(which, phase, f):
@@ -304,7 +298,6 @@
     place = jnp.broadcast_to(jnp.pad(facts, (0, 3))[:, None], (8, width))
     swap_a = [(i, i ^ 1) for i in range(grid_size)]
     swap_b = [(i, ((i + 1) ^ 1) - 1) for i in range(1, grid_size - 1)]
-    pairs_a = [[2 * i, 2 * i + 1] for i in range(grid_size // 2)]
     cores = [[2 * i, 2 * i + 1] for i in range(half)]
     same_core = [[2 * i + c for i in range(half)] for c in range(2)]
 
@@ -342,8 +335,8 @@
         total_kernel, jax.ShapeDtypeStruct((variables * 8 + meta_rows, width), f32), [VMEM, VMEM]
     )(arrived, meta)
 
+    share_a = lax.ppermute(share, "grid", swap_a)
     share_b = lax.ppermute(share, "grid", swap_b)
-    share_a = lax.all_gather(share, "grid", axis=0, axis_index_groups=pairs_a)
     spread = call(
         observe_kernel,
         block,

time: 92.1 us -> 91.7 us (level)
  starting transfers between devices: 18.1 us -> 22.9 us
  blocking collectives: 46.8 us -> 42.7 us
  waiting for transfers between devices: 22 us -> 20.7 us
    all_gather x1 -> x0, blocking collectives: 3.62 us -> none  [per_device(): share_a = lax.all_gather(share, 'grid', axis=0, axis_index_groups=pairs_a)]
    ppermute x1, starting transfers between devices: 3.01 us -> 5.89 us  [per_device(): projected_b = lax.ppermute(projected, 'grid', swap_b)]
    ppermute x1, waiting for transfers between devices: 6.17 us -> 3.94 us  [per_device(): projected_b = lax.ppermute(projected, 'grid', swap_b)]
    ppermute x0 -> x1, starting transfers between devices: none -> 1.92 us  [per_device(): share_a = lax.ppermute(share, 'grid', swap_a)]
    ppermute x1, waiting for transfers between devices: 0.01 us -> 1.19 us  [per_device(): share_b = lax.ppermute(share, 'grid', swap_b)]
  transfers between devices with their start and end apart: 5 -> 6, of which waited for: 4 -> 5; matrix products, arithmetic and copies ran while one was open for 0% -> 0% of each run, Pallas kernels for 1% -> 1%
where the time goes in v6:
time: 91.7 us; the launch traced here: 91.3 us
  blocking collectives  42.7 us (47%)
  starting transfers between devices  22.9 us (25%)
  waiting for transfers between devices  20.7 us (23%)
  Pallas kernels  3.45 us (4%)
  other arithmetic  0.98 us (1%)
    all_to_all x1, blocking collectives, per_device(): lax.all_to_all(paired, 'mem', 0, 0, axis_index_groups=same_core, tiled=True)  20.8 us
    all_to_all x1, blocking collectives, per_device(): lax.all_to_all(spread, 'mem', 0, 0, axis_index_groups=same_core, tiled=True)  14.4 us
    ppermute x1, waiting for transfers between devices, per_device(): wide_a = lax.ppermute(wide, 'grid', swap_a)  6.65 us
    ppermute x1, starting transfers between devices, per_device(): share_b = lax.ppermute(share, 'grid', swap_b)  6.08 us
    ppermute x1, waiting for transfers between devices, per_device(): projected_a = lax.ppermute(projected, 'grid', swap_a)  6.07 us
    ppermute x1, starting transfers between devices, per_device(): projected_b = lax.ppermute(projected, 'grid', swap_b)  5.89 us
    all_gather x1, blocking collectives, per_device(): adjoint = lax.all_gather(mine, 'mem', axis=0, axis_index_groups=cores)  5.29 us
    ppermute x1, starting transfers between devices, per_device(): wide_b = lax.ppermute(wide, 'grid', swap_b)  5.18 us
  transfers between devices with their start and end apart: 6, of which 5 were waited for; matrix products, arithmetic and copies ran while one was open for 0% of the time, Pallas kernels for 1%

profile of v6, /device:TPU:195, one launch (start us, length us, event | category | flops | bytes accessed | tf_op | source)
XLA Modules:
  0.0 91.3 jit_solution(13233180311259898269)
XLA Ops:
  0.0 0.0 copy-start.1
  0.0 0.0 copy-start
  0.0 1.0 %convert.5.after.control = f32[512,128]{1,0:T(8,128)S(1)} convert(bf16[512,128]{1,0:T(8,128)(2,1)} %bitcast.16) | non-fusion elementwise | flops 65536 | bytes 393216 | tf_op jit(solution)/shard_map/convert_element_type | solution.py:309
  1.0 5.2 %collective-permute-start.1 = (f32[512,128]{1,0:T(8,128)S(1)}, f32[512,128]{1,0:T(8,128)S(1)}, u32[]{:S(2)}, u32[]{:S(2)}) collective-permute-start(f32[512,128]{1,0:T(8,128)S(1)} %convert.5.after.control), channel_id=1, source_target_pairs={{1,2},{2,1},{3,4},{4,3},{5,6},{6,5},{7,8},{8,7},{9,10},{10,9},{11,... | collective-permute-start | bytes 786440 | tf_op jit(solution)/shard_map/ppermute | solution.py:311
  6.2 1.9 %collective-permute-start = (f32[512,128]{1,0:T(8,128)S(1)}, f32[512,128]{1,0:T(8,128)S(1)}, u32[]{:S(2)}, u32[]{:S(2)}) collective-permute-start(f32[512,128]{1,0:T(8,128)S(1)} %convert.5.after.control), channel_id=1, source_target_pairs={{0,1},{1,0},{2,3},{3,2},{4,5},{5,4},{6,7},{7,6},{8,9},{9,8},{10,11... | collective-permute-start | bytes 786440 | tf_op jit(solution)/shard_map/ppermute | solution.py:310
  8.1 0.1 stack.39
  8.2 0.1 broadcast_in_dim.2.place
  8.3 0.0 copy-done.1
  8.3 0.0 copy-start.2
  8.3 0.0 copy-start.3
  8.3 0.0 copy-start.4
  8.3 0.5 shard_map.65.own
  8.8 0.0 copy-done
  8.8 0.2 copy-done.2
  9.0 0.0 copy-done.3
  9.0 0.0 copy-done.4
  9.0 0.3 shard_map.64
  9.4 2.8 %collective-permute-done.1.side_b = f32[512,128]{1,0:T(8,128)S(1)} collective-permute-done((f32[512,128]{1,0:T(8,128)S(1)}, f32[512,128]{1,0:T(8,128)S(1)}, u32[]{:S(2)}, u32[]{:S(2)}) %collective-permute-start.1) | collective-permute-done | bytes 262176 | tf_op jit(solution)/shard_map/ppermute | solution.py:311
  12.2 6.7 %collective-permute-done.side_a = f32[512,128]{1,0:T(8,128)S(1)} collective-permute-done((f32[512,128]{1,0:T(8,128)S(1)}, f32[512,128]{1,0:T(8,128)S(1)}, u32[]{:S(2)}, u32[]{:S(2)}) %collective-permute-start) | collective-permute-done | bytes 262176 | tf_op jit(solution)/shard_map/ppermute | solution.py:310
  18.8 0.5 shard_map.66
  19.4 2.3 %all-gather = f32[32,4,8,128]{3,2,1,0:T(8,128)S(1)} all-gather(f32[16,4,8,128]{3,2,1,0:T(8,128)S(1)} %get-tuple-element.17), channel_id=2, replica_groups={{0,16},{32,48},{64,80},{96,112},{128,144},{160,176},{192,208},{224,240}..., dimensions={0}, use_global_device_ids=true | all-gather | bytes 786432 | tf_op jit(solution)/shard_map/all_gather | solution.py:330
  21.7 0.1 shard_map.67
  21.7 20.8 %all_to_all.10.arrived = f32[16,4,8,128]{3,2,1,0:T(8,128)S(1)} all-to-all(f32[16,4,8,128]{3,2,1,0:T(8,128)S(1)} %shard_map.67), channel_id=1, replica_groups={{0,32,64,96,128,160,192,224,256,288,320,352,384,416,448,480},{16,48,80,..., dimensions={0} | all-to-all | bytes 524288 | tf_op jit(solution)/shard_map/all_to_all | solution.py:333
  42.6 1.9 %collective-permute-start.3 = (f32[48,128]{1,0:T(8,128)S(1)}, f32[48,128]{1,0:T(8,128)S(1)}, u32[]{:S(2)}, u32[]{:S(2)}) collective-permute-start(f32[48,128]{1,0:T(8,128)S(1)} %shard_map.68.share), channel_id=1, source_target_pairs={{0,1},{1,0},{2,3},{3,2},{4,5},{5,4},{6,7},{7,6},{8,9},{9,8},{10,11... | collective-permute-start | bytes 73736 | tf_op jit(solution)/shard_map/ppermute | solution.py:338
  44.5 6.1 %collective-permute-start.2 = (f32[48,128]{1,0:T(8,128)S(1)}, f32[48,128]{1,0:T(8,128)S(1)}, u32[]{:S(2)}, u32[]{:S(2)}) collective-permute-start(f32[48,128]{1,0:T(8,128)S(1)} %shard_map.68.share), channel_id=1, source_target_pairs={{1,2},{2,1},{3,4},{4,3},{5,6},{6,5},{7,8},{8,7},{9,10},{10,9},{11,... | collective-permute-start | bytes 73736 | tf_op jit(solution)/shard_map/ppermute | solution.py:339
  50.6 0.0 collective-permute-done.3.swap_a
  50.6 1.2 %collective-permute-done.2.swap_b = f32[48,128]{1,0:T(8,128)S(1)} collective-permute-done((f32[48,128]{1,0:T(8,128)S(1)}, f32[48,128]{1,0:T(8,128)S(1)}, u32[]{:S(2)}, u32[]{:S(2)}) %collective-permute-start.2) | collective-permute-done | bytes 24608 | tf_op jit(solution)/shard_map/ppermute | solution.py:339
  51.8 0.4 shard_map.69
  52.1 14.4 %all_to_all.11 = f32[16,4,8,128]{3,2,1,0:T(8,128)S(1)} all-to-all(f32[16,4,8,128]{3,2,1,0:T(8,128)S(1)} %shard_map.69), channel_id=1, replica_groups={{0,32,64,96,128,160,192,224,256,288,320,352,384,416,448,480},{16,48,80,..., dimensions={0} | all-to-all | bytes 524288 | tf_op jit(solution)/shard_map/all_to_all | solution.py:346
  66.5 5.3 %all-gather.1 = f32[32,4,8,128]{3,2,1,0:T(8,128)S(1)} all-gather(f32[16,4,8,128]{3,2,1,0:T(8,128)S(1)} %all_to_all.11), channel_id=3, replica_groups={{0,16},{32,48},{64,80},{96,112},{128,144},{160,176},{192,208},{224,240}..., dimensions={0}, use_global_device_ids=true | all-gather | bytes 786432 | tf_op jit(solution)/shard_map/all_gather | solution.py:347
  71.8 0.1 shard_map.70.field
  71.9 5.9 %collective-permute-start.5 = (f32[512,128]{1,0:T(8,128)S(1)}, f32[512,128]{1,0:T(8,128)S(1)}, u32[]{:S(2)}, u32[]{:S(2)}) collective-permute-start(f32[512,128]{1,0:T(8,128)S(1)} %shard_map.70.field), channel_id=1, source_target_pairs={{1,2},{2,1},{3,4},{4,3},{5,6},{6,5},{7,8},{8,7},{9,10},{10,9},{11,... | collective-permute-start | bytes 786440 | tf_op jit(solution)/shard_map/ppermute | solution.py:355
  77.8 1.9 %collective-permute-start.4 = (f32[512,128]{1,0:T(8,128)S(1)}, f32[512,128]{1,0:T(8,128)S(1)}, u32[]{:S(2)}, u32[]{:S(2)}) collective-permute-start(f32[512,128]{1,0:T(8,128)S(1)} %shard_map.70.field), channel_id=1, source_target_pairs={{0,1},{1,0},{2,3},{3,2},{4,5},{5,4},{6,7},{7,6},{8,9},{9,8},{10,11... | collective-permute-start | bytes 786440 | tf_op jit(solution)/shard_map/ppermute | solution.py:354
  79.7 0.4 shard_map.71
  80.1 3.9 %collective-permute-done.5.side_b = f32[512,128]{1,0:T(8,128)S(1)} collective-permute-done((f32[512,128]{1,0:T(8,128)S(1)}, f32[512,128]{1,0:T(8,128)S(1)}, u32[]{:S(2)}, u32[]{:S(2)}) %collective-permute-start.5) | collective-permute-done | bytes 262176 | tf_op jit(solution)/shard_map/ppermute | solution.py:355
  84.1 6.1 %collective-permute-done.4.side_a = f32[512,128]{1,0:T(8,128)S(1)} collective-permute-done((f32[512,128]{1,0:T(8,128)S(1)}, f32[512,128]{1,0:T(8,128)S(1)}, u32[]{:S(2)}, u32[]{:S(2)}) %collective-permute-start.4) | collective-permute-done | bytes 262176 | tf_op jit(solution)/shard_map/ppermute | solution.py:354
  90.2 1.1 %shard_map.72 = f32[2,256,128]{2,1,0:T(8,128)} custom-call(f32[8,128]{1,0:T(8,128)S(1)} %broadcast_in_dim.2.place, f32[2,2,128,128]{3,2,1,0:T(8,128)S(1)} %get-tuple-element.23.own, f32[512,128]{1,0:T(8,128)S(1)} %collective-permute-done.4.side_a, f32[512,128]{1,0:T(8,128)S(1)} %collective-permute-done.5.side_b, f32[512,128]{1,0:T(8,128)S(1)} %convert.5.after.control, ...), custom_call_target="tpu_custom_call" | custom-call | flops 1000000 | bytes 1000000 | tf_op jit(solution)/shard_map/pallas_call | solution.py:362
  (2 shorter events, 0.0 us)
Async XLA Ops:
  0.0 8.3 %copy-start.1 = (bf16[128,128]{1,0:T(8,128)(2,1)S(1)}, bf16[128,128]{1,0:T(8,128)(2,1)}, u32[]{:S(2)}) copy-start(bf16[128,128]{1,0:T(8,128)(2,1)} %vertical.5) | copy-start | bytes 98308
  0.0 8.8 %copy-start = (bf16[2,4,128,2,128]{4,3,2,1,0:T(2,128)(2,1)S(1)}, bf16[2,4,128,2,128]{4,3,2,1,0:T(2,128)(2,1)}, u32[]{:S(2)}) copy-start(bf16[2,4,128,2,128]{4,3,2,1,0:T(2,128)(2,1)} %param.6) | copy-start | bytes 1572868
  1.0 11.2 %collective-permute-start.1 = (f32[512,128]{1,0:T(8,128)S(1)}, f32[512,128]{1,0:T(8,128)S(1)}, u32[]{:S(2)}, u32[]{:S(2)}) collective-permute-start(f32[512,128]{1,0:T(8,128)S(1)} %convert.5.after.control), channel_id=1, source_target_pairs={{1,2},{2,1},{3,4},{4,3},{5,6},{6,5},{7,8},{8,7},{9,10},{10,9},{11,... | collective-permute-start | bytes 786440 | tf_op jit(solution)/shard_map/ppermute | solution.py:311
  6.2 12.7 %collective-permute-start = (f32[512,128]{1,0:T(8,128)S(1)}, f32[512,128]{1,0:T(8,128)S(1)}, u32[]{:S(2)}, u32[]{:S(2)}) collective-permute-start(f32[512,128]{1,0:T(8,128)S(1)} %convert.5.after.control), channel_id=1, source_target_pairs={{0,1},{1,0},{2,3},{3,2},{4,5},{5,4},{6,7},{7,6},{8,9},{9,8},{10,11... | collective-permute-start | bytes 786440 | tf_op jit(solution)/shard_map/ppermute | solution.py:310
  8.3 0.7 copy-start.2
  8.3 0.7 copy-start.3
  8.3 0.7 copy-start.4
  42.6 8.0 %collective-permute-start.3 = (f32[48,128]{1,0:T(8,128)S(1)}, f32[48,128]{1,0:T(8,128)S(1)}, u32[]{:S(2)}, u32[]{:S(2)}) collective-permute-start(f32[48,128]{1,0:T(8,128)S(1)} %shard_map.68.share), channel_id=1, source_target_pairs={{0,1},{1,0},{2,3},{3,2},{4,5},{5,4},{6,7},{7,6},{8,9},{9,8},{10,11... | collective-permute-start | bytes 73736 | tf_op jit(solution)/shard_map/ppermute | solution.py:338
  44.5 7.3 %collective-permute-start.2 = (f32[48,128]{1,0:T(8,128)S(1)}, f32[48,128]{1,0:T(8,128)S(1)}, u32[]{:S(2)}, u32[]{:S(2)}) collective-permute-start(f32[48,128]{1,0:T(8,128)S(1)} %shard_map.68.share), channel_id=1, source_target_pairs={{1,2},{2,1},{3,4},{4,3},{5,6},{6,5},{7,8},{8,7},{9,10},{10,9},{11,... | collective-permute-start | bytes 73736 | tf_op jit(solution)/shard_map/ppermute | solution.py:339
  71.9 12.2 %collective-permute-start.5 = (f32[512,128]{1,0:T(8,128)S(1)}, f32[512,128]{1,0:T(8,128)S(1)}, u32[]{:S(2)}, u32[]{:S(2)}) collective-permute-start(f32[512,128]{1,0:T(8,128)S(1)} %shard_map.70.field), channel_id=1, source_target_pairs={{1,2},{2,1},{3,4},{4,3},{5,6},{6,5},{7,8},{8,7},{9,10},{10,9},{11,... | collective-permute-start | bytes 786440 | tf_op jit(solution)/shard_map/ppermute | solution.py:355
  77.8 12.4 %collective-permute-start.4 = (f32[512,128]{1,0:T(8,128)S(1)}, f32[512,128]{1,0:T(8,128)S(1)}, u32[]{:S(2)}, u32[]{:S(2)}) collective-permute-start(f32[512,128]{1,0:T(8,128)S(1)} %shard_map.70.field), channel_id=1, source_target_pairs={{0,1},{1,0},{2,3},{3,2},{4,5},{5,4},{6,7},{7,6},{8,9},{9,8},{10,11... | collective-permute-start | bytes 786440 | tf_op jit(solution)/shard_map/ppermute | solution.py:354

commit v7 on v5

--- a/solution.py
+++ b/solution.py
@@ -276,15 +276,19 @@
 
 def product_kernel(place, own, side_a, side_b, control, transposed, far, out, sems):
     members, _, levels, width = own.shape
+    rounded = [
+        row.astype(jnp.bfloat16)
+        for k in range(members)
+        for row in smoothed_rows(place, k, own, side_a, side_b)
+    ]
+    back = jnp.dot(
+        transposed[...], jnp.concatenate(rounded, axis=1), preferred_element_type=f32
+    )
     for k in range(members):
         before = rows_of(control, 2 * k * levels, levels)
-        both = smoothed_rows(place, k, own, side_a, side_b)
-        rounded = jnp.concatenate([row.astype(jnp.bfloat16) for row in both], axis=1)
-        back = jnp.dot(transposed[...], rounded, preferred_element_type=f32)
         for r in range(2):
-            out[k, pl.ds(r, levels, stride=2), :] = (
-                before[r] + back[:, r * width : (r + 1) * width]
-            )
+            at = (2 * k + r) * width
+            out[k, pl.ds(r, levels, stride=2), :] = before[r] + back[:, at : at + width]
         pltpu.make_async_copy(out.at[k], far.at[k], sems.at[k]).start()
     for k in range(members):
         pltpu.make_async_copy(out.at[k], far.at[k], sems.at[k]).wait()

time: 92.1 us -> 92.1 us (level)
  no operation moved by 1% of the time
where the time goes in v7:
time: 92.1 us; the launch traced here: 91.8 us
  blocking collectives  46.8 us (51%)
  waiting for transfers between devices  22 us (24%)
  starting transfers between devices  18.1 us (20%)
  Pallas kernels  3.45 us (4%)
  other arithmetic  0.98 us (1%)
    all_to_all x1, blocking collectives, per_device(): lax.all_to_all(paired, 'mem', 0, 0, axis_index_groups=same_core, tiled=True)  20.8 us
    all_to_all x1, blocking collectives, per_device(): lax.all_to_all(spread, 'mem', 0, 0, axis_index_groups=same_core, tiled=True)  14.1 us
    ppermute x1, waiting for transfers between devices, per_device(): wide_a = lax.ppermute(wide, 'grid', swap_a)  6.65 us
    ppermute x1, waiting for transfers between devices, per_device(): projected_a = lax.ppermute(projected, 'grid', swap_a)  6.31 us
    ppermute x1, waiting for transfers between devices, per_device(): projected_b = lax.ppermute(projected, 'grid', swap_b)  6.17 us
    ppermute x1, starting transfers between devices, per_device(): share_b = lax.ppermute(share, 'grid', swap_b)  6.08 us
    all_gather x1, blocking collectives, per_device(): adjoint = lax.all_gather(mine, 'mem', axis=0, axis_index_groups=cores)  5.99 us
    ppermute x1, starting transfers between devices, per_device(): wide_b = lax.ppermute(wide, 'grid', swap_b)  5.18 us
  transfers between devices with their start and end apart: 5, of which 4 were waited for; matrix products, arithmetic and copies ran while one was open for 0% of the time, Pallas kernels for 1%

profile of v7, /device:TPU:195, one launch (start us, length us, event | category | flops | bytes accessed | tf_op | source)
XLA Modules:
  0.0 91.8 jit_solution(3671095219226799731)
XLA Ops:
  0.0 0.0 copy-start.1
  0.0 0.0 copy-start
  0.0 1.0 %convert.5.after.control = f32[512,128]{1,0:T(8,128)S(1)} convert(bf16[512,128]{1,0:T(8,128)(2,1)} %bitcast.18) | non-fusion elementwise | flops 65536 | bytes 393216 | tf_op jit(solution)/shard_map/convert_element_type | solution.py:320
  1.0 5.2 %collective-permute-start.1 = (f32[512,128]{1,0:T(8,128)S(1)}, f32[512,128]{1,0:T(8,128)S(1)}, u32[]{:S(2)}, u32[]{:S(2)}) collective-permute-start(f32[512,128]{1,0:T(8,128)S(1)} %convert.5.after.control), channel_id=1, source_target_pairs={{1,2},{2,1},{3,4},{4,3},{5,6},{6,5},{7,8},{8,7},{9,10},{10,9},{11,... | collective-permute-start | bytes 786440 | tf_op jit(solution)/shard_map/ppermute | solution.py:322
  6.2 1.9 %collective-permute-start = (f32[512,128]{1,0:T(8,128)S(1)}, f32[512,128]{1,0:T(8,128)S(1)}, u32[]{:S(2)}, u32[]{:S(2)}) collective-permute-start(f32[512,128]{1,0:T(8,128)S(1)} %convert.5.after.control), channel_id=1, source_target_pairs={{0,1},{1,0},{2,3},{3,2},{4,5},{5,4},{6,7},{7,6},{8,9},{9,8},{10,11... | collective-permute-start | bytes 786440 | tf_op jit(solution)/shard_map/ppermute | solution.py:321
  8.1 0.1 stack.39
  8.2 0.1 broadcast_in_dim.2.place
  8.3 0.0 copy-done.1
  8.3 0.0 copy-start.2
  8.3 0.0 copy-start.3
  8.3 0.0 copy-start.4
  8.3 0.5 shard_map.65.own
  8.8 0.0 copy-done
  8.8 0.2 copy-done.2
  9.0 0.0 copy-done.3
  9.0 0.0 copy-done.4
  9.0 0.3 shard_map.64
  9.4 2.8 %collective-permute-done.1.side_b = f32[512,128]{1,0:T(8,128)S(1)} collective-permute-done((f32[512,128]{1,0:T(8,128)S(1)}, f32[512,128]{1,0:T(8,128)S(1)}, u32[]{:S(2)}, u32[]{:S(2)}) %collective-permute-start.1) | collective-permute-done | bytes 262176 | tf_op jit(solution)/shard_map/ppermute | solution.py:322
  12.2 6.7 %collective-permute-done.side_a = f32[512,128]{1,0:T(8,128)S(1)} collective-permute-done((f32[512,128]{1,0:T(8,128)S(1)}, f32[512,128]{1,0:T(8,128)S(1)}, u32[]{:S(2)}, u32[]{:S(2)}) %collective-permute-start) | collective-permute-done | bytes 262176 | tf_op jit(solution)/shard_map/ppermute | solution.py:321
  18.8 0.5 shard_map.66
  19.4 2.3 %all-gather = f32[32,4,8,128]{3,2,1,0:T(8,128)S(1)} all-gather(f32[16,4,8,128]{3,2,1,0:T(8,128)S(1)} %get-tuple-element.17), channel_id=2, replica_groups={{0,16},{32,48},{64,80},{96,112},{128,144},{160,176},{192,208},{224,240}..., dimensions={0}, use_global_device_ids=true | all-gather | bytes 786432 | tf_op jit(solution)/shard_map/all_gather | solution.py:341
  21.7 0.1 shard_map.67
  21.7 20.8 %all_to_all.10.arrived = f32[16,4,8,128]{3,2,1,0:T(8,128)S(1)} all-to-all(f32[16,4,8,128]{3,2,1,0:T(8,128)S(1)} %shard_map.67), channel_id=1, replica_groups={{0,32,64,96,128,160,192,224,256,288,320,352,384,416,448,480},{16,48,80,..., dimensions={0} | all-to-all | bytes 524288 | tf_op jit(solution)/shard_map/all_to_all | solution.py:344
  42.6 6.1 %collective-permute-start.2 = (f32[48,128]{1,0:T(8,128)S(1)}, f32[48,128]{1,0:T(8,128)S(1)}, u32[]{:S(2)}, u32[]{:S(2)}) collective-permute-start(f32[48,128]{1,0:T(8,128)S(1)} %shard_map.68.share), channel_id=1, source_target_pairs={{1,2},{2,1},{3,4},{4,3},{5,6},{6,5},{7,8},{8,7},{9,10},{10,9},{11,... | collective-permute-start | bytes 73736 | tf_op jit(solution)/shard_map/ppermute | solution.py:349
  48.6 3.6 %all-gather.1 = f32[96,128]{1,0:T(8,128)S(1)} all-gather(f32[48,128]{1,0:T(8,128)S(1)} %shard_map.68.share), channel_id=3, replica_groups={{0,1},{2,3},{4,5},{6,7},{8,9},{10,11},{12,13},{14,15},{16,17},{18,19},{..., dimensions={0}, use_global_device_ids=true | all-gather | bytes 73728 | tf_op jit(solution)/shard_map/all_gather | solution.py:350
  52.2 0.0 collective-permute-done.2.swap_b
  52.3 0.4 shard_map.69
  52.6 14.1 %all_to_all.11 = f32[16,4,8,128]{3,2,1,0:T(8,128)S(1)} all-to-all(f32[16,4,8,128]{3,2,1,0:T(8,128)S(1)} %shard_map.69), channel_id=1, replica_groups={{0,32,64,96,128,160,192,224,256,288,320,352,384,416,448,480},{16,48,80,..., dimensions={0} | all-to-all | bytes 524288 | tf_op jit(solution)/shard_map/all_to_all | solution.py:357
  66.7 6.0 %all-gather.2 = f32[32,4,8,128]{3,2,1,0:T(8,128)S(1)} all-gather(f32[16,4,8,128]{3,2,1,0:T(8,128)S(1)} %all_to_all.11), channel_id=4, replica_groups={{0,16},{32,48},{64,80},{96,112},{128,144},{160,176},{192,208},{224,240}..., dimensions={0}, use_global_device_ids=true | all-gather | bytes 786432 | tf_op jit(solution)/shard_map/all_gather | solution.py:358
  72.7 0.1 shard_map.70.field
  72.8 3.0 %collective-permute-start.4 = (f32[512,128]{1,0:T(8,128)S(1)}, f32[512,128]{1,0:T(8,128)S(1)}, u32[]{:S(2)}, u32[]{:S(2)}) collective-permute-start(f32[512,128]{1,0:T(8,128)S(1)} %shard_map.70.field), channel_id=1, source_target_pairs={{1,2},{2,1},{3,4},{4,3},{5,6},{6,5},{7,8},{8,7},{9,10},{10,9},{11,... | collective-permute-start | bytes 786440 | tf_op jit(solution)/shard_map/ppermute | solution.py:366
  75.8 1.9 %collective-permute-start.3 = (f32[512,128]{1,0:T(8,128)S(1)}, f32[512,128]{1,0:T(8,128)S(1)}, u32[]{:S(2)}, u32[]{:S(2)}) collective-permute-start(f32[512,128]{1,0:T(8,128)S(1)} %shard_map.70.field), channel_id=1, source_target_pairs={{0,1},{1,0},{2,3},{3,2},{4,5},{5,4},{6,7},{7,6},{8,9},{9,8},{10,11... | collective-permute-start | bytes 786440 | tf_op jit(solution)/shard_map/ppermute | solution.py:365
  77.8 0.4 shard_map.71
  78.2 6.2 %collective-permute-done.4.side_b = f32[512,128]{1,0:T(8,128)S(1)} collective-permute-done((f32[512,128]{1,0:T(8,128)S(1)}, f32[512,128]{1,0:T(8,128)S(1)}, u32[]{:S(2)}, u32[]{:S(2)}) %collective-permute-start.4) | collective-permute-done | bytes 262176 | tf_op jit(solution)/shard_map/ppermute | solution.py:366
  84.3 6.3 %collective-permute-done.3.side_a = f32[512,128]{1,0:T(8,128)S(1)} collective-permute-done((f32[512,128]{1,0:T(8,128)S(1)}, f32[512,128]{1,0:T(8,128)S(1)}, u32[]{:S(2)}, u32[]{:S(2)}) %collective-permute-start.3) | collective-permute-done | bytes 262176 | tf_op jit(solution)/shard_map/ppermute | solution.py:365
  90.7 1.1 %shard_map.72 = f32[2,256,128]{2,1,0:T(8,128)} custom-call(f32[8,128]{1,0:T(8,128)S(1)} %broadcast_in_dim.2.place, f32[2,2,128,128]{3,2,1,0:T(8,128)S(1)} %get-tuple-element.23.own, f32[512,128]{1,0:T(8,128)S(1)} %collective-permute-done.3.side_a, f32[512,128]{1,0:T(8,128)S(1)} %collective-permute-done.4.side_b, f32[512,128]{1,0:T(8,128)S(1)} %convert.5.after.control, ...), custom_call_target="tpu_custom_call" | custom-call | flops 1000000 | bytes 1000000 | tf_op jit(solution)/shard_map/pallas_call | solution.py:373
  (2 shorter events, 0.0 us)
Async XLA Ops:
  0.0 8.3 %copy-start.1 = (bf16[128,128]{1,0:T(8,128)(2,1)S(1)}, bf16[128,128]{1,0:T(8,128)(2,1)}, u32[]{:S(2)}) copy-start(bf16[128,128]{1,0:T(8,128)(2,1)} %vertical.5) | copy-start | bytes 98308
  0.0 8.8 %copy-start = (bf16[2,4,128,2,128]{4,3,2,1,0:T(2,128)(2,1)S(1)}, bf16[2,4,128,2,128]{4,3,2,1,0:T(2,128)(2,1)}, u32[]{:S(2)}) copy-start(bf16[2,4,128,2,128]{4,3,2,1,0:T(2,128)(2,1)} %param.6) | copy-start | bytes 1572868
  1.0 11.2 %collective-permute-start.1 = (f32[512,128]{1,0:T(8,128)S(1)}, f32[512,128]{1,0:T(8,128)S(1)}, u32[]{:S(2)}, u32[]{:S(2)}) collective-permute-start(f32[512,128]{1,0:T(8,128)S(1)} %convert.5.after.control), channel_id=1, source_target_pairs={{1,2},{2,1},{3,4},{4,3},{5,6},{6,5},{7,8},{8,7},{9,10},{10,9},{11,... | collective-permute-start | bytes 786440 | tf_op jit(solution)/shard_map/ppermute | solution.py:322
  6.2 12.7 %collective-permute-start = (f32[512,128]{1,0:T(8,128)S(1)}, f32[512,128]{1,0:T(8,128)S(1)}, u32[]{:S(2)}, u32[]{:S(2)}) collective-permute-start(f32[512,128]{1,0:T(8,128)S(1)} %convert.5.after.control), channel_id=1, source_target_pairs={{0,1},{1,0},{2,3},{3,2},{4,5},{5,4},{6,7},{7,6},{8,9},{9,8},{10,11... | collective-permute-start | bytes 786440 | tf_op jit(solution)/shard_map/ppermute | solution.py:321
  8.3 0.7 copy-start.2
  8.3 0.7 copy-start.3
  8.3 0.7 copy-start.4
  42.6 9.7 %collective-permute-start.2 = (f32[48,128]{1,0:T(8,128)S(1)}, f32[48,128]{1,0:T(8,128)S(1)}, u32[]{:S(2)}, u32[]{:S(2)}) collective-permute-start(f32[48,128]{1,0:T(8,128)S(1)} %shard_map.68.share), channel_id=1, source_target_pairs={{1,2},{2,1},{3,4},{4,3},{5,6},{6,5},{7,8},{8,7},{9,10},{10,9},{11,... | collective-permute-start | bytes 73736 | tf_op jit(solution)/shard_map/ppermute | solution.py:349
  72.8 11.5 %collective-permute-start.4 = (f32[512,128]{1,0:T(8,128)S(1)}, f32[512,128]{1,0:T(8,128)S(1)}, u32[]{:S(2)}, u32[]{:S(2)}) collective-permute-start(f32[512,128]{1,0:T(8,128)S(1)} %shard_map.70.field), channel_id=1, source_target_pairs={{1,2},{2,1},{3,4},{4,3},{5,6},{6,5},{7,8},{8,7},{9,10},{10,9},{11,... | collective-permute-start | bytes 786440 | tf_op jit(solution)/shard_map/ppermute | solution.py:366
  75.8 14.8 %collective-permute-start.3 = (f32[512,128]{1,0:T(8,128)S(1)}, f32[512,128]{1,0:T(8,128)S(1)}, u32[]{:S(2)}, u32[]{:S(2)}) collective-permute-start(f32[512,128]{1,0:T(8,128)S(1)} %shard_map.70.field), channel_id=1, source_target_pairs={{0,1},{1,0},{2,3},{3,2},{4,5},{5,4},{6,7},{7,6},{8,9},{9,8},{10,11... | collective-permute-start | bytes 786440 | tf_op jit(solution)/shard_map/ppermute | solution.py:365
